TPU v7x, 32 devices: a whole 2x2x4 slice. The times are simulated.
32 devices in a mesh: ctx: 16 (over z, x, core), wa: 2 (over y).
Axes of the slice: x: 2, y: 2, z: 4, core: 2. Of those that a mesh axis runs over, the one named last changes fastest.
Arguments:
- tokens: bfloat16 [2, 6144, 768], P('wa', 'ctx'), may hold values from -6 to 6
- cotangent: bfloat16 [2, 6144, 768], P('wa', 'ctx'), may hold values from -6 to 6
- lengths: int32 [2, 3], P('wa'), may hold values from 1024 to 3072, as said below
- block_order: int32 [32], replicated, may hold values from 0 to 31, each once
- w_query: float32 [768, 768], P('wa'), may hold values from -0.21875 to 0.21875
- b_query: float32 [768], P('wa'), may hold values from -4 to 4
- w_key: float32 [768, 768], P('wa'), may hold values from -0.21875 to 0.21875
- w_value: float32 [768, 768], P('wa'), may hold values from -0.21875 to 0.21875
- b_value: float32 [768], P('wa'), may hold values from -4 to 4
- w_out: float32 [768, 768], P('wa'), may hold values from -6 to 6
- b_out: float32 [768], P('wa'), may hold values from -4 to 4
- gain_one: float32 [768], P('wa'), may hold values from 0.5 to 1.5
- shift_one: float32 [768], P('wa'), may hold values from -4 to 4
- w_up: float32 [768, 3072], P('wa'), may hold values from -0.21875 to 0.21875
- b_up: float32 [3072], P('wa'), may hold values from -4 to 4
- w_down: float32 [3072, 768], P('wa'), may hold values from -0.109375 to 0.109375
- b_down: float32 [768], P('wa'), may hold values from -4 to 4
- gain_two: float32 [768], P('wa'), may hold values from 0.5 to 1.5
- shift_two: float32 [768], P('wa'), may hold values from -4 to 4
Outputs:
- activations: bfloat16 [2, 6144, 768], P('wa', 'ctx')
- input_grad: bfloat16 [2, 6144, 768], P('wa', 'ctx')
- grad_w_query: float32 [768, 768], P('wa')
- grad_b_query: float32 [768], P('wa')
- grad_w_key: float32 [768, 768], P('wa')
- grad_w_value: float32 [768, 768], P('wa')
- grad_b_value: float32 [768], P('wa')
- grad_w_out: float32 [768, 768], P('wa')
- grad_b_out: float32 [768], P('wa')
- grad_gain_one: float32 [768], P('wa')
- grad_shift_one: float32 [768], P('wa')
- grad_w_up: float32 [768, 3072], P('wa')
- grad_b_up: float32 [3072], P('wa')
- grad_w_down: float32 [3072, 768], P('wa')
- grad_b_down: float32 [768], P('wa')
- grad_gain_two: float32 [768], P('wa')
- grad_shift_two: float32 [768], P('wa')
Inputs may be any that keep to these rules, and one draw needn't show every extreme that they name: `lengths`: each slot holds three sequences, each of 1024 tokens or more, one of them exactly 3072; the rest of the slot, 2 tokens or more, is padding. `block_order`: each block number appears once.
All inputs are finite; a program needn't handle non-finite values.
Results may differ from a plain program's by a relative error of at most 0.023.
Values may be sent and summed in bfloat16 or wider, within the bound.
A program may use at most 256 MiB of HBM per device.

v0:
```python
from functools import partial

import jax
import jax.numpy as jnp
from jax import lax
from jax.sharding import PartitionSpec as P

HEADS = 12
HEAD_DIM = 64


epsilon = 1e-05


def layer_norm(hidden, gain_vec, shift_vec):
    centre = hidden - jnp.mean(hidden, axis=-1, keepdims=True)
    spread = jnp.mean(centre * centre, axis=-1, keepdims=True)
    return centre * lax.rsqrt(spread + epsilon) * gain_vec + shift_vec


def segment_of(position, seq_ends):
    return jnp.sum((position[:, None] >= seq_ends[None, :]).astype(jnp.int32), axis=1)


def segment_ids(row_ids, block_order, seq_ends, half_len):
    dealt_slot = row_ids // (2 * half_len) * 2 + row_ids // half_len % 2
    table_ids = jnp.arange(block_order.shape[0], dtype=jnp.int32)
    block_ids = jnp.sum(
        jnp.where(dealt_slot[:, None] == table_ids[None, :], block_order[None, :], 0), axis=1
    )
    position = block_ids * half_len + row_ids % half_len
    return segment_of(position, seq_ends)


def block_steps(tok_rows):
    return 2 * tok_rows


def body(
    tokens,
    cotangent,
    lengths,
    block_order,
    w_query,
    b_query,
    w_key,
    w_value,
    b_value,
    w_out,
    b_out,
    gain_one,
    shift_one,
    w_up,
    b_up,
    w_down,
    b_down,
    gain_two,
    shift_two,
):
    low_type = jnp.bfloat16
    inputs = tokens[0]
    tok_rows = inputs.shape[0]
    width = inputs.shape[1]
    half_len = tok_rows // 2
    seq_ends = jnp.cumsum(lengths[0])
    own_rows = lax.axis_index("ctx") * tok_rows + jnp.arange(tok_rows, dtype=jnp.int32)
    own_seg = segment_ids(own_rows, block_order, seq_ends, half_len)
    (
        query_weight,
        query_bias,
        key_weight,
        value_weight,
        value_bias,
        out_weight,
        out_bias,
        gain_first,
        shift_first,
    ) = (
        lax.all_gather(w_query.astype(low_type), "wa", axis=0, tiled=True),
        lax.all_gather(b_query.astype(low_type), "wa", axis=0, tiled=True),
        lax.all_gather(w_key.astype(low_type), "wa", axis=0, tiled=True),
        lax.all_gather(w_value.astype(low_type), "wa", axis=0, tiled=True),
        lax.all_gather(b_value.astype(low_type), "wa", axis=0, tiled=True),
        lax.all_gather(w_out.astype(low_type), "wa", axis=0, tiled=True),
        lax.all_gather(b_out.astype(low_type), "wa", axis=0, tiled=True),
        lax.all_gather(gain_one.astype(low_type), "wa", axis=0, tiled=True),
        lax.all_gather(shift_one.astype(low_type), "wa", axis=0, tiled=True),
    )
    query_proj = (
        ((jnp.dot(inputs, query_weight, preferred_element_type=jnp.float32) + query_bias) * 0.125)
        .astype(low_type)
        .reshape(tok_rows, HEADS, HEAD_DIM)
    )
    key_proj = (
        jnp.dot(inputs, key_weight, preferred_element_type=jnp.float32)
        .astype(low_type)
        .reshape(tok_rows, HEADS, HEAD_DIM)
    )
    value_proj = (
        (jnp.dot(inputs, value_weight, preferred_element_type=jnp.float32) + value_bias)
        .astype(low_type)
        .reshape(tok_rows, HEADS, HEAD_DIM)
    )

    def key_segments(first_row, block_num, step_rows):
        rows_now = first_row + block_num * step_rows + jnp.arange(step_rows, dtype=jnp.int32)
        return segment_ids(rows_now, block_order, seq_ends, half_len)

    def forward_block(state, key_blk, value_blk, key_seg):
        acc_sum, total = state
        scores = jnp.einsum("qhd,khd->hqk", query_proj, key_blk, preferred_element_type=jnp.float32)
        mask = own_seg[:, None] == key_seg[None, :]
        expo = jnp.where(mask[None], jnp.exp(scores), 0.0)
        total = total + jnp.sum(expo, axis=-1)
        acc_sum = acc_sum + jnp.einsum(
            "hqk,khd->qhd", expo.astype(low_type), value_blk, preferred_element_type=jnp.float32
        )
        return (acc_sum, total)

    start_state = (
        jnp.zeros((tok_rows, HEADS, HEAD_DIM), jnp.float32),
        jnp.zeros((HEADS, tok_rows), jnp.float32),
    )
    key_whole, value_whole = (
        lax.all_gather(key_proj, "ctx", axis=0, tiled=True),
        lax.all_gather(value_proj, "ctx", axis=0, tiled=True),
    )
    row_count = key_whole.shape[0]
    step_rows = block_steps(tok_rows)
    count = row_count // step_rows
    stacked = (
        key_whole.reshape(count, step_rows, HEADS, HEAD_DIM),
        value_whole.reshape(count, step_rows, HEADS, HEAD_DIM),
        jnp.arange(count, dtype=jnp.int32),
    )

    def advance(carry_state, scan_item):
        key_blk, value_blk, block_num = scan_item
        key_seg = key_segments(0, block_num, step_rows)
        fresh = forward_block(carry_state, key_blk, value_blk, key_seg)
        return (fresh, None)

    final_state, _ = lax.scan(advance, start_state, stacked)
    acc_sum, total = final_state
    context = acc_sum / total.T[:, :, None]
    context_low = context.astype(low_type).reshape(tok_rows, width)
    up_weight, up_bias, down_weight, down_bias, gain_second, shift_second = (
        lax.all_gather(w_up.astype(low_type), "wa", axis=0, tiled=True),
        lax.all_gather(b_up.astype(low_type), "wa", axis=0, tiled=True),
        lax.all_gather(w_down.astype(low_type), "wa", axis=0, tiled=True),
        lax.all_gather(b_down.astype(low_type), "wa", axis=0, tiled=True),
        lax.all_gather(gain_two.astype(low_type), "wa", axis=0, tiled=True),
        lax.all_gather(shift_two.astype(low_type), "wa", axis=0, tiled=True),
    )
    attn_out = jnp.dot(context_low, out_weight, preferred_element_type=jnp.float32) + out_bias
    h_one = inputs.astype(jnp.float32) + attn_out
    norm_one, norm_one_back = jax.vjp(
        layer_norm, h_one, gain_first.astype(jnp.float32), shift_first.astype(jnp.float32)
    )
    norm_low = norm_one.astype(low_type)
    up_pre = jnp.dot(norm_low, up_weight, preferred_element_type=jnp.float32) + up_bias
    gelu_out, gelu_back = jax.vjp(partial(jax.nn.gelu, approximate=False), up_pre)
    gelu_low = gelu_out.astype(low_type)
    down_out = jnp.dot(gelu_low, down_weight, preferred_element_type=jnp.float32) + down_bias
    h_two = norm_one + down_out
    result, norm_two_back = jax.vjp(
        layer_norm, h_two, gain_second.astype(jnp.float32), shift_second.astype(jnp.float32)
    )
    activations = result.astype(low_type)[None]
    valid = (own_seg < 3).astype(jnp.float32)
    g_out = cotangent[0].astype(jnp.float32) * valid[:, None]
    d_htwo, grad_gain_second, grad_shift_second = norm_two_back(g_out)
    d_down = d_htwo.astype(low_type)
    grad_wdown = jnp.einsum("tf,td->fd", gelu_low, d_down, preferred_element_type=jnp.float32)
    grad_bdown = jnp.sum(d_down.astype(jnp.float32), axis=0)
    d_gelu = jnp.einsum("td,fd->tf", d_down, down_weight, preferred_element_type=jnp.float32)
    (d_uppre,) = gelu_back(d_gelu)
    d_up = d_uppre.astype(low_type)
    grad_wup = jnp.einsum("td,tf->df", norm_low, d_up, preferred_element_type=jnp.float32)
    grad_bup = jnp.sum(d_up.astype(jnp.float32), axis=0)
    d_yone = d_htwo + jnp.einsum("tf,df->td", d_up, up_weight, preferred_element_type=jnp.float32)
    d_hone, grad_gain_first, grad_shift_first = norm_one_back(d_yone)
    d_attn = d_hone.astype(low_type)
    grad_wout = jnp.einsum("tc,td->cd", context_low, d_attn, preferred_element_type=jnp.float32)
    grad_bout = jnp.sum(d_attn.astype(jnp.float32), axis=0)
    d_context = jnp.einsum(
        "td,cd->tc", d_attn, out_weight, preferred_element_type=jnp.float32
    ).reshape(tok_rows, HEADS, HEAD_DIM)
    d_acc = (d_context / total.T[:, :, None]).astype(low_type)
    d_total = -jnp.sum(d_context * context, axis=-1).T / total

    def block_scores(key_blk, value_blk, key_seg):
        scores = jnp.einsum("qhd,khd->hqk", query_proj, key_blk, preferred_element_type=jnp.float32)
        mask = own_seg[:, None] == key_seg[None, :]
        expo = jnp.where(mask[None], jnp.exp(scores), 0.0)
        d_prob = jnp.einsum("qhd,khd->hqk", d_acc, value_blk, preferred_element_type=jnp.float32)
        d_scores = (expo * (d_prob + d_total[:, :, None])).astype(low_type)
        return (expo, d_scores)

    def backward_block(dq_sum, key_blk, value_blk, key_seg):
        expo, d_scores = block_scores(key_blk, value_blk, key_seg)
        dq_sum = dq_sum + jnp.einsum(
            "hqk,khd->qhd", d_scores, key_blk, preferred_element_type=jnp.float32
        )
        d_keyblk = jnp.einsum(
            "hqk,qhd->khd", d_scores, query_proj, preferred_element_type=jnp.float32
        )
        d_valueblk = jnp.einsum(
            "hqk,qhd->khd", expo.astype(low_type), d_acc, preferred_element_type=jnp.float32
        )
        return (dq_sum, (d_keyblk, d_valueblk))

    whole_rows = key_whole.shape[0]
    back_rows = 2 * tok_rows
    back_count = whole_rows // back_rows
    back_stack = (
        key_whole.reshape(back_count, back_rows, HEADS, HEAD_DIM),
        value_whole.reshape(back_count, back_rows, HEADS, HEAD_DIM),
        jnp.arange(back_count, dtype=jnp.int32),
    )
    dq_start = jnp.zeros((tok_rows, HEADS, HEAD_DIM), jnp.float32)

    def retreat(dq_sum, scan_item):
        key_blk, value_blk, block_num = scan_item
        key_seg = key_segments(0, block_num, back_rows)
        return backward_block(dq_sum, key_blk, value_blk, key_seg)

    dq_sum, (key_terms, value_terms) = lax.scan(retreat, dq_start, back_stack)
    key_terms = key_terms.reshape(whole_rows, HEADS, HEAD_DIM)
    value_terms = value_terms.reshape(whole_rows, HEADS, HEAD_DIM)
    key_sum, value_sum = (
        lax.psum_scatter(
            key_terms.astype(jnp.bfloat16), "ctx", scatter_dimension=0, tiled=True
        ).astype(jnp.float32),
        lax.psum_scatter(
            value_terms.astype(jnp.bfloat16), "ctx", scatter_dimension=0, tiled=True
        ).astype(jnp.float32),
    )
    d_keys = key_sum.astype(low_type).reshape(tok_rows, width)
    d_values = value_sum.astype(low_type).reshape(tok_rows, width)
    d_queries = (
        (dq_sum.astype(low_type).astype(jnp.float32) * 0.125)
        .astype(low_type)
        .reshape(tok_rows, width)
    )
    grad_wquery = jnp.einsum("tc,td->cd", inputs, d_queries, preferred_element_type=jnp.float32)
    grad_bquery = jnp.sum(d_queries.astype(jnp.float32), axis=0)
    grad_wkey = jnp.einsum("tc,td->cd", inputs, d_keys, preferred_element_type=jnp.float32)
    grad_wvalue = jnp.einsum("tc,td->cd", inputs, d_values, preferred_element_type=jnp.float32)
    grad_bvalue = jnp.sum(d_values.astype(jnp.float32), axis=0)
    d_input = d_hone + jnp.einsum(
        "td,cd->tc", d_queries, query_weight, preferred_element_type=jnp.float32
    )
    d_input = d_input + jnp.einsum(
        "td,cd->tc", d_keys, key_weight, preferred_element_type=jnp.float32
    )
    d_input = d_input + jnp.einsum(
        "td,cd->tc", d_values, value_weight, preferred_element_type=jnp.float32
    )
    input_grad = d_input.astype(low_type)[None]
    shards = (
        lax.psum_scatter(
            grad_wquery.astype(jnp.bfloat16), "wa", scatter_dimension=0, tiled=True
        ).astype(jnp.float32),
        lax.psum_scatter(
            grad_bquery.astype(jnp.bfloat16), "wa", scatter_dimension=0, tiled=True
        ).astype(jnp.float32),
        lax.psum_scatter(
            grad_wkey.astype(jnp.bfloat16), "wa", scatter_dimension=0, tiled=True
        ).astype(jnp.float32),
        lax.psum_scatter(
            grad_wvalue.astype(jnp.bfloat16), "wa", scatter_dimension=0, tiled=True
        ).astype(jnp.float32),
        lax.psum_scatter(
            grad_bvalue.astype(jnp.bfloat16), "wa", scatter_dimension=0, tiled=True
        ).astype(jnp.float32),
        lax.psum_scatter(
            grad_wout.astype(jnp.bfloat16), "wa", scatter_dimension=0, tiled=True
        ).astype(jnp.float32),
        lax.psum_scatter(
            grad_bout.astype(jnp.bfloat16), "wa", scatter_dimension=0, tiled=True
        ).astype(jnp.float32),
        lax.psum_scatter(
            grad_gain_first.astype(jnp.bfloat16), "wa", scatter_dimension=0, tiled=True
        ).astype(jnp.float32),
        lax.psum_scatter(
            grad_shift_first.astype(jnp.bfloat16), "wa", scatter_dimension=0, tiled=True
        ).astype(jnp.float32),
        lax.psum_scatter(
            grad_wup.astype(jnp.bfloat16), "wa", scatter_dimension=0, tiled=True
        ).astype(jnp.float32),
        lax.psum_scatter(
            grad_bup.astype(jnp.bfloat16), "wa", scatter_dimension=0, tiled=True
        ).astype(jnp.float32),
        lax.psum_scatter(
            grad_wdown.astype(jnp.bfloat16), "wa", scatter_dimension=0, tiled=True
        ).astype(jnp.float32),
        lax.psum_scatter(
            grad_bdown.astype(jnp.bfloat16), "wa", scatter_dimension=0, tiled=True
        ).astype(jnp.float32),
        lax.psum_scatter(
            grad_gain_second.astype(jnp.bfloat16), "wa", scatter_dimension=0, tiled=True
        ).astype(jnp.float32),
        lax.psum_scatter(
            grad_shift_second.astype(jnp.bfloat16), "wa", scatter_dimension=0, tiled=True
        ).astype(jnp.float32),
    )
    summed = (
        lax.psum(shards[0].astype(jnp.bfloat16), "ctx").astype(jnp.float32),
        lax.psum(shards[1].astype(jnp.bfloat16), "ctx").astype(jnp.float32),
        lax.psum(shards[2].astype(jnp.bfloat16), "ctx").astype(jnp.float32),
        lax.psum(shards[3].astype(jnp.bfloat16), "ctx").astype(jnp.float32),
        lax.psum(shards[4].astype(jnp.bfloat16), "ctx").astype(jnp.float32),
        lax.psum(shards[5].astype(jnp.bfloat16), "ctx").astype(jnp.float32),
        lax.psum(shards[6].astype(jnp.bfloat16), "ctx").astype(jnp.float32),
        lax.psum(shards[7].astype(jnp.bfloat16), "ctx").astype(jnp.float32),
        lax.psum(shards[8].astype(jnp.bfloat16), "ctx").astype(jnp.float32),
        lax.psum(shards[9].astype(jnp.bfloat16), "ctx").astype(jnp.float32),
        lax.psum(shards[10].astype(jnp.bfloat16), "ctx").astype(jnp.float32),
        lax.psum(shards[11].astype(jnp.bfloat16), "ctx").astype(jnp.float32),
        lax.psum(shards[12].astype(jnp.bfloat16), "ctx").astype(jnp.float32),
        lax.psum(shards[13].astype(jnp.bfloat16), "ctx").astype(jnp.float32),
        lax.psum(shards[14].astype(jnp.bfloat16), "ctx").astype(jnp.float32),
    )
    return (
        activations,
        input_grad,
        summed[0],
        summed[1],
        summed[2],
        summed[3],
        summed[4],
        summed[5],
        summed[6],
        summed[7],
        summed[8],
        summed[9],
        summed[10],
        summed[11],
        summed[12],
        summed[13],
        summed[14],
    )


def solution(mesh):
    placed = (
        P("wa", "ctx", None),
        P("wa", "ctx", None),
        P("wa", None),
        P(),
        P("wa", None),
        P("wa"),
        P("wa", None),
        P("wa", None),
        P("wa"),
        P("wa", None),
        P("wa"),
        P("wa"),
        P("wa"),
        P("wa", None),
        P("wa"),
        P("wa", None),
        P("wa"),
        P("wa"),
        P("wa"),
    )
    return jax.shard_map(
        body,
        mesh=mesh,
        in_specs=placed,
        out_specs=(
            P("wa", "ctx", None),
            P("wa", "ctx", None),
            P("wa", None),
            P("wa"),
            P("wa", None),
            P("wa", None),
            P("wa"),
            P("wa", None),
            P("wa"),
            P("wa"),
            P("wa"),
            P("wa", None),
            P("wa"),
            P("wa", None),
            P("wa"),
            P("wa"),
            P("wa"),
        ),
        check_vma=False,
    )
```

profile of v0, /device:TPU:9, one launch (start us, length us, event | category | flops | bytes accessed | tf_op | source)
XLA Modules:
  0.0 1422.9 jit_solution(14266771286409439732)
XLA Ops:
  14.8 19.1 %all-gather.18.cloned.1.call-done = bf16[768,768]{1,0:T(8,128)(2,1)} async-done(((bf16[384,768]{1,0:T(8,128)(2,1)}), bf16[768,768]{1,0:T(8,128)(2,1)}) %all-gather.18.cloned.1.call-update) | async-done | bytes 1179664 | tf_op jit(solution)/shard_map/all_gather | solution.py:82
  37.0 21.9 %all-gather.22.cloned.1.call-done = bf16[768,768]{1,0:T(8,128)(2,1)} async-done(((bf16[384,768]{1,0:T(8,128)(2,1)}), bf16[768,768]{1,0:T(8,128)(2,1)}) %all-gather.22.cloned.1.call-update) | async-done | bytes 1179664 | tf_op jit(solution)/shard_map/all_gather | solution.py:81
  102.4 66.6 %all-gather.20.cloned.1.call-done = bf16[6144,12,64]{0,2,1:T(8,128)(2,1)} async-done(((bf16[384,12,64]{0,2,1:T(8,128)(2,1)}), bf16[6144,12,64]{0,2,1:T(8,128)(2,1)}) %all-gather.20.cloned.1.call-update) | async-done | bytes 9437200 | tf_op jit(solution)/shard_map/all_gather | solution.py:126
  177.6 76.2 %all-gather.24.cloned.1.call-done = bf16[6144,12,64]{0,2,1:T(8,128)(2,1)} async-done(((bf16[384,12,64]{0,2,1:T(8,128)(2,1)}), bf16[6144,12,64]{0,2,1:T(8,128)(2,1)}) %all-gather.24.cloned.1.call-update) | async-done | bytes 9437200 | tf_op jit(solution)/shard_map/all_gather | solution.py:125
  262.4 154.0 %while.34 = (s32[]{:T(128)}, f32[384,12,64]{0,2,1:T(8,128)S(1)}, f32[12,384]{1,0:T(8,128)S(1)}, bf16[8,768,12,64]{1,3,2,0:T(8,128)(2,1)}, s32[384]{0:T(512)S(1)}...) while((s32[]{:T(128)}, f32[384,12,64]{0,2,1:T(8,128)S(1)}, ...), condition=%wide.region_7.8_spmd.clone, body=%wide.region_3.7_spmd.clone.sunk | while | flops 921122304 | bytes 34605872 | solution.py:143
  283.3 10.4 fusion.174
  350.2 9.8 fusion.175
  420.0 15.7 %multiply_convert_fusion = (bf16[384,3072]{1,0:T(8,128)(2,1)}, f32[384,3072]{1,0:T(8,128)}, f32[384,3072]{1,0:T(8,128)}) fusion(f32[3072]{0:T(1024)S(1)} %bitcast.223, bf16[768,3072]{1,0:T(8,128)(2,1)} %all-gather.30.cloned.1.call-done, f32[384,768]{1,0:T(8,128)S(1)} %get-tuple-element.736, f32[768]{0:T(1024)S(1)} %reshape.392, f32[768]{0:T(1024)S(1)} %reshape.391, ...), kind=kOutput, calls=%fused_computation.90 | convolution fusion | flops 1891270656 | bytes 17716224 | tf_op jit(solution)/shard_map/dot_general | solution.py:161
  457.9 282.3 %while.35 = (s32[]{:T(128)}, f32[384,12,64]{0,2,1:T(8,128)}, bf16[8,768,12,64]{1,3,2,0:T(8,128)(2,1)}, bf16[8,768,12,64]{1,3,2,0:T(8,128)(2,1)}, bf16[8,768,12,6...) while((s32[]{:T(128)}, f32[384,12,64]{0,2,1:T(8,128)}, ...), condition=%wide.region_20.21_spmd.clone, body=%wide.region_17.20_spmd.clone.sunk | while | flops 2287150080 | bytes 150747632 | solution.py:228
  533.8 9.2 fusion.189
  604.3 9.2 fusion.189
  740.2 28.1 %copy.113 = bf16[8,768,12,64]{3,2,1,0:T(8,128)(2,1)} copy(bf16[8,768,12,64]{1,3,2,0:T(8,128)(2,1)} %get-tuple-element.403) | data formatting | bytes 18874368
  768.3 30.0 %reshape.397 = bf16[6144,768]{1,0:T(8,128)(2,1)} reshape(bf16[6144,12,64]{2,1,0:T(8,128)(2,1)} %bitcast.205) | data formatting | bytes 18874368
  798.4 29.0 %copy.115 = bf16[8,768,12,64]{3,2,1,0:T(8,128)(2,1)} copy(bf16[8,768,12,64]{1,3,2,0:T(8,128)(2,1)} %get-tuple-element.404) | data formatting | bytes 18874368
  827.3 30.2 %reshape.399 = bf16[6144,768]{1,0:T(8,128)(2,1)} reshape(bf16[6144,12,64]{2,1,0:T(8,128)(2,1)} %bitcast.206) | data formatting | bytes 18874368
  861.3 48.0 %reduce-scatter.25.cloned.1.call-done = bf16[384,768]{1,0:T(8,128)(2,1)} async-done(((bf16[6144,768]{1,0:T(8,128)(2,1)}), bf16[384,768]{1,0:T(8,128)(2,1)}) %reduce-scatter.25.cloned.1.call-update) | async-done | bytes 589840 | tf_op jit(solution)/shard_map/reshape | solution.py:239
  912.7 111.4 %reduce-scatter.27.cloned.1.call-done = bf16[384,768]{1,0:T(8,128)(2,1)} async-done(((bf16[6144,768]{1,0:T(8,128)(2,1)}), bf16[384,768]{1,0:T(8,128)(2,1)}) %reduce-scatter.27.cloned.1.call-update) | async-done | bytes 589840 | tf_op jit(solution)/shard_map/reshape | solution.py:240
  1050.7 22.4 %reduce-scatter.31.cloned.1.call-done = bf16[384,768]{1,0:T(8,128)(2,1)} async-done(((bf16[768,768]{1,0:T(8,128)(2,1)}), bf16[384,768]{1,0:T(8,128)(2,1)}) %reduce-scatter.31.cloned.1.call-update) | async-done | bytes 589840
  1075.2 22.6 %reduce-scatter.33.cloned.1.call-done = bf16[384,768]{1,0:T(8,128)(2,1)} async-done(((bf16[768,768]{1,0:T(8,128)(2,1)}), bf16[384,768]{1,0:T(8,128)(2,1)}) %reduce-scatter.33.cloned.1.call-update) | async-done | bytes 589840
  1099.9 21.9 %reduce-scatter.19.cloned.1.call-done = bf16[384,768]{1,0:T(8,128)(2,1)} async-done(((bf16[768,768]{1,0:T(8,128)(2,1)}), bf16[384,768]{1,0:T(8,128)(2,1)}) %reduce-scatter.19.cloned.1.call-update) | async-done | bytes 589840 | tf_op jit(solution)/shard_map/reduce_scatter | solution.py:277
  1121.8 62.8 %reduce-scatter.21.cloned.1.call-done = bf16[384,3072]{1,0:T(8,128)(2,1)} async-done(((bf16[768,3072]{1,0:T(8,128)(2,1)}), bf16[384,3072]{1,0:T(8,128)(2,1)}) %reduce-scatter.21.cloned.1.call-update) | async-done | bytes 2359312 | tf_op jit(solution)/shard_map/reduce_scatter | solution.py:289
  1184.6 62.8 %reduce-scatter.23.cloned.1.call-done = bf16[1536,768]{1,0:T(8,128)(2,1)} async-done(((bf16[3072,768]{1,0:T(8,128)(2,1)}), bf16[1536,768]{1,0:T(8,128)(2,1)}) %reduce-scatter.23.cloned.1.call-update) | async-done | bytes 2359312 | tf_op jit(solution)/shard_map/reduce_scatter | solution.py:295
  1260.5 51.3 %all-reduce.9 = (bf16[384]{0:T(512)(128)(2,1)S(1)}, bf16[384]{0:T(512)(128)(2,1)S(1)}, bf16[384]{0:T(512)(128)(2,1)S(1)}, bf16[384]{0:T(512)(128)(2,1)S(1)}, bf1...) all-reduce(bf16[384]{0:T(512)(128)(2,1)S(1)} %dynamic-slice.1, ...), channel_id=1, replica_groups=mesh['ctx'=16,'wa'=2] {'ctx'}, use_global_device_ids=true, to_apply=%region_27.28 | all-reduce | flops 4608 | bytes 18432 | tf_op jit(solution)/shard_map/psum | solution.py:310
  1320.7 83.2 %all-reduce.14.cloned.1.call-done = (bf16[384,768]{0,1:T(8,128)(2,1)}, bf16[384,768]{0,1:T(8,128)(2,1)}, bf16[384,768]{0,1:T(8,128)(2,1)}, bf16[384,768]{1,0:T(8...) async-done(((bf16[384,768]{0,1:T(8,128)(2,1)}, bf16[384,768]{0,1:T(8,128)(2,1)}, bf16[384,768]{0,1:T(8,128)(2,1)}, bf16[384,768]{1,0:T(8,128)(2,1)}, ...) | async-done | bytes 7077904 | tf_op jit(solution)/shard_map/psum | solution.py:309
  (540 shorter events, 553.3 us)
Async XLA Ops:
  7.2 26.7 %all-gather.18.cloned.1.call-start = ((), (), s32[]{:S(2)}) async-start(), calls=%async_computation.8 | async-start | bytes 1769472 | tf_op jit(solution)/shard_map/all_gather | solution.py:82
  9.6 49.2 %all-gather.22.cloned.1.call-start = ((), (), s32[]{:S(2)}) async-start(), calls=%async_computation.10 | async-start | bytes 1769472 | tf_op jit(solution)/shard_map/all_gather | solution.py:81
  10.6 89.7 %all-gather.26.cloned.1.call-start = ((), (), s32[]{:S(2)}) async-start(), calls=%async_computation.12 | async-start | bytes 1769472 | tf_op jit(solution)/shard_map/all_gather | solution.py:79
  11.5 157.6 %all-gather.20.cloned.1.call-start = ((), (), s32[]{:S(2)}) async-start(), calls=%async_computation.9 | async-start | bytes 10027008 | tf_op jit(solution)/shard_map/all_gather | solution.py:126
  36.9 216.9 %all-gather.24.cloned.1.call-start = ((), (), s32[]{:S(2)}) async-start(), calls=%async_computation.11 | async-start | bytes 10027008 | tf_op jit(solution)/shard_map/all_gather | solution.py:125
  61.8 355.6 %all-gather.28.cloned.1.call-start = ((), (), s32[]{:S(2)}) async-start(), calls=%async_computation.13 | async-start | bytes 1769472 | tf_op jit(solution)/shard_map/all_gather | solution.py:84
  62.8 357.3 %all-gather.30.cloned.1.call-start = ((), (), s32[]{:S(2)}) async-start(), calls=%async_computation.14 | async-start | bytes 7077888 | tf_op jit(solution)/shard_map/all_gather | solution.py:148
  66.9 368.8 %all-gather.32.cloned.1.call-start = ((), (), s32[]{:S(2)}) async-start(), calls=%async_computation.15 | async-start | bytes 7077888 | tf_op jit(solution)/shard_map/all_gather | solution.py:150
  71.3 25.3 %copy-start.52 = (f32[384]{0:T(512)S(1)}, f32[384]{0:T(512)}, u32[]{:S(2)}) copy-start(f32[384]{0:T(512)} %param.41) | copy-start | bytes 4612
  71.4 837.9 %reduce-scatter.25.cloned.1.call-start = ((), (), s32[]{:S(2)}) async-start(), calls=%async_computation.19 | async-start | bytes 10027008 | tf_op jit(solution)/shard_map/reshape | solution.py:239
  83.4 370.3 %copy-start.35 = (f32[768]{0:T(1024)}, f32[768]{0:T(1024)S(1)}, u32[]{:S(2)}) copy-start(f32[768]{0:T(1024)S(1)} %reshape.391) | copy-start | bytes 9220
  86.7 349.1 %copy-start.43 = (f32[768]{0:T(1024)}, f32[768]{0:T(1024)S(1)}, u32[]{:S(2)}) copy-start(f32[768]{0:T(1024)S(1)} %reshape.392) | copy-start | bytes 9220
  419.7 34.0 %copy-start.11 = (f32[384,768]{1,0:T(8,128)}, f32[384,768]{1,0:T(8,128)S(1)}, u32[]{:S(2)}) copy-start(f32[384,768]{1,0:T(8,128)S(1)} %get-tuple-element.736) | copy-start | bytes 3538948
  419.7 34.0 %copy-start.33 = (f32[384]{0:T(512)}, f32[384]{0:T(512)S(1)}, u32[]{:S(2)}) copy-start(f32[384]{0:T(512)S(1)} %broadcast_multiply_fusion.1) | copy-start | bytes 4612
  420.0 33.7 %copy-start.37 = (f32[384]{0:T(512)}, f32[384]{0:T(512)S(1)}, u32[]{:S(2)}) copy-start(f32[384]{0:T(512)S(1)} %fusion.98) | copy-start | bytes 4612
  798.3 225.8 %reduce-scatter.27.cloned.1.call-start = ((), (), s32[]{:S(2)}) async-start(), calls=%async_computation.20 | async-start | bytes 10027008 | tf_op jit(solution)/shard_map/reshape | solution.py:240
  857.6 191.0 %reduce-scatter.29.cloned.1.call-start = ((), (), s32[]{:S(2)}) async-start(), calls=%async_computation.21 | async-start | bytes 1769472
  861.3 211.8 %reduce-scatter.31.cloned.1.call-start = ((), (), s32[]{:S(2)}) async-start(), calls=%async_computation.22 | async-start | bytes 1769472
  912.6 185.2 %reduce-scatter.33.cloned.1.call-start = ((), (), s32[]{:S(2)}) async-start(), calls=%async_computation.23 | async-start | bytes 1769472
  1027.5 94.3 %reduce-scatter.19.cloned.1.call-start = ((), (), s32[]{:S(2)}) async-start(), calls=%async_computation.16 | async-start | bytes 1769472 | tf_op jit(solution)/shard_map/reduce_scatter | solution.py:277
  1029.4 155.2 %reduce-scatter.21.cloned.1.call-start = ((), (), s32[]{:S(2)}) async-start(), calls=%async_computation.17 | async-start | bytes 7077888 | tf_op jit(solution)/shard_map/reduce_scatter | solution.py:289
  1035.7 211.7 %reduce-scatter.23.cloned.1.call-start = ((), (), s32[]{:S(2)}) async-start(), calls=%async_computation.18 | async-start | bytes 7077888 | tf_op jit(solution)/shard_map/reduce_scatter | solution.py:295
  1043.3 360.5 %all-reduce.14.cloned.1.call-start = ((), (), s32[]{:S(2)}) async-start(), calls=%async_computation.24 | async-start | bytes 14155776 | tf_op jit(solution)/shard_map/psum | solution.py:309
  1253.0 66.2 %copy-start.17 = (bf16[768,768]{1,0:T(8,128)(2,1)S(1)}, bf16[768,768]{1,0:T(8,128)(2,1)}, u32[]{:S(2)}) copy-start(bf16[768,768]{1,0:T(8,128)(2,1)} %all-gather.18.cloned.1.call-done) | copy-start | bytes 3538948
  (95 other events, 506.5 us)
Sparse Core Ops, SparseCore 0:
  10.1 23.7 all-gather.17
  36.0 22.7 all-gather.21
  60.9 22.8 all-gather.25
  86.4 82.6 all-gather.19
  171.7 82.0 all-gather.23
  255.8 22.1 all-gather.27
  280.1 62.6 all-gather.29
  344.4 62.6 all-gather.31
  798.5 110.7 reduce-scatter.24
  913.2 110.8 reduce-scatter.26
  1026.9 21.5 reduce-scatter.28
  1051.2 21.8 reduce-scatter.30
  1075.9 21.8 reduce-scatter.32
  1099.9 21.8 reduce-scatter.18
  1124.5 60.0 reduce-scatter.20
  1187.3 60.0 reduce-scatter.22
  1252.3 151.5 all-reduce.13
where the time goes:
time: 1430 us; the launch traced here: 1420 us
  waiting for transfers between devices  624 us (44%)
  matrix products  463 us (32%)
  local copies, waits for them, and re-layouts  176 us (12%)
  blocking collectives  88.4 us (6%)
  other arithmetic  42.1 us (3%)
  between operations  16.7 us (1%)
    unnamed x140, local copies, waits for them, and re-layouts  137 us
    reshape x1, waiting for transfers between devices, body(): d_values = value_sum.astype(low_type).reshape(tok_rows, width)  111 us
    psum x1, waiting for transfers between devices, body(): lax.psum(shards[0].astype(jnp.bfloat16), 'ctx').astype(jnp.float32)  83.2 us
    all_gather x1, waiting for transfers between devices, body(): lax.all_gather(key_proj, 'ctx', axis=0, tiled=True)  76.2 us
    dot_general x8, matrix products, block_scores(): jnp.einsum('qhd,khd->hqk', d_acc, value_blk, preferred_element_type=jnp.f...  73.6 us
    dot_general x8, matrix products, forward_block(): jnp.einsum('qhd,khd->hqk', query_proj, key_blk, preferred_element_type=jn...  73.4 us
    dot_general x8, matrix products, backward_block(): jnp.einsum('hqk,qhd->khd', expo.astype(low_type), d_acc, preferred_elemen...  68.4 us
    all_gather x1, waiting for transfers between devices, body(): lax.all_gather(value_proj, 'ctx', axis=0, tiled=True)  66.6 us
  transfers between devices with their start and end apart: 17, of which 13 were waited for; matrix products, arithmetic and copies ran while one was open for 22% of the time, Pallas kernels for 0%

commit v1 on v0

v1 whole, which is shorter than its diff:
```python
from functools import partial

import jax
import jax.numpy as jnp
from jax import lax
from jax.experimental import pallas as pl
from jax.experimental.pallas import tpu as pltpu
from jax.sharding import PartitionSpec as P

HEADS = 12
HEAD_DIM = 64
LANES = 128
TILE = 512
FAR = -(2.0**40)
VMEM_BYTES = 60 << 20

low_type = jnp.bfloat16
epsilon = 1e-05


def dot_nt(left, right):
    return lax.dot_general(
        left, right, (((1,), (1,)), ((), ())), preferred_element_type=jnp.float32
    )


def dot_nn(left, right):
    return lax.dot_general(
        left, right, (((1,), (0,)), ((), ())), preferred_element_type=jnp.float32
    )


def layer_norm(hidden, gain_vec, shift_vec):
    centre = hidden - jnp.mean(hidden, axis=-1, keepdims=True)
    spread = jnp.mean(centre * centre, axis=-1, keepdims=True)
    return centre * lax.rsqrt(spread + epsilon) * gain_vec + shift_vec


def segment_of(position, seq_ends):
    return jnp.sum((position[:, None] >= seq_ends[None, :]).astype(jnp.int32), axis=1)


def owner_of(head, count):
    return head * count // HEADS


def greet_all(count, me):
    barrier = pltpu.get_barrier_semaphore()

    def greet(step, _):
        other = lax.rem(me + step, count)
        pl.semaphore_signal(
            barrier, inc=1, device_id={"ctx": other}, device_id_type=pl.DeviceIdType.MESH
        )
        return 0

    lax.fori_loop(1, count, greet, 0)
    pl.semaphore_wait(barrier, count - 1)


def to_heads_kernel(count, send_ref, recv_ref, send_sem, recv_sem, own_sem):
    me = lax.axis_index("ctx")
    greet_all(count, me)
    first = me * HEADS // count + 1

    def copy_for(head, source, owner):
        return pltpu.make_async_remote_copy(
            src_ref=send_ref.at[head],
            dst_ref=recv_ref.at[source],
            send_sem=send_sem.at[head],
            recv_sem=recv_sem.at[source],
            device_id={"ctx": owner},
            device_id_type=pl.DeviceIdType.MESH,
        )

    def own_copy(head):
        return pltpu.make_async_copy(send_ref.at[head], recv_ref.at[me], own_sem)

    def begin(step, _):
        head = lax.rem(first + step, HEADS)
        owner = owner_of(head, count)

        @pl.when(owner != me)
        def _():
            copy_for(head, me, owner).start()

        @pl.when(owner == me)
        def _():
            own_copy(head).start()

        return 0

    lax.fori_loop(0, HEADS, begin, 0)

    def finish(head, _):
        owner = owner_of(head, count)

        @pl.when(owner != me)
        def _():
            copy_for(head, me, owner).wait_send()

        @pl.when(owner == me)
        def _():
            own_copy(head).wait()

            def arrive(source, _):
                @pl.when(source != me)
                def _():
                    copy_for(head, source, owner).wait_recv()

                return 0

            lax.fori_loop(0, count, arrive, 0)

        return 0

    lax.fori_loop(0, HEADS, finish, 0)


def to_heads(send, count, collective_id):
    rows = send.shape[1]
    return pl.pallas_call(
        partial(to_heads_kernel, count),
        out_shape=jax.ShapeDtypeStruct((count, rows, LANES), low_type),
        in_specs=[pl.BlockSpec(memory_space=pltpu.VMEM)],
        out_specs=pl.BlockSpec(memory_space=pltpu.VMEM),
        scratch_shapes=[
            pltpu.SemaphoreType.DMA((HEADS,)),
            pltpu.SemaphoreType.DMA((count,)),
            pltpu.SemaphoreType.DMA,
        ],
        compiler_params=pltpu.CompilerParams(
            collective_id=collective_id, has_side_effects=True, vmem_limit_bytes=VMEM_BYTES
        ),
        cost_estimate=pl.CostEstimate(
            flops=rows * 40_000_000, bytes_accessed=send.size * 4, transcendentals=0
        ),
        name=f"to_heads_{rows}",
    )(send)


def to_rows_kernel(count, send_ref, recv_ref, send_sem, recv_sem, own_sem):
    me = lax.axis_index("ctx")
    greet_all(count, me)

    def copy_for(head, target):
        return pltpu.make_async_remote_copy(
            src_ref=send_ref.at[target],
            dst_ref=recv_ref.at[head],
            send_sem=send_sem.at[target],
            recv_sem=recv_sem.at[head],
            device_id={"ctx": target},
            device_id_type=pl.DeviceIdType.MESH,
        )

    def own_copy(head):
        return pltpu.make_async_copy(send_ref.at[me], recv_ref.at[head], own_sem)

    def begin(head, _):
        @pl.when(owner_of(head, count) == me)
        def _():
            own_copy(head).start()

            def push(step, _):
                copy_for(head, lax.rem(me + step, count)).start()
                return 0

            lax.fori_loop(1, count, push, 0)

        return 0

    lax.fori_loop(0, HEADS, begin, 0)

    def finish(head, _):
        @pl.when(owner_of(head, count) == me)
        def _():
            own_copy(head).wait()

            def leave(step, _):
                copy_for(head, lax.rem(me + step, count)).wait_send()
                return 0

            lax.fori_loop(1, count, leave, 0)

        @pl.when(owner_of(head, count) != me)
        def _():
            copy_for(head, me).wait_recv()

        return 0

    lax.fori_loop(0, HEADS, finish, 0)


def to_rows(send, count, collective_id):
    rows = send.shape[1]
    return pl.pallas_call(
        partial(to_rows_kernel, count),
        out_shape=jax.ShapeDtypeStruct((HEADS, rows, LANES), low_type),
        in_specs=[pl.BlockSpec(memory_space=pltpu.VMEM)],
        out_specs=pl.BlockSpec(memory_space=pltpu.VMEM),
        scratch_shapes=[
            pltpu.SemaphoreType.DMA((count,)),
            pltpu.SemaphoreType.DMA((HEADS,)),
            pltpu.SemaphoreType.DMA,
        ],
        compiler_params=pltpu.CompilerParams(
            collective_id=collective_id, has_side_effects=True, vmem_limit_bytes=VMEM_BYTES
        ),
        cost_estimate=pl.CostEstimate(
            flops=rows * 40_000_000, bytes_accessed=send.size * 4, transcendentals=0
        ),
        name=f"to_rows_{rows}",
    )(send)


def project_kernel(x_ref, wq_ref, wkv_ref, bq_ref, bkv_ref, out_ref):
    rows = x_ref.shape[0]
    half = rows // 2
    step = 4
    for base in range(0, HEADS, step):
        cols = slice(base * LANES, (base + step) * LANES)
        both = (dot_nn(x_ref[...], wkv_ref[:, cols]) + bkv_ref[:, cols]).astype(low_type)
        for at in range(step):
            out_ref[base + at, 0:rows, :] = both[:, at * LANES : (at + 1) * LANES]
        cols = slice(base * HEAD_DIM, (base + step) * HEAD_DIM)
        query = ((dot_nn(x_ref[...], wq_ref[:, cols]) + bq_ref[:, cols]) * 0.125).astype(low_type)
        for at in range(step):
            lanes = slice(at * HEAD_DIM, (at + 1) * HEAD_DIM)
            out_ref[base + at, rows : rows + half, :] = jnp.concatenate(
                [query[:half, lanes], query[half:, lanes]], axis=1
            )


def project(x, wq, wkv, bq, bkv):
    rows = x.shape[0]
    vmem = pl.BlockSpec(memory_space=pltpu.VMEM)
    return pl.pallas_call(
        project_kernel,
        out_shape=jax.ShapeDtypeStruct((HEADS, rows + rows // 2, LANES), low_type),
        in_specs=[vmem] * 5,
        out_specs=vmem,
        compiler_params=pltpu.CompilerParams(vmem_limit_bytes=VMEM_BYTES),
        name="project",
    )(x, wq, wkv, bq, bkv)


def tile_range(meta_ref, first, last, total):
    end_a, end_b, end_c = meta_ref[0], meta_ref[1], meta_ref[2]
    low = jnp.where(
        first >= end_c, end_c, jnp.where(first >= end_b, end_b, jnp.where(first >= end_a, end_a, 0))
    )
    high = jnp.where(
        last >= end_c,
        total,
        jnp.where(last >= end_b, end_c, jnp.where(last >= end_a, end_b, end_a)),
    )
    return low // TILE, (high + TILE - 1) // TILE


def attend_kernel(meta_ref, order_ref, recv_ref, out_ref, qa_ref, ka_ref, va_ref, sum_ref):
    count = recv_ref.shape[0]
    half = recv_ref.shape[1] // 3
    total = qa_ref.shape[0]

    @pl.when(meta_ref[3] == 1)
    def _():
        lane = lax.broadcasted_iota(jnp.int32, (half, LANES), 1)
        lower = lane < HEAD_DIM
        row = lax.broadcasted_iota(jnp.int32, (half, LANES), 0)

        def place(source, _):
            query = recv_ref[source, 2 * half :, :].astype(jnp.float32)
            for part in range(2):
                first = pl.multiple_of(order_ref[2 * source + part] * half, half)
                position = first + row
                segment = (
                    (position >= meta_ref[0]).astype(jnp.int32)
                    + (position >= meta_ref[1]).astype(jnp.int32)
                    + (position >= meta_ref[2]).astype(jnp.int32)
                )
                mine = (lane - HEAD_DIM) == segment
                other = (lane < HEAD_DIM + 4) & (~mine)
                pair = recv_ref[source, part * half : (part + 1) * half, :].astype(jnp.float32)
                if part == 1:
                    query = pltpu.roll(query, HEAD_DIM, 1)
                mark_k = jnp.where(
                    other, FAR, jnp.where((lane >= HEAD_DIM + 4) & (lane < HEAD_DIM + 7), 1.0, 0.0)
                )
                rows = pl.ds(first, half)
                qa_ref[rows, :] = jnp.where(lower, query, jnp.where(mine, 1.0, 0.0)).astype(low_type)
                ka_ref[rows, :] = jnp.where(lower, pair, mark_k).astype(low_type)
                va_ref[rows, :] = jnp.where(lower, 1.0, pair).astype(low_type)
            return 0

        lax.fori_loop(0, count, place, 0)

        def query_step(index, _):
            first = pl.multiple_of(index * TILE, TILE)
            rows = pl.ds(first, TILE)
            begin, end = tile_range(meta_ref, first, first + TILE - 1, total)
            query = qa_ref[rows, :]
            sum_ref[rows, :] = jnp.zeros((TILE, LANES), jnp.float32)

            def key_step(key_index, _):
                keys = pl.ds(pl.multiple_of(key_index * TILE, TILE), TILE)
                expo = jnp.exp(dot_nt(query, ka_ref[keys, :])).astype(low_type)
                sum_ref[rows, :] += dot_nn(expo, va_ref[keys, :])
                return 0

            lax.fori_loop(begin, end, key_step, 0)
            return 0

        lax.fori_loop(0, total // TILE, query_step, 0)

        def give(source, _):
            parts = []
            for part in range(2):
                first = pl.multiple_of(order_ref[2 * source + part] * half, half)
                block = sum_ref[pl.ds(first, half), :]
                parts.append((block, pltpu.roll(block, HEAD_DIM, 1)))
            top = jnp.where(lower, parts[0][1], parts[1][0])
            bottom = jnp.where(lower, parts[0][0], parts[1][1])
            out_ref[source] = (top / bottom).astype(low_type)
            return 0

        lax.fori_loop(0, count, give, 0)


def attend(meta, order, recv):
    count, rows, _ = recv.shape
    total = count * rows * 2 // 3
    vmem = pl.BlockSpec(memory_space=pltpu.VMEM)
    smem = pl.BlockSpec(memory_space=pltpu.SMEM)
    whole = jax.ShapeDtypeStruct((total, LANES), low_type)
    return pl.pallas_call(
        attend_kernel,
        out_shape=(
            jax.ShapeDtypeStruct((count, rows // 3, LANES), low_type),
            whole,
            whole,
            whole,
            jax.ShapeDtypeStruct((total, LANES), jnp.float32),
        ),
        in_specs=[smem, smem, vmem],
        out_specs=(vmem,) * 5,
        compiler_params=pltpu.CompilerParams(vmem_limit_bytes=VMEM_BYTES),
        cost_estimate=pl.CostEstimate(
            flops=total * total * LANES * 8, bytes_accessed=total * LANES * 12, transcendentals=0
        ),
        name="attend",
    )(meta, order, recv)


def split_three(value):
    first = value.astype(low_type).astype(jnp.float32)
    rest = value - first
    second = rest.astype(low_type).astype(jnp.float32)
    return first, second, rest - second


def attend_back_kernel(
    meta_ref,
    order_ref,
    recv_ref,
    qa_ref,
    ka_ref,
    va_ref,
    sum_ref,
    out_ref,
    qb_ref,
    da_ref,
    kt_ref,
    dkv_ref,
    dq_ref,
    acc_ref,
):
    count = recv_ref.shape[0]
    half = recv_ref.shape[1]
    total = qa_ref.shape[0]

    @pl.when(meta_ref[3] == 1)
    def _():
        lane = lax.broadcasted_iota(jnp.int32, (half, LANES), 1)
        lower = lane < HEAD_DIM

        def place(source, _):
            given = recv_ref[source].astype(jnp.float32)
            for part in range(2):
                first = pl.multiple_of(order_ref[2 * source + part] * half, half)
                rows = pl.ds(first, half)
                block = sum_ref[rows, :]
                turned = pltpu.roll(block, HEAD_DIM, 1)
                d_context = pltpu.roll(given, HEAD_DIM, 1) if part == 0 else given
                product = jnp.where(lower, 0.0, d_context * (block / turned))
                minus = -jnp.sum(product, axis=1, keepdims=True)
                one, two, three = split_three(minus)
                mark = jnp.where(
                    lane == 0, one, jnp.where(lane == 1, two, jnp.where(lane == 2, three, 0.0))
                )
                da_ref[rows, :] = jnp.where(lower, mark, d_context).astype(low_type)
                one, two, three = split_three(-jnp.log(turned))
                at = lane - (HEAD_DIM + 4)
                mark = jnp.where(at == 0, one, jnp.where(at == 1, two, three))
                query = qa_ref[rows, :].astype(jnp.float32)
                qb_ref[rows, :] = jnp.where((at >= 0) & (at < 3), mark, query).astype(low_type)
            return 0

        lax.fori_loop(0, count, place, 0)

        def prepare(index, _):
            rows = pl.ds(pl.multiple_of(index * TILE, TILE), TILE)
            kt_ref[:, rows] = jnp.transpose(ka_ref[rows, :])[:HEAD_DIM, :]
            dkv_ref[rows, :] = jnp.zeros((TILE, LANES), jnp.float32)
            return 0

        lax.fori_loop(0, total // TILE, prepare, 0)

        lower_tile = lax.broadcasted_iota(jnp.int32, (TILE, LANES), 1) < HEAD_DIM

        def query_step(index, _):
            first = pl.multiple_of(index * TILE, TILE)
            rows = pl.ds(first, TILE)
            begin, end = tile_range(meta_ref, first, first + TILE - 1, total)
            query = qb_ref[rows, :]
            given = da_ref[rows, :]
            query_only = jnp.where(lower_tile, query.astype(jnp.float32), 0.0).astype(low_type)
            given_only = jnp.where(lower_tile, 0.0, given.astype(jnp.float32)).astype(low_type)
            acc_ref[...] = jnp.zeros_like(acc_ref)

            def key_step(key_index, _):
                keys = pl.ds(pl.multiple_of(key_index * TILE, TILE), TILE)
                prob = jnp.exp(dot_nt(ka_ref[keys, :], query))
                d_scores = (prob * dot_nt(va_ref[keys, :], given)).astype(low_type)
                dkv_ref[keys, :] += dot_nn(d_scores, query_only) + dot_nn(
                    prob.astype(low_type), given_only
                )
                acc_ref[...] += dot_nn(kt_ref[:, keys], d_scores)
                return 0

            lax.fori_loop(begin, end, key_step, 0)
            dq_ref[rows, :] = jnp.transpose(acc_ref[...])
            return 0

        lax.fori_loop(0, total // TILE, query_step, 0)

        def give(source, _):
            queries = []
            for part in range(2):
                first = pl.multiple_of(order_ref[2 * source + part] * half, half)
                rows = pl.ds(first, half)
                out_ref[source, part * half : (part + 1) * half, :] = dkv_ref[rows, :].astype(low_type)
                queries.append(dq_ref[rows, :])
            out_ref[source, 2 * half :, :] = jnp.concatenate(queries, axis=1).astype(low_type)
            return 0

        lax.fori_loop(0, count, give, 0)


def attend_back(meta, order, recv, qa, ka, va, sums):
    count, half, _ = recv.shape
    total = qa.shape[0]
    vmem = pl.BlockSpec(memory_space=pltpu.VMEM)
    smem = pl.BlockSpec(memory_space=pltpu.SMEM)
    return pl.pallas_call(
        attend_back_kernel,
        out_shape=jax.ShapeDtypeStruct((count, 3 * half, LANES), low_type),
        in_specs=[smem, smem] + [vmem] * 5,
        out_specs=vmem,
        scratch_shapes=[
            pltpu.VMEM((total, LANES), low_type),
            pltpu.VMEM((total, LANES), low_type),
            pltpu.VMEM((HEAD_DIM, total), low_type),
            pltpu.VMEM((total, LANES), jnp.float32),
            pltpu.VMEM((total, HEAD_DIM), jnp.float32),
            pltpu.VMEM((HEAD_DIM, TILE), jnp.float32),
        ],
        compiler_params=pltpu.CompilerParams(vmem_limit_bytes=VMEM_BYTES),
        cost_estimate=pl.CostEstimate(
            flops=total * total * LANES * 16, bytes_accessed=total * LANES * 16, transcendentals=0
        ),
        name="attend_back",
    )(meta, order, recv, qa, ka, va, sums)


def pack_columns(vectors, rows):
    columns = jnp.stack([vec.astype(low_type) for vec in vectors], axis=1)
    return jnp.pad(columns, ((0, 0), (0, LANES - len(vectors))))


def column_sums(terms):
    block = jnp.stack([jnp.sum(term, axis=0) for term in terms], axis=1).astype(low_type)
    return jnp.pad(block, ((0, 0), (0, LANES - len(terms))))


def rows_of_columns(block, wanted):
    pick = jnp.eye(LANES, 8, dtype=low_type)
    return jnp.einsum("fk,kj->jf", block, pick, preferred_element_type=jnp.float32)[:wanted]


def reduce_shards(grad):
    part = lax.psum_scatter(
        grad.astype(low_type), ("wa", "ctx"), scatter_dimension=0, tiled=True
    )
    return lax.all_gather(part, "ctx", axis=0, tiled=True)


def body(
    count,
    tokens,
    cotangent,
    lengths,
    block_order,
    w_query,
    b_query,
    w_key,
    w_value,
    b_value,
    w_out,
    b_out,
    gain_one,
    shift_one,
    w_up,
    b_up,
    w_down,
    b_down,
    gain_two,
    shift_two,
):
    inputs = tokens[0]
    tok_rows, width = inputs.shape
    wide = w_up.shape[1]
    half = tok_rows // 2
    shard = w_query.shape[0]
    me = lax.axis_index("ctx")
    seq_ends = jnp.cumsum(lengths[0])
    own_blocks = lax.dynamic_slice(block_order, (2 * me,), (2,))
    position = (own_blocks[:, None] * half + jnp.arange(half, dtype=jnp.int32)[None, :]).reshape(-1)
    own_seg = segment_of(position, seq_ends)
    owns = jnp.any(me == jnp.arange(HEADS, dtype=jnp.int32) * count // HEADS).astype(jnp.int32)
    meta = jnp.concatenate([seq_ends.astype(jnp.int32), owns[None]])

    def gather_rows(shard_block):
        return lax.all_gather(shard_block, "wa", axis=0, tiled=True)

    pair = jnp.stack(
        [
            w_key.astype(low_type).reshape(shard, HEADS, HEAD_DIM),
            w_value.astype(low_type).reshape(shard, HEADS, HEAD_DIM),
        ],
        axis=2,
    ).reshape(shard, 2 * width)
    vectors = pack_columns(
        [b_query, b_value, b_out, gain_one, shift_one, gain_two, shift_two, b_down], shard
    )
    first_pack = gather_rows(
        jnp.concatenate([w_query.astype(low_type), pair, vectors], axis=1)
    )
    query_weight = first_pack[:, :width]
    pair_weight = first_pack[:, width : 3 * width]
    vector_rows = rows_of_columns(first_pack[:, 3 * width :], 8)
    query_bias, value_bias, out_bias, gain_first, shift_first, gain_second, shift_second, down_bias = (
        vector_rows[index] for index in range(8)
    )
    pair_bias = jnp.stack(
        [jnp.zeros((HEADS, HEAD_DIM), jnp.float32), value_bias.reshape(HEADS, HEAD_DIM)], axis=1
    ).reshape(1, 2 * width)

    out_weight = gather_rows(w_out.astype(low_type))
    up_weight = gather_rows(w_up.astype(low_type))
    down_pack = gather_rows(
        jnp.concatenate([w_down.astype(low_type), pack_columns([b_up], 4 * shard)], axis=1)
    )
    down_weight = down_pack[:, :width]
    up_bias = rows_of_columns(down_pack[:, width:], 1)[0]

    packed = project(inputs, query_weight, pair_weight, query_bias[None, :], pair_bias)
    at_head = to_heads(packed, count, 0)
    context_out, qa, ka, va, sums = attend(meta, block_order, at_head)
    context_in = to_rows(context_out, count, 1)
    context_low = (
        context_in.reshape(HEADS, half, 2, HEAD_DIM).transpose(2, 1, 0, 3).reshape(tok_rows, width)
    )

    attn_out = jnp.dot(context_low, out_weight, preferred_element_type=jnp.float32) + out_bias
    h_one = inputs.astype(jnp.float32) + attn_out
    norm_one, norm_one_back = jax.vjp(layer_norm, h_one, gain_first, shift_first)
    norm_low = norm_one.astype(low_type)
    up_pre = jnp.dot(norm_low, up_weight, preferred_element_type=jnp.float32) + up_bias
    gelu_out, gelu_back = jax.vjp(partial(jax.nn.gelu, approximate=False), up_pre)
    gelu_low = gelu_out.astype(low_type)
    down_out = jnp.dot(gelu_low, down_weight, preferred_element_type=jnp.float32) + down_bias
    h_two = norm_one + down_out
    result, norm_two_back = jax.vjp(layer_norm, h_two, gain_second, shift_second)
    activations = result.astype(low_type)[None]
    valid = (own_seg < 3).astype(jnp.float32)
    g_out = cotangent[0].astype(jnp.float32) * valid[:, None]
    d_htwo, grad_gain_second, grad_shift_second = norm_two_back(g_out)
    d_down = d_htwo.astype(low_type)
    d_gelu = jnp.einsum("td,fd->tf", d_down, down_weight, preferred_element_type=jnp.float32)
    (d_uppre,) = gelu_back(d_gelu)
    d_up = d_uppre.astype(low_type)
    d_yone = d_htwo + jnp.einsum("tf,df->td", d_up, up_weight, preferred_element_type=jnp.float32)
    d_hone, grad_gain_first, grad_shift_first = norm_one_back(d_yone)
    d_attn = d_hone.astype(low_type)
    d_context = jnp.einsum("td,cd->tc", d_attn, out_weight, preferred_element_type=jnp.float32)
    context_back = (
        d_context.astype(low_type)
        .reshape(2, half, HEADS, HEAD_DIM)
        .transpose(2, 1, 0, 3)
        .reshape(HEADS, half, LANES)
    )

    grad_wdown = jnp.einsum("tf,td->fd", gelu_low, d_down, preferred_element_type=jnp.float32)
    grad_wup = jnp.einsum("td,tf->df", norm_low, d_up, preferred_element_type=jnp.float32)
    grad_wout = jnp.einsum("tc,td->cd", context_low, d_attn, preferred_element_type=jnp.float32)
    down_block = jnp.concatenate(
        [grad_wdown.astype(low_type), column_sums([d_up.astype(jnp.float32)])], axis=1
    )
    vec_block = jnp.stack(
        [
            jnp.sum(d_attn.astype(jnp.float32), axis=0),
            grad_gain_first,
            grad_shift_first,
            jnp.sum(d_down.astype(jnp.float32), axis=0),
            grad_gain_second,
            grad_shift_second,
        ],
        axis=1,
    ).astype(low_type)
    out_block = jnp.concatenate(
        [grad_wout.astype(low_type), jnp.pad(vec_block, ((0, 0), (0, LANES - 6)))], axis=1
    )
    up_block = grad_wup.astype(low_type)
    context_back, down_block, out_block, up_block = lax.optimization_barrier(
        (context_back, down_block, out_block, up_block)
    )
    up_sum = reduce_shards(up_block)
    down_sum = reduce_shards(down_block)
    out_sum = reduce_shards(out_block)

    back_at_head = to_heads(context_back, count, 2)
    grads_out = attend_back(meta, block_order, back_at_head, qa, ka, va, sums)
    grads_in = to_rows(grads_out, count, 3)

    d_pair = grads_in[:, :tok_rows, :].transpose(1, 0, 2).reshape(tok_rows, 2 * width)
    d_queries = (
        grads_in[:, tok_rows:, :]
        .reshape(HEADS, half, 2, HEAD_DIM)
        .transpose(2, 1, 0, 3)
        .reshape(tok_rows, width)
        * jnp.asarray(0.125, low_type)
    )
    d_all = jnp.concatenate([d_queries, d_pair], axis=1)
    grad_all = jnp.einsum("tc,td->cd", inputs, d_all, preferred_element_type=jnp.float32)
    d_values = d_pair.reshape(tok_rows, HEADS, 2, HEAD_DIM)[:, :, 1, :].reshape(tok_rows, width)
    last_block = jnp.concatenate(
        [
            grad_all.astype(low_type),
            column_sums([d_queries.astype(jnp.float32), d_values.astype(jnp.float32)]),
        ],
        axis=1,
    )
    last_sum = reduce_shards(last_block)
    d_input = (
        d_hone
        + jnp.einsum("td,cd->tc", d_queries, query_weight, preferred_element_type=jnp.float32)
        + jnp.einsum("td,cd->tc", d_pair, pair_weight, preferred_element_type=jnp.float32)
    )
    input_grad = d_input.astype(low_type)[None]

    wide_grad = last_sum.astype(jnp.float32)
    pair_grad = wide_grad[:, width : 3 * width].reshape(shard, HEADS, 2, HEAD_DIM)
    out_grad = out_sum.astype(jnp.float32)
    down_grad = down_sum.astype(jnp.float32)
    return (
        activations,
        input_grad,
        wide_grad[:, :width],
        wide_grad[:, 3 * width],
        pair_grad[:, :, 0, :].reshape(shard, width),
        pair_grad[:, :, 1, :].reshape(shard, width),
        wide_grad[:, 3 * width + 1],
        out_grad[:, :width],
        out_grad[:, width],
        out_grad[:, width + 1],
        out_grad[:, width + 2],
        up_sum.astype(jnp.float32),
        down_grad[:, width],
        down_grad[:, :width],
        out_grad[:, width + 3],
        out_grad[:, width + 4],
        out_grad[:, width + 5],
    )


def solution(mesh):
    placed = (
        P("wa", "ctx", None),
        P("wa", "ctx", None),
        P("wa", None),
        P(),
        P("wa", None),
        P("wa"),
        P("wa", None),
        P("wa", None),
        P("wa"),
        P("wa", None),
        P("wa"),
        P("wa"),
        P("wa"),
        P("wa", None),
        P("wa"),
        P("wa", None),
        P("wa"),
        P("wa"),
        P("wa"),
    )
    return jax.shard_map(
        partial(body, mesh.shape["ctx"]),
        mesh=mesh,
        in_specs=placed,
        out_specs=(
            P("wa", "ctx", None),
            P("wa", "ctx", None),
            P("wa", None),
            P("wa"),
            P("wa", None),
            P("wa", None),
            P("wa"),
            P("wa", None),
            P("wa"),
            P("wa"),
            P("wa"),
            P("wa", None),
            P("wa"),
            P("wa", None),
            P("wa"),
            P("wa"),
            P("wa"),
        ),
        check_vma=False,
    )
```

time: 1430 us -> 970 us (0.68)
  matrix products: 463 us -> 50 us
  Pallas kernels: 0 us -> 248 us
  local copies, waits for them, and re-layouts: 176 us -> 57.2 us
  waiting for transfers between devices: 624 us -> 519 us
  blocking collectives: 88.4 us -> 22.3 us
    dot_general x64 -> x4, matrix products: 414 us -> 8.69 us  [the longest x1 3.27 us: body(): jnp.einsum('tc,td->cd', inputs, d_all, preferred_element_type=jnp.float32)]
    pallas_call x0 -> x7, Pallas kernels: none -> 248 us  [the longest x2 82.4 us: to_rows(): pl.pallas_call(partial(to_rows_kernel, count), out_shape=jax.ShapeDtypeSt...]
    reshape x2 -> x0, waiting for transfers between devices: 159 us -> none  [the longest x1 111 us: body(): d_values = value_sum.astype(low_type).reshape(tok_rows, width)]
    unnamed x140 -> x69, local copies, waits for them, and re-layouts: 137 us -> 22.5 us
    unnamed x20 -> x11, waiting for transfers between devices: 50.5 us -> 136 us
    psum x1 -> x0, waiting for transfers between devices: 83.2 us -> none  [body(): lax.psum(shards[0].astype(jnp.bfloat16), 'ctx').astype(jnp.float32)]
    reduce_scatter x3 -> x2, waiting for transfers between devices: 148 us -> 225 us  [reduce_shards(): lax.psum_scatter(grad.astype(low_type), ('wa', 'ctx'), scatter_dimension=...]
    psum x1 -> x0, blocking collectives: 51.3 us -> none  [body(): lax.psum(shards[1].astype(jnp.bfloat16), 'ctx').astype(jnp.float32)]
  transfers between devices with their start and end apart: 17 -> 10, of which waited for: 13 -> 8; matrix products, arithmetic and copies ran while one was open for 22% -> 7% of each run, Pallas kernels for 0% -> 12%
where the time goes in v1:
time: 970 us; the launch traced here: 958 us
  waiting for transfers between devices  519 us (54%)
  Pallas kernels  248 us (26%)
  local copies, waits for them, and re-layouts  57.2 us (6%)
  matrix products  50 us (5%)
  other arithmetic  44.1 us (5%)
  blocking collectives  22.3 us (2%)
  between operations  16.6 us (2%)
    reduce_scatter x2, waiting for transfers between devices, reduce_shards(): lax.psum_scatter(grad.astype(low_type), ('wa', 'ctx'), scatter_dimension=...  225 us
    unnamed x11, waiting for transfers between devices  136 us
    pallas_call x2, Pallas kernels, to_rows(): pl.pallas_call(partial(to_rows_kernel, count), out_shape=jax.ShapeDtypeSt...  82.4 us
    all_gather x3, waiting for transfers between devices, reduce_shards(): return lax.all_gather(part, 'ctx', axis=0, tiled=True)  82.1 us
    all_gather x4, waiting for transfers between devices, gather_rows(): return lax.all_gather(shard_block, 'wa', axis=0, tiled=True)  77 us
    pallas_call x2, Pallas kernels, to_heads(): pl.pallas_call(partial(to_heads_kernel, count), out_shape=jax.ShapeDtypeS...  64.2 us
    pallas_call x1, Pallas kernels, attend_back(): pl.pallas_call(attend_back_kernel, out_shape=jax.ShapeDtypeStruct((count,...  59.5 us
    pallas_call x1, Pallas kernels, attend(): pl.pallas_call(attend_kernel, out_shape=(jax.ShapeDtypeStruct((count, row...  36.4 us
  transfers between devices with their start and end apart: 10, of which 8 were waited for; matrix products, arithmetic and copies ran while one was open for 7% of the time, Pallas kernels for 12%

profile of v1, /device:TPU:9, one launch (start us, length us, event | category | flops | bytes accessed | tf_op | source)
XLA Modules:
  0.0 957.9 jit_solution(4150947741185200620)
XLA Ops:
  25.1 4.2 convert_element_type.173
  32.5 39.7 %all-gather.8.cloned.1.call-done = bf16[768,2432]{1,0:T(8,128)(2,1)} async-done(((bf16[384,2432]{1,0:T(8,128)(2,1)}), bf16[768,2432]{1,0:T(8,128)(2,1)}) %all-gather.8.cloned.1.call-update) | async-done | bytes 3735568 | tf_op jit(solution)/shard_map/all_gather | solution.py:543
  80.8 5.3 project.1.send_ref
  86.1 45.2 %to_heads_576.1.recv_ref = bf16[16,576,128]{2,1,0:T(8,128)(2,1)} custom-call(bf16[12,576,128]{2,1,0:T(8,128)(2,1)} %project.1.send_ref), custom_call_target="tpu_custom_call" | custom-call | flops 23040000000 | bytes 3538944 | tf_op jit(solution)/shard_map/to_heads_576/pallas_call | solution.py:122
  131.3 36.4 %attend.1 = (bf16[16,192,128]{2,1,0:T(8,128)(2,1)}, bf16[6144,128]{1,0:T(8,128)(2,1)}, bf16[6144,128]{1,0:T(8,128)(2,1)}, bf16[6144,128]{1,0:T(8,128)(2,1)}, f32[6144,128]{1,0:T(8,128)}) custom-call(s32[4]{0:T(128)} %pad_add_fusion.meta_ref, s32[32]{0:T(128)} %order_ref.3, bf16[16,576,128]{2,1,0:T(8,128)(2,1)} %to_heads_576.1.recv_ref), custom_call_target="tpu_custom_call" | custom-call | flops 38654705664 | bytes 9437184 | tf_op jit(solution)/shard_map/attend/pallas_call | solution.py:335
  167.8 23.8 %to_rows_192.1 = bf16[12,192,128]{2,1,0:T(8,128)(2,1)} custom-call(bf16[16,192,128]{2,1,0:T(8,128)(2,1)} %get-tuple-element.26.send_ref), custom_call_target="tpu_custom_call" | custom-call | flops 7680000000 | bytes 1572864 | tf_op jit(solution)/shard_map/to_rows_192/pallas_call | solution.py:196
  198.1 37.2 %all-gather.12.cloned.1.call-done = bf16[768,3072]{1,0:T(8,128)(2,1)} async-done(((bf16[384,3072]{1,0:T(8,128)(2,1)}), bf16[768,3072]{1,0:T(8,128)(2,1)}) %all-gather.12.cloned.1.call-update) | async-done | bytes 4718608 | tf_op jit(solution)/shard_map/all_gather | solution.py:543
  235.3 13.6 %multiply_convert_fusion = (bf16[384,3072]{1,0:T(8,128)(2,1)S(1)}, f32[384,3072]{1,0:T(8,128)S(1)}, f32[384,3072]{1,0:T(8,128)S(1)}) fusion(f32[3072]{0:T(1024)S(1)} %bitcast.81, bf16[768,3072]{1,0:T(8,128)(2,1)} %all-gather.12.cloned.1.call-done, f32[384,768]{1,0:T(8,128)S(1)} %get-tuple-element.158, f32[768]{0:T(1024)S(1)} %copy-done.20, ...), kind=kOutput, calls=%fused_computation.11 | convolution fusion | flops 1891270656 | bytes 17716224 | tf_op jit(solution)/shard_map/dot_general | solution.py:588
  254.7 4.5 convolution_convert_fusion.2
  264.7 4.6 convolution_convert_fusion.1
  269.3 6.0 multiply_reduce_fusion
  281.2 5.3 fusion.1
  288.8 19.1 %to_heads_192.1.recv_ref = bf16[16,192,128]{2,1,0:T(8,128)(2,1)} custom-call(bf16[12,192,128]{2,1,0:T(8,128)(2,1)} %copy.130.send_ref), custom_call_target="tpu_custom_call" | custom-call | flops 7680000000 | bytes 1179648 | tf_op jit(solution)/shard_map/to_heads_192/pallas_call | solution.py:122
  307.9 59.5 %attend_back.1.send_ref = bf16[16,576,128]{2,1,0:T(8,128)(2,1)} custom-call(s32[4]{0:T(128)} %pad_add_fusion.meta_ref, s32[32]{0:T(128)} %order_ref.3, bf16[16,192,128]{2,1,0:T(8,128)(2,1)} %to_heads_192.1.recv_ref, bf16[6144,128]{1,0:T(8,128)(2,1)} %get-tuple-element.28.qa_ref, bf16[6144,128]{1,0:T(8,128)(2,1)} %get-tuple-element.29.ka_ref, ...), custom_call_target="tpu_custom_call" | custom-call | flops 77309411328 | bytes 12582912 | tf_op jit(solution)/shard_map/attend_back/pallas_call | solution.py:464
  367.3 58.6 %to_rows_576.1 = bf16[12,576,128]{2,1,0:T(8,128)(2,1)} custom-call(bf16[16,576,128]{2,1,0:T(8,128)(2,1)} %attend_back.1.send_ref), custom_call_target="tpu_custom_call" | custom-call | flops 23040000000 | bytes 4718592 | tf_op jit(solution)/shard_map/to_rows_576/pallas_call | solution.py:196
  438.8 8.3 copy.146
  449.0 135.0 %all-reduce.11.cloned.1.call-done = (bf16[768,2432]{0,1:T(8,128)(2,1)}, bf16[768,896]{0,1:T(8,128)(2,1)}) async-done(((bf16[768,2432]{0,1:T(8,128)(2,1)}, bf16[768,896]{0,1:T(8,128)(2,1)}), (bf16[768,2432]{0,1:T(8,128)(2,1)}, bf16[768,896]{0,1:T(8,128)(2,1)})) %all-reduce.11.cloned.1.call-update) | async-done | bytes 5111824
  586.5 109.4 %reduce-scatter.7.cloned.1.call-done = bf16[24,3072]{1,0:T(8,128)(2,1)} async-done(((bf16[768,3072]{1,0:T(8,128)(2,1)}), bf16[24,3072]{1,0:T(8,128)(2,1)}) %reduce-scatter.7.cloned.1.call-update) | async-done | bytes 147472 | tf_op jit(solution)/shard_map/reduce_scatter | solution.py:501
  696.0 115.2 %reduce-scatter.9.cloned.1.call-done = bf16[96,896]{1,0:T(8,128)(2,1)} async-done(((bf16[3072,896]{1,0:T(8,128)(2,1)}), bf16[96,896]{1,0:T(8,128)(2,1)}) %reduce-scatter.9.cloned.1.call-update) | async-done | bytes 172048 | tf_op jit(solution)/shard_map/reduce_scatter | solution.py:501
  818.3 22.3 %all_gather.29 = bf16[384,896]{1,0:T(8,128)(2,1)S(1)} all-gather(bf16[24,896]{1,0:T(8,128)(2,1)S(1)} %copy.137), channel_id=1, replica_groups=mesh['ctx'=16,'wa'=2] {'ctx'}, dimensions={0}, use_global_device_ids=true | all-gather | bytes 731136 | tf_op jit(solution)/shard_map/all_gather | solution.py:504
  843.1 13.1 %all-gather.16.cloned.1.call-done = bf16[384,2432]{1,0:T(8,128)(2,1)} async-done(((bf16[24,2432]{1,0:T(8,128)(2,1)}), bf16[384,2432]{1,0:T(8,128)(2,1)}) %all-gather.16.cloned.1.call-update) | async-done | bytes 1867792 | tf_op jit(solution)/shard_map/all_gather | solution.py:504
  871.4 28.6 %all-gather.18.cloned.1.call-done = bf16[384,3072]{1,0:T(8,128)(2,1)} async-done(((bf16[24,3072]{1,0:T(8,128)(2,1)}), bf16[384,3072]{1,0:T(8,128)(2,1)}) %all-gather.18.cloned.1.call-update) | async-done | bytes 2359312 | tf_op jit(solution)/shard_map/all_gather | solution.py:504
  900.1 4.4 convert_element_type.199
  904.5 40.4 %all-gather.20.cloned.1.call-done = bf16[1536,896]{1,0:T(8,128)(2,1)} async-done(((bf16[96,896]{1,0:T(8,128)(2,1)}), bf16[1536,896]{1,0:T(8,128)(2,1)}) %all-gather.20.cloned.1.call-update) | async-done | bytes 2752528 | tf_op jit(solution)/shard_map/all_gather | solution.py:504
  (202 shorter events, 101.5 us)
Async XLA Ops:
  7.2 8.1 copy-start.7
  7.2 64.9 %all-gather.8.cloned.1.call-start = ((), (), s32[]{:S(2)}) async-start(), calls=%async_computation.2 | async-start | bytes 5603328 | tf_op jit(solution)/shard_map/all_gather | solution.py:543
  19.4 174.8 %all-gather.10.cloned.1.call-start = ((), (), s32[]{:S(2)}) async-start(), calls=%async_computation.3 | async-start | bytes 1769472 | tf_op jit(solution)/shard_map/all_gather | solution.py:543
  20.4 176.2 %all-gather.14.cloned.1.call-start = ((), (), s32[]{:S(2)}) async-start(), calls=%async_computation.5 | async-start | bytes 8257536 | tf_op jit(solution)/shard_map/all_gather | solution.py:543
  25.1 210.2 %all-gather.12.cloned.1.call-start = ((), (), s32[]{:S(2)}) async-start(), calls=%async_computation.4 | async-start | bytes 7077888 | tf_op jit(solution)/shard_map/all_gather | solution.py:543
  29.4 554.6 %all-reduce.11.cloned.1.call-start = ((), (), s32[]{:S(2)}) async-start(), calls=%async_computation.11 | async-start | bytes 10223616
  191.6 2.7 copy-start.10
  194.3 41.1 %copy-start.20 = (f32[768]{0:T(1024)S(1)}, f32[768]{0:T(1024)}, u32[]{:S(2)}) copy-start(f32[768]{0:T(1024)} %get-tuple-element.137) | copy-start | bytes 9220
  235.3 13.6 %copy-start.13 = (bf16[3072,896]{1,0:T(8,128)(2,1)S(1)}, bf16[3072,896]{1,0:T(8,128)(2,1)}, u32[]{:S(2)}) copy-start(bf16[3072,896]{1,0:T(8,128)(2,1)} %all-gather.14.cloned.1.call-done) | copy-start | bytes 16515076
  235.3 13.6 %copy-start.22 = (f32[768]{0:T(1024)S(1)}, f32[768]{0:T(1024)}, u32[]{:S(2)}) copy-start(f32[768]{0:T(1024)} %get-tuple-element.136) | copy-start | bytes 9220
  259.2 5.4 copy-start.21
  278.1 3.1 copy-start.16
  278.1 3.1 copy-start.15
  278.1 3.1 copy-start.14
  429.4 3.3 copy-start.11
  430.9 5.1 copy-start.5
  438.2 257.8 %reduce-scatter.7.cloned.1.call-start = ((), (), s32[]{:S(2)}) async-start(), calls=%async_computation.7 | async-start | bytes 4866048 | tf_op jit(solution)/shard_map/reduce_scatter | solution.py:501
  438.7 372.5 %reduce-scatter.9.cloned.1.call-start = ((), (), s32[]{:S(2)}) async-start(), calls=%async_computation.10 | async-start | bytes 5677056 | tf_op jit(solution)/shard_map/reduce_scatter | solution.py:501
  447.2 364.1 %copy-start.3 = (bf16[384,12,128]{0,2,1:T(8,128)(2,1)S(1)}, bf16[384,12,128]{0,2,1:T(8,128)(2,1)}, u32[]{:S(2)}) copy-start(bf16[384,12,128]{0,2,1:T(8,128)(2,1)} %copy.133) | copy-start | bytes 3538948
  447.2 409.0 %all-gather.16.cloned.1.call-start = ((), (), s32[]{:S(2)}) async-start(), calls=%async_computation.6 | async-start | bytes 1984512 | tf_op jit(solution)/shard_map/all_gather | solution.py:504
  586.4 313.6 %all-gather.18.cloned.1.call-start = ((), (), s32[]{:S(2)}) async-start(), calls=%async_computation.8 | async-start | bytes 2506752 | tf_op jit(solution)/shard_map/all_gather | solution.py:504
  695.9 249.0 %all-gather.20.cloned.1.call-start = ((), (), s32[]{:S(2)}) async-start(), calls=%async_computation.9 | async-start | bytes 2924544 | tf_op jit(solution)/shard_map/all_gather | solution.py:504
  811.3 2.9 copy-start.6
  944.9 3.2 copy-start
  (16 other events, 31.9 us)
Sparse Core Ops, SparseCore 0:
  19.6 52.5 all-gather.7
  74.3 22.7 all-gather.9
  99.2 71.4 all-gather.13
  172.7 62.6 all-gather.11
  438.3 145.6 all-reduce.10
  589.9 105.9 reduce-scatter.6
  701.5 109.7 reduce-scatter.8
  814.0 42.1 all-gather.15
  858.4 41.5 all-gather.17
  902.2 42.6 all-gather.19

commit v2 on v1

--- a/solution.py
+++ b/solution.py
@@ -480,6 +480,212 @@
         ),
         name="attend_back",
     )(meta, order, recv, qa, ka, va, sums)
+
+
+PART_ORDERS = (("x", "z", "wa"), ("wa", "x", "z"), ("z", "wa", "x"))
+GATHER_ORDERS = (("x", "z"), ("z", "x"), ("z", "x"))
+SIZES = {"wa": 2, "x": 2, "z": 4}
+
+
+class Links:
+    def __init__(self):
+        me = lax.axis_index("ctx")
+        self.at = {
+            "core": lax.rem(me, 2),
+            "x": lax.rem(me // 2, 2),
+            "z": me // 4,
+            "wa": lax.axis_index("wa"),
+        }
+
+    def peer(self, axis, value):
+        at = dict(self.at)
+        at[axis] = value
+        return {"ctx": at["z"] * 4 + at["x"] * 2 + at["core"], "wa": at["wa"]}
+
+
+def part_columns(width):
+    units = width // 512
+    third = units // 4
+    second = (units - third) // 2
+    first = units - third - second
+    bounds = [0, first * 512, (first + second) * 512, width]
+    return [(bounds[k], bounds[k + 1]) for k in range(3)]
+
+
+def grad_sum_kernel(g_ref, out_ref, core_buf, *rest):
+    bufs, sems = rest[:9], rest[9:]
+    send_sem, recv_sem = sems
+    links = Links()
+    rows, width = g_ref.shape[3], g_ref.shape[4]
+    core, x, z, wa = (links.at[name] for name in ("core", "x", "z", "wa"))
+    barrier = pltpu.get_barrier_semaphore()
+    peers = [links.peer("core", 1 - core), links.peer("x", 1 - x), links.peer("wa", 1 - wa)]
+    peers += [links.peer("z", lax.rem(z + step, 4)) for step in range(1, 4)]
+    for peer in peers:
+        pl.semaphore_signal(barrier, inc=1, device_id=peer, device_id_type=pl.DeviceIdType.MESH)
+    pl.semaphore_wait(barrier, len(peers))
+    used = [0]
+
+    def remote(src, dst, peer):
+        index = used[0]
+        used[0] += 1
+        copy = pltpu.make_async_remote_copy(
+            src_ref=src,
+            dst_ref=dst,
+            send_sem=send_sem.at[index],
+            recv_sem=recv_sem.at[index],
+            device_id=peer,
+            device_id_type=pl.DeviceIdType.MESH,
+        )
+        copy.start()
+        return copy
+
+    columns = part_columns(width)
+
+    def z_columns(part, value):
+        low, high = columns[part]
+        quarter = (high - low) // 4
+        return pl.ds(pl.multiple_of(low + value * quarter, LANES), quarter)
+
+    def slab(part, held, axis=None, value=None):
+        at = dict(links.at)
+        if axis is not None:
+            at[axis] = value
+            held = held | {axis}
+        low, high = columns[part]
+        return g_ref.at[
+            pl.ds(at["wa"], 1) if "wa" in held else pl.ds(0, 2),
+            core,
+            pl.ds(at["x"], 1) if "x" in held else pl.ds(0, 2),
+            :,
+            z_columns(part, at["z"]) if "z" in held else pl.ds(low, high - low),
+        ]
+
+    def add_into(target, sources):
+        outer, inner, _, _ = target.shape
+        for a in range(outer):
+            for b in range(inner):
+
+                def add(group, _):
+                    some = pl.ds(pl.multiple_of(group * 16, 16), 16)
+                    total = target[a, b, some, :].astype(jnp.float32)
+                    for source in sources:
+                        total = total + source[a, b, some, :].astype(jnp.float32)
+                    target[a, b, some, :] = total.astype(low_type)
+                    return 0
+
+                lax.fori_loop(0, rows // 16, add, 0)
+
+    core_copies = []
+    for part in range(3):
+        low, high = columns[part]
+        cols = pl.ds(low, high - low)
+        core_copies.append(
+            remote(
+                g_ref.at[:, 1 - core, :, :, cols],
+                core_buf.at[:, :, :, cols],
+                links.peer("core", 1 - core),
+            )
+        )
+
+    def begin(part, stage):
+        axis = PART_ORDERS[part][stage]
+        held = set(PART_ORDERS[part][:stage])
+        buf = bufs[part * 3 + stage]
+        copies = []
+        for step in range(1, SIZES[axis]):
+            value = lax.rem(links.at[axis] + step, SIZES[axis])
+            copies.append(
+                remote(slab(part, held, axis, value), buf.at[step - 1], links.peer(axis, value))
+            )
+        return copies
+
+    flying = {}
+    for part in range(3):
+        low, high = columns[part]
+        core_copies[part].wait()
+        add_into(slab(part, set()), [core_buf.at[:, :, :, pl.ds(low, high - low)]])
+        flying[part] = begin(part, 0)
+    for stage in range(3):
+        for part in range(3):
+            axis = PART_ORDERS[part][stage]
+            for copy in flying[part]:
+                copy.wait()
+            buf = bufs[part * 3 + stage]
+            add_into(
+                slab(part, set(PART_ORDERS[part][: stage + 1])),
+                [buf.at[step] for step in range(SIZES[axis] - 1)],
+            )
+            if stage < 2:
+                flying[part] = begin(part, stage + 1)
+
+    def out_slab(part, held):
+        low, high = columns[part]
+        return out_ref.at[
+            core,
+            pl.ds(x, 1) if "x" in held else pl.ds(0, 2),
+            :,
+            z_columns(part, z) if "z" in held else pl.ds(low, high - low),
+        ]
+
+    def spread(part, stage):
+        axis = GATHER_ORDERS[part][stage]
+        block = out_slab(part, set(GATHER_ORDERS[part][stage:]))
+        return [
+            remote(block, block, links.peer(axis, lax.rem(links.at[axis] + step, SIZES[axis])))
+            for step in range(1, SIZES[axis])
+        ]
+
+    for part in range(3):
+        out_slab(part, {"x", "z"})[...] = slab(part, {"wa", "x", "z"})[0]
+        flying[part] = spread(part, 0)
+    for stage in range(2):
+        for part in range(3):
+            for copy in flying[part]:
+                copy.wait()
+            if stage == 0:
+                flying[part] = spread(part, 1)
+            else:
+                block = out_slab(part, set())
+                flying[part] = [remote(block, block, links.peer("core", 1 - core))]
+    for part in range(3):
+        for copy in flying[part]:
+            copy.wait()
+
+
+def grad_sum(grad, collective_id):
+    rows, width = grad.shape
+    piece = rows // 8
+    columns = part_columns(width)
+    bufs = []
+    for part in range(3):
+        shape = {"wa": 2, "x": 2, "z": columns[part][1] - columns[part][0]}
+        for axis in PART_ORDERS[part]:
+            shape[axis] //= SIZES[axis]
+            bufs.append(
+                pltpu.VMEM((SIZES[axis] - 1, shape["wa"], shape["x"], piece, shape["z"]), low_type)
+            )
+    vmem = pl.BlockSpec(memory_space=pltpu.VMEM)
+    total = pl.pallas_call(
+        grad_sum_kernel,
+        out_shape=jax.ShapeDtypeStruct((2, 2, piece, width), low_type),
+        in_specs=[vmem],
+        out_specs=vmem,
+        scratch_shapes=[
+            pltpu.VMEM((2, 2, piece, width), low_type),
+            *bufs,
+            pltpu.SemaphoreType.DMA((40,)),
+            pltpu.SemaphoreType.DMA((40,)),
+        ],
+        compiler_params=pltpu.CompilerParams(
+            collective_id=collective_id, has_side_effects=True, vmem_limit_bytes=VMEM_BYTES
+        ),
+        cost_estimate=pl.CostEstimate(
+            flops=width * 15_000_000, bytes_accessed=grad.size * 4, transcendentals=0
+        ),
+        name=f"grad_sum_{width}",
+    )(grad.reshape(2, 2, 2, piece, width))
+    return total.reshape(rows // 2, width)
 
 
 def pack_columns(vectors, rows):
@@ -531,6 +737,7 @@
     wide = w_up.shape[1]
     half = tok_rows // 2
     shard = w_query.shape[0]
+    direct = count == 16 and width == 2 * shard and shard % 64 == 0 and wide == 4 * width
     me = lax.axis_index("ctx")
     seq_ends = jnp.cumsum(lengths[0])
     own_blocks = lax.dynamic_slice(block_order, (2 * me,), (2,))
@@ -634,10 +841,6 @@
     context_back, down_block, out_block, up_block = lax.optimization_barrier(
         (context_back, down_block, out_block, up_block)
     )
-    up_sum = reduce_shards(up_block)
-    down_sum = reduce_shards(down_block)
-    out_sum = reduce_shards(out_block)
-
     back_at_head = to_heads(context_back, count, 2)
     grads_out = attend_back(meta, block_order, back_at_head, qa, ka, va, sums)
     grads_in = to_rows(grads_out, count, 3)
@@ -660,7 +863,30 @@
         ],
         axis=1,
     )
-    last_sum = reduce_shards(last_block)
+    if direct:
+        fold = (2, 4, shard, width + LANES)
+        wide_block = jnp.concatenate(
+            [
+                up_block,
+                down_block.reshape(fold).transpose(0, 2, 1, 3).reshape(2 * shard, -1),
+                out_block,
+                last_block,
+            ],
+            axis=1,
+        )
+        unused = -wide_block.shape[1] % 512
+        wide_sum = grad_sum(jnp.pad(wide_block, ((0, 0), (0, unused))), 4)
+        edges = [0]
+        for piece in (wide, 4 * (width + LANES), width + LANES, 3 * width + LANES):
+            edges.append(edges[-1] + piece)
+        up_sum, down_sum, out_sum, last_sum = (
+            wide_sum[:, edges[k] : edges[k + 1]] for k in range(4)
+        )
+        down_sum = down_sum.reshape(shard, 4, -1).transpose(1, 0, 2).reshape(4 * shard, -1)
+    else:
+        up_sum, down_sum, out_sum, last_sum = (
+            reduce_shards(block) for block in (up_block, down_block, out_block, last_block)
+        )
     d_input = (
         d_hone
         + jnp.einsum("td,cd->tc", d_queries, query_weight, preferred_element_type=jnp.float32)

time: 970 us -> 738 us (0.76); the launches traced: 958 us -> 737 us
  waiting for transfers between devices: 519 us -> 72.9 us
  Pallas kernels: 248 us -> 453 us
  local copies, waits for them, and re-layouts: 57.2 us -> 107 us
  blocking collectives: 22.3 us -> 0 us
    reduce_scatter x2 -> x0, waiting for transfers between devices: 225 us -> none  [reduce_shards(): lax.psum_scatter(grad.astype(low_type), ('wa', 'ctx'), scatter_dimension=...]
    pallas_call x0 -> x1, Pallas kernels: none -> 191 us  [grad_sum(): pl.pallas_call(grad_sum_kernel, out_shape=jax.ShapeDtypeStruct((2, 2, pie...]
    unnamed x11 -> x4, waiting for transfers between devices: 136 us -> 0.07 us
    all_gather x3 -> x0, waiting for transfers between devices: 82.1 us -> none  [reduce_shards(): return lax.all_gather(part, 'ctx', axis=0, tiled=True)]
    all_gather x1 -> x0, blocking collectives: 22.3 us -> none  [reduce_shards(): return lax.all_gather(part, 'ctx', axis=0, tiled=True)]
    transpose x0 -> x1, local copies, waits for them, and re-layouts: none -> 12 us  [body(): down_block.reshape(fold).transpose(0, 2, 1, 3).reshape(2 * shard, -1)]
    pad x0 -> x1, local copies, waits for them, and re-layouts: none -> 11.3 us  [body(): wide_sum = grad_sum(jnp.pad(wide_block, ((0, 0), (0, unused))), 4)]
    reshape x0 -> x1, local copies, waits for them, and re-layouts: none -> 10.9 us  [body(): down_block.reshape(fold).transpose(0, 2, 1, 3).reshape(2 * shard, -1)]
  transfers between devices with their start and end apart: 10 -> 4, of which waited for: 8 -> 2; matrix products, arithmetic and copies ran while one was open for 7% -> 4% of each run, Pallas kernels for 12% -> 16%
where the time goes in v2:
time: 738 us; the launch traced here: 737 us
  Pallas kernels  453 us (61%)
  local copies, waits for them, and re-layouts  107 us (14%)
  waiting for transfers between devices  72.9 us (10%)
  matrix products  50.5 us (7%)
  other arithmetic  38.2 us (5%)
  between operations  15.2 us (2%)
    pallas_call x1, Pallas kernels, grad_sum(): pl.pallas_call(grad_sum_kernel, out_shape=jax.ShapeDtypeStruct((2, 2, pie...  191 us
    pallas_call x2, Pallas kernels, to_rows(): pl.pallas_call(partial(to_rows_kernel, count), out_shape=jax.ShapeDtypeSt...  82.6 us
    all_gather x4, waiting for transfers between devices, gather_rows(): return lax.all_gather(shard_block, 'wa', axis=0, tiled=True)  72.9 us
    pallas_call x1, Pallas kernels, attend_back(): pl.pallas_call(attend_back_kernel, out_shape=jax.ShapeDtypeStruct((count,...  68.6 us
    pallas_call x2, Pallas kernels, to_heads(): pl.pallas_call(partial(to_heads_kernel, count), out_shape=jax.ShapeDtypeS...  64.3 us
    pallas_call x1, Pallas kernels, attend(): pl.pallas_call(attend_kernel, out_shape=(jax.ShapeDtypeStruct((count, row...  41.8 us
    unnamed x64, local copies, waits for them, and re-layouts  33 us
    dot_general x1, matrix products, body(): jnp.dot(norm_low, up_weight, preferred_element_type=jnp.float32) + up_bias  14.9 us
  transfers between devices with their start and end apart: 4, of which 2 were waited for; matrix products, arithmetic and copies ran while one was open for 4% of the time, Pallas kernels for 16%

profile of v2, /device:TPU:9, one launch (start us, length us, event | category | flops | bytes accessed | tf_op | source)
XLA Modules:
  0.0 736.7 jit_solution(1331673678086244412)
XLA Ops:
  25.2 4.2 convert_element_type.184
  31.8 40.3 %all-gather.5.cloned.1.call-done = bf16[768,2432]{1,0:T(8,128)(2,1)} async-done(((bf16[384,2432]{1,0:T(8,128)(2,1)}), bf16[768,2432]{1,0:T(8,128)(2,1)}) %all-gather.5.cloned.1.call-update) | async-done | bytes 3735568 | tf_op jit(solution)/shard_map/all_gather | solution.py:750
  80.2 5.3 project.1.send_ref
  85.6 45.2 %to_heads_576.1.recv_ref = bf16[16,576,128]{2,1,0:T(8,128)(2,1)} custom-call(bf16[12,576,128]{2,1,0:T(8,128)(2,1)} %project.1.send_ref), custom_call_target="tpu_custom_call" | custom-call | flops 23040000000 | bytes 3538944 | tf_op jit(solution)/shard_map/to_heads_576/pallas_call | solution.py:122
  130.8 41.8 %attend.1 = (bf16[16,192,128]{2,1,0:T(8,128)(2,1)}, bf16[6144,128]{1,0:T(8,128)(2,1)}, bf16[6144,128]{1,0:T(8,128)(2,1)}, bf16[6144,128]{1,0:T(8,128)(2,1)}, f32[6144,128]{1,0:T(8,128)}) custom-call(s32[4]{0:T(128)} %pad_add_fusion.meta_ref, s32[32]{0:T(128)} %order_ref.3, bf16[16,576,128]{2,1,0:T(8,128)(2,1)} %to_heads_576.1.recv_ref), custom_call_target="tpu_custom_call" | custom-call | flops 38654705664 | bytes 9437184 | tf_op jit(solution)/shard_map/attend/pallas_call | solution.py:335
  172.6 23.8 %to_rows_192.1 = bf16[12,192,128]{2,1,0:T(8,128)(2,1)} custom-call(bf16[16,192,128]{2,1,0:T(8,128)(2,1)} %get-tuple-element.26.send_ref), custom_call_target="tpu_custom_call" | custom-call | flops 7680000000 | bytes 1572864 | tf_op jit(solution)/shard_map/to_rows_192/pallas_call | solution.py:196
  202.9 32.5 %all-gather.9.cloned.1.call-done = bf16[768,3072]{1,0:T(8,128)(2,1)} async-done(((bf16[384,3072]{1,0:T(8,128)(2,1)}), bf16[768,3072]{1,0:T(8,128)(2,1)}) %all-gather.9.cloned.1.call-update) | async-done | bytes 4718608 | tf_op jit(solution)/shard_map/all_gather | solution.py:750
  235.4 14.9 %multiply_convert_fusion = (bf16[384,3072]{1,0:T(8,128)(2,1)S(1)}, f32[384,3072]{1,0:T(8,128)S(1)}, f32[384,3072]{1,0:T(8,128)}) fusion(f32[3072]{0:T(1024)S(1)} %bitcast.103, bf16[768,3072]{1,0:T(8,128)(2,1)} %all-gather.9.cloned.1.call-done, f32[384,768]{1,0:T(8,128)S(1)} %get-tuple-element.122, f32[768]{0:T(1024)S(1)} %get-tuple-element.103, ...), kind=kOutput, calls=%fused_computation.12 | convolution fusion | flops 1891270656 | bytes 17716224 | tf_op jit(solution)/shard_map/dot_general | solution.py:795
  255.0 4.5 convolution_convert_fusion.2
  259.5 5.2 fusion.67
  264.7 4.6 convolution_convert_fusion.1
  275.9 5.2 fusion.1
  282.3 19.1 %to_heads_192.1.recv_ref = bf16[16,192,128]{2,1,0:T(8,128)(2,1)} custom-call(bf16[12,192,128]{2,1,0:T(8,128)(2,1)} %copy.112.send_ref), custom_call_target="tpu_custom_call" | custom-call | flops 7680000000 | bytes 1179648 | tf_op jit(solution)/shard_map/to_heads_192/pallas_call | solution.py:122
  301.4 68.6 %attend_back.1.send_ref = bf16[16,576,128]{2,1,0:T(8,128)(2,1)} custom-call(s32[4]{0:T(128)} %pad_add_fusion.meta_ref, s32[32]{0:T(128)} %order_ref.3, bf16[16,192,128]{2,1,0:T(8,128)(2,1)} %to_heads_192.1.recv_ref, bf16[6144,128]{1,0:T(8,128)(2,1)} %get-tuple-element.28.qa_ref, bf16[6144,128]{1,0:T(8,128)(2,1)} %get-tuple-element.29.ka_ref, ...), custom_call_target="tpu_custom_call" | custom-call | flops 77309411328 | bytes 12582912 | tf_op jit(solution)/shard_map/attend_back/pallas_call | solution.py:464
  370.1 58.8 %to_rows_576.1 = bf16[12,576,128]{2,1,0:T(8,128)(2,1)} custom-call(bf16[16,576,128]{2,1,0:T(8,128)(2,1)} %attend_back.1.send_ref), custom_call_target="tpu_custom_call" | custom-call | flops 23040000000 | bytes 4718592 | tf_op jit(solution)/shard_map/to_rows_576/pallas_call | solution.py:196
  434.5 5.1 constant_dynamic-update-slice_fusion.3
  439.6 10.9 %reshape.220 = bf16[2,4,384,896]{2,1,0,3:T(4,128)(2,1)} reshape(bf16[3072,896]{0,1:T(8,128)(2,1)} %fusion.1) | data formatting | bytes 11010048 | tf_op jit(solution)/shard_map/reshape | solution.py:871
  450.5 12.0 %copy.116 = bf16[2,384,4,896]{3,2,1,0:T(4,128)(2,1)} copy(bf16[2,384,4,896]{1,2,0,3:T(4,128)(2,1)} %bitcast.79) | data formatting | bytes 11010048 | tf_op jit(solution)/shard_map/transpose | solution.py:871
  462.5 5.9 copy.131
  469.9 4.9 fusion.9
  474.8 4.3 copy.119
  483.4 5.4 constant_dynamic-update-slice_fusion.2
  493.0 11.3 %pad.30 = bf16[768,10240]{1,0:T(8,128)(2,1)} pad(bf16[768,9984]{1,0:T(8,128)(2,1)} %pad_dynamic-update-slice_fusion, bf16[]{:T(256)} %constant.24.clone.1), padding=0_0x0_256 | pad | bytes 31064066 | tf_op jit(solution)/shard_map/jit(_pad)/pad | solution.py:878
  504.3 190.6 %grad_sum_10240.1 = bf16[2,2,96,10240]{3,2,1,0:T(8,128)(2,1)} custom-call(bf16[2,2,2,96,10240]{4,3,2,1,0:T(8,128)(2,1)} %bitcast.82), custom_call_target="tpu_custom_call" | custom-call | flops 153600000000 | bytes 31457280 | tf_op jit(solution)/shard_map/grad_sum_10240/pallas_call | solution.py:669
  (185 shorter events, 97.1 us)
Async XLA Ops:
  7.2 8.1 %copy-start.10 = (f32[384,768]{1,0:T(8,128)S(1)}, f32[384,768]{1,0:T(8,128)}, u32[]{:S(2)}) copy-start(f32[384,768]{1,0:T(8,128)} %param.25) | copy-start | bytes 3538948
  7.2 65.0 %all-gather.5.cloned.1.call-start = ((), (), s32[]{:S(2)}) async-start(), calls=%async_computation | async-start | bytes 5603328 | tf_op jit(solution)/shard_map/all_gather | solution.py:750
  17.1 2.5 copy-start.12
  19.5 179.6 %all-gather.7.cloned.1.call-start = ((), (), s32[]{:S(2)}) async-start(), calls=%async_computation.1 | async-start | bytes 1769472 | tf_op jit(solution)/shard_map/all_gather | solution.py:750
  20.4 181.0 %all-gather.11.cloned.1.call-start = ((), (), s32[]{:S(2)}) async-start(), calls=%async_computation.3 | async-start | bytes 8257536 | tf_op jit(solution)/shard_map/all_gather | solution.py:750
  25.1 210.2 %all-gather.9.cloned.1.call-start = ((), (), s32[]{:S(2)}) async-start(), calls=%async_computation.2 | async-start | bytes 7077888 | tf_op jit(solution)/shard_map/all_gather | solution.py:750
  196.4 2.7 copy-start.14
  235.3 14.9 %copy-start.15 = (bf16[3072,896]{1,0:T(8,128)(2,1)S(1)}, bf16[3072,896]{1,0:T(8,128)(2,1)}, u32[]{:S(2)}) copy-start(bf16[3072,896]{1,0:T(8,128)(2,1)} %all-gather.11.cloned.1.call-done) | copy-start | bytes 16515076
  250.3 2.4 copy-start.7
  255.0 14.4 %slice-start.2 = ((s8[4718592]{0:T(1024)(128)(4,1)}), s8[4194304]{0:T(1024)(128)(4,1)S(1)}, s32[]{:S(2)}) async-start(s8[4718592]{0:T(1024)(128)(4,1)} %bitcast.106), calls=%async_computation.6 | async-start | bytes 8388608
  259.5 9.8 %slice-start.3 = ((s8[4718592]{0:T(1024)(128)(4,1)}), s8[524288]{0:T(1024)(128)(4,1)S(1)}, s32[]{:S(2)}) async-start(s8[4718592]{0:T(1024)(128)(4,1)} %bitcast.106), calls=%async_computation.7 | async-start | bytes 1048576
  272.2 2.1 copy-start.19
  428.9 1.8 copy-start.4
  434.5 35.4 %copy-start.8 = (bf16[384,768]{0,1:T(8,128)(2,1)}, bf16[384,768]{0,1:T(8,128)(2,1)S(1)}, u32[]{:S(2)}) copy-start(bf16[384,768]{0,1:T(8,128)(2,1)S(1)} %mul.217) | copy-start | bytes 1769476
  468.3 1.6 copy-start.5
  483.4 5.4 copy-start.3
  490.2 2.1 copy-start.13
  700.9 8.0 %slice-start = ((s8[7864320]{0:T(1024)(128)(4,1)}), s8[4194304]{0:T(1024)(128)(4,1)S(1)}, s32[]{:S(2)}) async-start(s8[7864320]{0:T(1024)(128)(4,1)} %bitcast.86), calls=%async_computation.4 | async-start | bytes 8388608
  703.0 5.8 slice-start.1
  716.0 2.8 copy-start.2
  720.0 4.1 copy-start.6
  724.2 2.9 copy-start.1
  724.2 2.9 copy-start.9
  724.2 3.0 copy-start.17
  (6 other events, 7.4 us)
Sparse Core Ops, SparseCore 0:
  19.6 52.5 all-gather.4
  74.3 22.7 all-gather.6
  99.2 71.4 all-gather.10
  172.7 62.6 all-gather.8

commit v3 on v2

--- a/solution.py
+++ b/solution.py
@@ -133,7 +133,7 @@
             collective_id=collective_id, has_side_effects=True, vmem_limit_bytes=VMEM_BYTES
         ),
         cost_estimate=pl.CostEstimate(
-            flops=rows * 40_000_000, bytes_accessed=send.size * 4, transcendentals=0
+            flops=rows * 250_000_000, bytes_accessed=send.size * 4, transcendentals=0
         ),
         name=f"to_heads_{rows}",
     )(send)
@@ -207,7 +207,7 @@
             collective_id=collective_id, has_side_effects=True, vmem_limit_bytes=VMEM_BYTES
         ),
         cost_estimate=pl.CostEstimate(
-            flops=rows * 40_000_000, bytes_accessed=send.size * 4, transcendentals=0
+            flops=rows * 250_000_000, bytes_accessed=send.size * 4, transcendentals=0
         ),
         name=f"to_rows_{rows}",
     )(send)
@@ -503,20 +503,14 @@
         return {"ctx": at["z"] * 4 + at["x"] * 2 + at["core"], "wa": at["wa"]}
 
 
-def part_columns(width):
-    units = width // 512
-    third = units // 4
-    second = (units - third) // 2
-    first = units - third - second
-    bounds = [0, first * 512, (first + second) * 512, width]
-    return [(bounds[k], bounds[k + 1]) for k in range(3)]
-
-
-def grad_sum_kernel(g_ref, out_ref, core_buf, *rest):
-    bufs, sems = rest[:9], rest[9:]
-    send_sem, recv_sem = sems
+def splits_rows(piece):
+    return piece % 64 == 0
+
+
+def grad_sum_kernel(*refs):
+    g_refs, out_refs, core_bufs, bufs = refs[:3], refs[3:6], refs[6:9], refs[9:18]
+    send_sem, recv_sem = refs[18:]
     links = Links()
-    rows, width = g_ref.shape[3], g_ref.shape[4]
     core, x, z, wa = (links.at[name] for name in ("core", "x", "z", "wa"))
     barrier = pltpu.get_barrier_semaphore()
     peers = [links.peer("core", 1 - core), links.peer("x", 1 - x), links.peer("wa", 1 - wa)]
@@ -540,29 +534,28 @@
         copy.start()
         return copy
 
-    columns = part_columns(width)
-
-    def z_columns(part, value):
-        low, high = columns[part]
-        quarter = (high - low) // 4
-        return pl.ds(pl.multiple_of(low + value * quarter, LANES), quarter)
+    def z_share(ref, value):
+        piece, width = ref.shape[-2:]
+        if value is None:
+            return slice(None), slice(None)
+        if splits_rows(piece):
+            return pl.ds(pl.multiple_of(value * (piece // 4), 16), piece // 4), slice(None)
+        return slice(None), pl.ds(pl.multiple_of(value * (width // 4), LANES), width // 4)
 
     def slab(part, held, axis=None, value=None):
         at = dict(links.at)
         if axis is not None:
             at[axis] = value
             held = held | {axis}
-        low, high = columns[part]
-        return g_ref.at[
+        return g_refs[part].at[
             pl.ds(at["wa"], 1) if "wa" in held else pl.ds(0, 2),
             core,
             pl.ds(at["x"], 1) if "x" in held else pl.ds(0, 2),
-            :,
-            z_columns(part, at["z"]) if "z" in held else pl.ds(low, high - low),
+            *z_share(g_refs[part], at["z"] if "z" in held else None),
         ]
 
     def add_into(target, sources):
-        outer, inner, _, _ = target.shape
+        outer, inner, rows, _ = target.shape
         for a in range(outer):
             for b in range(inner):
 
@@ -576,17 +569,10 @@
 
                 lax.fori_loop(0, rows // 16, add, 0)
 
-    core_copies = []
-    for part in range(3):
-        low, high = columns[part]
-        cols = pl.ds(low, high - low)
-        core_copies.append(
-            remote(
-                g_ref.at[:, 1 - core, :, :, cols],
-                core_buf.at[:, :, :, cols],
-                links.peer("core", 1 - core),
-            )
-        )
+    core_copies = [
+        remote(g_refs[part].at[:, 1 - core], core_bufs[part], links.peer("core", 1 - core))
+        for part in range(3)
+    ]
 
     def begin(part, stage):
         axis = PART_ORDERS[part][stage]
@@ -602,9 +588,8 @@
 
     flying = {}
     for part in range(3):
-        low, high = columns[part]
         core_copies[part].wait()
-        add_into(slab(part, set()), [core_buf.at[:, :, :, pl.ds(low, high - low)]])
+        add_into(slab(part, set()), [core_bufs[part]])
         flying[part] = begin(part, 0)
     for stage in range(3):
         for part in range(3):
@@ -620,12 +605,10 @@
                 flying[part] = begin(part, stage + 1)
 
     def out_slab(part, held):
-        low, high = columns[part]
-        return out_ref.at[
+        return out_refs[part].at[
             core,
             pl.ds(x, 1) if "x" in held else pl.ds(0, 2),
-            :,
-            z_columns(part, z) if "z" in held else pl.ds(low, high - low),
+            *z_share(out_refs[part], z if "z" in held else None),
         ]
 
     def spread(part, stage):
@@ -653,26 +636,34 @@
             copy.wait()
 
 
-def grad_sum(grad, collective_id):
-    rows, width = grad.shape
-    piece = rows // 8
-    columns = part_columns(width)
-    bufs = []
-    for part in range(3):
-        shape = {"wa": 2, "x": 2, "z": columns[part][1] - columns[part][0]}
+def grad_sum(grads, collective_id):
+    bufs, core_bufs, outs, given = [], [], [], []
+    for part, grad in enumerate(grads):
+        rows, width = grad.shape
+        piece = rows // 8
+        shape = {"wa": 2, "x": 2, "z": 4}
         for axis in PART_ORDERS[part]:
             shape[axis] //= SIZES[axis]
+            share = (
+                (piece * shape["z"] // 4, width)
+                if splits_rows(piece)
+                else (piece, width * shape["z"] // 4)
+            )
             bufs.append(
-                pltpu.VMEM((SIZES[axis] - 1, shape["wa"], shape["x"], piece, shape["z"]), low_type)
+                pltpu.VMEM((SIZES[axis] - 1, shape["wa"], shape["x"], *share), low_type)
             )
+        core_bufs.append(pltpu.VMEM((2, 2, piece, width), low_type))
+        outs.append(jax.ShapeDtypeStruct((2, 2, piece, width), low_type))
+        given.append(grad.reshape(2, 2, 2, piece, width))
     vmem = pl.BlockSpec(memory_space=pltpu.VMEM)
-    total = pl.pallas_call(
+    size = sum(grad.size for grad in grads)
+    sums = pl.pallas_call(
         grad_sum_kernel,
-        out_shape=jax.ShapeDtypeStruct((2, 2, piece, width), low_type),
-        in_specs=[vmem],
-        out_specs=vmem,
+        out_shape=tuple(outs),
+        in_specs=[vmem] * 3,
+        out_specs=(vmem,) * 3,
         scratch_shapes=[
-            pltpu.VMEM((2, 2, piece, width), low_type),
+            *core_bufs,
             *bufs,
             pltpu.SemaphoreType.DMA((40,)),
             pltpu.SemaphoreType.DMA((40,)),
@@ -681,11 +672,11 @@
             collective_id=collective_id, has_side_effects=True, vmem_limit_bytes=VMEM_BYTES
         ),
         cost_estimate=pl.CostEstimate(
-            flops=width * 15_000_000, bytes_accessed=grad.size * 4, transcendentals=0
+            flops=size * 20_000, bytes_accessed=size * 4, transcendentals=0
         ),
-        name=f"grad_sum_{width}",
-    )(grad.reshape(2, 2, 2, piece, width))
-    return total.reshape(rows // 2, width)
+        name="grad_sum",
+    )(*given)
+    return [part.reshape(-1, part.shape[-1]) for part in sums]
 
 
 def pack_columns(vectors, rows):
@@ -693,9 +684,9 @@
     return jnp.pad(columns, ((0, 0), (0, LANES - len(vectors))))
 
 
-def column_sums(terms):
+def column_sums(terms, lanes):
     block = jnp.stack([jnp.sum(term, axis=0) for term in terms], axis=1).astype(low_type)
-    return jnp.pad(block, ((0, 0), (0, LANES - len(terms))))
+    return jnp.pad(block, ((0, 0), (0, lanes - len(terms))))
 
 
 def rows_of_columns(block, wanted):
@@ -746,8 +737,28 @@
     owns = jnp.any(me == jnp.arange(HEADS, dtype=jnp.int32) * count // HEADS).astype(jnp.int32)
     meta = jnp.concatenate([seq_ends.astype(jnp.int32), owns[None]])
 
-    def gather_rows(shard_block):
-        return lax.all_gather(shard_block, "wa", axis=0, tiled=True)
+    core = me % 2
+    wa = lax.axis_index("wa")
+
+    def fetch_half(shard_block, after=None):
+        if not direct:
+            return None
+        if after is not None:
+            shard_block, _ = lax.optimization_barrier((shard_block, after))
+        size, columns = shard_block.shape
+        part = lax.dynamic_slice(shard_block, (core * (size // 2), 0), (size // 2, columns))
+        return lax.ppermute(part, "wa", [(0, 1), (1, 0)])
+
+    def gather_rows(shard_block, fetched):
+        if not direct:
+            return lax.all_gather(shard_block, "wa", axis=0, tiled=True)
+        size, columns = shard_block.shape
+        swapped = lax.ppermute(fetched, "ctx", [(k, k ^ 1) for k in range(count)])
+        other = (1 - wa) * size
+        whole = jnp.zeros((2 * size, columns), shard_block.dtype)
+        whole = lax.dynamic_update_slice(whole, shard_block, (wa * size, 0))
+        whole = lax.dynamic_update_slice(whole, fetched, (other + core * (size // 2), 0))
+        return lax.dynamic_update_slice(whole, swapped, (other + (1 - core) * (size // 2), 0))
 
     pair = jnp.stack(
         [
@@ -759,9 +770,15 @@
     vectors = pack_columns(
         [b_query, b_value, b_out, gain_one, shift_one, gain_two, shift_two, b_down], shard
     )
-    first_pack = gather_rows(
-        jnp.concatenate([w_query.astype(low_type), pair, vectors], axis=1)
-    )
+    first_shard = jnp.concatenate([w_query.astype(low_type), pair, vectors], axis=1)
+    fetched = fetch_half(first_shard)
+    later_shards = (
+        w_out.astype(low_type),
+        w_up.astype(low_type),
+        jnp.concatenate([w_down.astype(low_type), pack_columns([b_up], 4 * shard)], axis=1),
+    )
+    later_fetched = tuple(fetch_half(block, fetched) for block in later_shards)
+    first_pack = gather_rows(first_shard, fetched)
     query_weight = first_pack[:, :width]
     pair_weight = first_pack[:, width : 3 * width]
     vector_rows = rows_of_columns(first_pack[:, 3 * width :], 8)
@@ -772,17 +789,15 @@
         [jnp.zeros((HEADS, HEAD_DIM), jnp.float32), value_bias.reshape(HEADS, HEAD_DIM)], axis=1
     ).reshape(1, 2 * width)
 
-    out_weight = gather_rows(w_out.astype(low_type))
-    up_weight = gather_rows(w_up.astype(low_type))
-    down_pack = gather_rows(
-        jnp.concatenate([w_down.astype(low_type), pack_columns([b_up], 4 * shard)], axis=1)
-    )
-    down_weight = down_pack[:, :width]
-    up_bias = rows_of_columns(down_pack[:, width:], 1)[0]
-
     packed = project(inputs, query_weight, pair_weight, query_bias[None, :], pair_bias)
     at_head = to_heads(packed, count, 0)
     context_out, qa, ka, va, sums = attend(meta, block_order, at_head)
+    context_out, later_fetched = lax.optimization_barrier((context_out, later_fetched))
+    out_weight, up_weight, down_pack = (
+        gather_rows(block, half_block) for block, half_block in zip(later_shards, later_fetched)
+    )
+    down_weight = down_pack[:, :width]
+    up_bias = rows_of_columns(down_pack[:, width:], 1)[0]
     context_in = to_rows(context_out, count, 1)
     context_low = (
         context_in.reshape(HEADS, half, 2, HEAD_DIM).transpose(2, 1, 0, 3).reshape(tok_rows, width)
@@ -820,27 +835,35 @@
     grad_wdown = jnp.einsum("tf,td->fd", gelu_low, d_down, preferred_element_type=jnp.float32)
     grad_wup = jnp.einsum("td,tf->df", norm_low, d_up, preferred_element_type=jnp.float32)
     grad_wout = jnp.einsum("tc,td->cd", context_low, d_attn, preferred_element_type=jnp.float32)
-    down_block = jnp.concatenate(
-        [grad_wdown.astype(low_type), column_sums([d_up.astype(jnp.float32)])], axis=1
-    )
-    vec_block = jnp.stack(
+    up_bias_sums = jnp.sum(d_up.astype(jnp.float32), axis=0)
+    lanes = 2 * LANES
+    vec_block = jnp.concatenate(
         [
-            jnp.sum(d_attn.astype(jnp.float32), axis=0),
-            grad_gain_first,
-            grad_shift_first,
-            jnp.sum(d_down.astype(jnp.float32), axis=0),
-            grad_gain_second,
-            grad_shift_second,
+            jnp.stack(
+                [
+                    jnp.sum(d_attn.astype(jnp.float32), axis=0),
+                    grad_gain_first,
+                    grad_shift_first,
+                    jnp.sum(d_down.astype(jnp.float32), axis=0),
+                    grad_gain_second,
+                    grad_shift_second,
+                ],
+                axis=1,
+            ),
+            up_bias_sums.reshape(width // shard, 4, shard).transpose(0, 2, 1).reshape(width, 4),
         ],
         axis=1,
     ).astype(low_type)
     out_block = jnp.concatenate(
-        [grad_wout.astype(low_type), jnp.pad(vec_block, ((0, 0), (0, LANES - 6)))], axis=1
+        [grad_wout.astype(low_type), jnp.pad(vec_block, ((0, 0), (0, lanes - 10)))], axis=1
     )
     up_block = grad_wup.astype(low_type)
+    down_block = grad_wdown.astype(low_type)
     context_back, down_block, out_block, up_block = lax.optimization_barrier(
         (context_back, down_block, out_block, up_block)
     )
+    up_sum = reduce_shards(up_block)
+
     back_at_head = to_heads(context_back, count, 2)
     grads_out = attend_back(meta, block_order, back_at_head, qa, ka, va, sums)
     grads_in = to_rows(grads_out, count, 3)
@@ -859,33 +882,15 @@
     last_block = jnp.concatenate(
         [
             grad_all.astype(low_type),
-            column_sums([d_queries.astype(jnp.float32), d_values.astype(jnp.float32)]),
+            column_sums([d_queries.astype(jnp.float32), d_values.astype(jnp.float32)], lanes),
         ],
         axis=1,
     )
     if direct:
-        fold = (2, 4, shard, width + LANES)
-        wide_block = jnp.concatenate(
-            [
-                up_block,
-                down_block.reshape(fold).transpose(0, 2, 1, 3).reshape(2 * shard, -1),
-                out_block,
-                last_block,
-            ],
-            axis=1,
-        )
-        unused = -wide_block.shape[1] % 512
-        wide_sum = grad_sum(jnp.pad(wide_block, ((0, 0), (0, unused))), 4)
-        edges = [0]
-        for piece in (wide, 4 * (width + LANES), width + LANES, 3 * width + LANES):
-            edges.append(edges[-1] + piece)
-        up_sum, down_sum, out_sum, last_sum = (
-            wide_sum[:, edges[k] : edges[k + 1]] for k in range(4)
-        )
-        down_sum = down_sum.reshape(shard, 4, -1).transpose(1, 0, 2).reshape(4 * shard, -1)
+        down_sum, last_sum, out_sum = grad_sum((down_block, last_block, out_block), 4)
     else:
-        up_sum, down_sum, out_sum, last_sum = (
-            reduce_shards(block) for block in (up_block, down_block, out_block, last_block)
+        down_sum, last_sum, out_sum = (
+            reduce_shards(block) for block in (down_block, last_block, out_block)
         )
     d_input = (
         d_hone
@@ -897,7 +902,6 @@
     wide_grad = last_sum.astype(jnp.float32)
     pair_grad = wide_grad[:, width : 3 * width].reshape(shard, HEADS, 2, HEAD_DIM)
     out_grad = out_sum.astype(jnp.float32)
-    down_grad = down_sum.astype(jnp.float32)
     return (
         activations,
         input_grad,
@@ -911,8 +915,8 @@
         out_grad[:, width + 1],
         out_grad[:, width + 2],
         up_sum.astype(jnp.float32),
-        down_grad[:, width],
-        down_grad[:, :width],
+        out_grad[:, width + 6 : width + 10].T.reshape(-1),
+        down_sum.astype(jnp.float32),
         out_grad[:, width + 3],
         out_grad[:, width + 4],
         out_grad[:, width + 5],

time: 738 us -> 585 us (0.79); the launches traced: 737 us -> 574 us
  waiting for transfers between devices: 72.9 us -> 2.81 us
  Pallas kernels: 453 us -> 390 us
  local copies, waits for them, and re-layouts: 107 us -> 72.1 us
    all_gather x4 -> x1, waiting for transfers between devices: 72.9 us -> 0.01 us  [reduce_shards(): return lax.all_gather(part, 'ctx', axis=0, tiled=True)]
    pallas_call x1, Pallas kernels: 191 us -> 137 us  [grad_sum(): pl.pallas_call(grad_sum_kernel, out_shape=tuple(outs), in_specs=[vmem] *...]
    unnamed x64 -> x75, local copies, waits for them, and re-layouts: 33 us -> 13.5 us
    dynamic_update_slice x0 -> x8, local copies, waits for them, and re-layouts: none -> 13.2 us  [the longest x4 8.93 us: gather_rows(): lax.dynamic_update_slice(whole, fetched, (other + core * (size // 2), 0))]
    pallas_call x1, Pallas kernels: 68.6 us -> 56.4 us  [attend_back(): pl.pallas_call(attend_back_kernel, out_shape=jax.ShapeDtypeStruct((count,...]
    transpose x1 -> x2, local copies, waits for them, and re-layouts: 12 us -> 0.2 us  [body(): out_grad[:, width + 6:width + 10].T.reshape(-1)]
    pad x1 -> x0, local copies, waits for them, and re-layouts: 11.3 us -> none  [body(): wide_sum = grad_sum(jnp.pad(wide_block, ((0, 0), (0, unused))), 4)]
    reshape x1 -> x2, local copies, waits for them, and re-layouts: 10.9 us -> 0.65 us  [the longest x1 0.64 us: body(): out_grad[:, width + 6:width + 10].T.reshape(-1)]
  transfers between devices with their start and end apart: 4 -> 10, of which waited for: 2 -> 1; matrix products, arithmetic and copies ran while one was open for 4% -> 16% of each run, Pallas kernels for 16% -> 65%
where the time goes in v3:
time: 585 us; the launch traced here: 574 us
  Pallas kernels  390 us (67%)
  local copies, waits for them, and re-layouts  72.1 us (12%)
  matrix products  47.7 us (8%)
  other arithmetic  37.7 us (6%)
  between operations  16 us (3%)
  starting transfers between devices  7.34 us (1%)
    pallas_call x1, Pallas kernels, grad_sum(): pl.pallas_call(grad_sum_kernel, out_shape=tuple(outs), in_specs=[vmem] *...  137 us
    pallas_call x2, Pallas kernels, to_rows(): pl.pallas_call(partial(to_rows_kernel, count), out_shape=jax.ShapeDtypeSt...  92.3 us
    pallas_call x2, Pallas kernels, to_heads(): pl.pallas_call(partial(to_heads_kernel, count), out_shape=jax.ShapeDtypeS...  64.4 us
    pallas_call x1, Pallas kernels, attend_back(): pl.pallas_call(attend_back_kernel, out_shape=jax.ShapeDtypeStruct((count,...  56.4 us
    pallas_call x1, Pallas kernels, attend(): pl.pallas_call(attend_kernel, out_shape=(jax.ShapeDtypeStruct((count, row...  34.8 us
    dot_general x1, matrix products, body(): jnp.dot(norm_low, up_weight, preferred_element_type=jnp.float32) + up_bias  13.6 us
    unnamed x75, local copies, waits for them, and re-layouts  13.5 us
  transfers between devices with their start and end apart: 10, of which 1 were waited for; matrix products, arithmetic and copies ran while one was open for 16% of the time, Pallas kernels for 65%

profile of v3, /device:TPU:9, one launch (start us, length us, event | category | flops | bytes accessed | tf_op | source)
XLA Modules:
  0.0 574.0 jit_solution(15049105320095869972)
XLA Ops:
  24.6 2.6 convert_element_type.170
  38.1 2.9 constant_dynamic-update-slice_fusion.5
  41.0 2.8 collective-permute-done
  57.6 3.2 slice.127.wkv_ref
  62.8 5.1 project.1.send_ref
  68.0 45.4 %to_heads_576.1.recv_ref = bf16[16,576,128]{2,1,0:T(8,128)(2,1)} custom-call(bf16[12,576,128]{2,1,0:T(8,128)(2,1)} %project.1.send_ref), custom_call_target="tpu_custom_call" | custom-call | flops 143999991808 | bytes 3538944 | tf_op jit(solution)/shard_map/to_heads_576/pallas_call | solution.py:122
  113.4 34.8 %attend.1 = (bf16[16,192,128]{2,1,0:T(8,128)(2,1)}, bf16[6144,128]{1,0:T(8,128)(2,1)}, bf16[6144,128]{1,0:T(8,128)(2,1)}, bf16[6144,128]{1,0:T(8,128)(2,1)}, f32[6144,128]{1,0:T(8,128)}) custom-call(s32[4]{0:T(128)} %pad_add_fusion.meta_ref, s32[32]{0:T(128)} %order_ref.3, bf16[16,576,128]{2,1,0:T(8,128)(2,1)} %to_heads_576.1.recv_ref), custom_call_target="tpu_custom_call" | custom-call | flops 38654705664 | bytes 9437184 | tf_op jit(solution)/shard_map/attend/pallas_call | solution.py:335
  149.0 23.5 %to_rows_192.1 = bf16[12,192,128]{2,1,0:T(8,128)(2,1)} custom-call(bf16[16,192,128]{2,1,0:T(8,128)(2,1)} %get-tuple-element.40.send_ref), custom_call_target="tpu_custom_call" | custom-call | flops 48000000000 | bytes 1572864 | tf_op jit(solution)/shard_map/to_rows_192/pallas_call | solution.py:196
  179.2 2.7 constant_dynamic-update-slice_fusion.1
  188.2 13.6 %multiply_convert_fusion = (bf16[384,3072]{1,0:T(8,128)(2,1)S(1)}, f32[384,3072]{1,0:T(8,128)S(1)}, f32[384,3072]{1,0:T(8,128)}) fusion(f32[3072]{0:T(1024)S(1)} %bitcast.95, bf16[768,3072]{1,0:T(8,128)(2,1)S(1)} %constant_dynamic-update-slice_fusion.3, f32[384,768]{1,0:T(8,128)S(1)} %get-tuple-element.150, f32[768]{0:T(1024)S(1)} %copy-done.30, ...), kind=kOutput, calls=%fused_computation.8 | convolution fusion | flops 1891270656 | bytes 17716224 | tf_op jit(solution)/shard_map/dot_general | solution.py:810
  206.5 4.5 convolution_convert_fusion.2
  211.1 5.1 fusion.68
  223.0 4.6 convolution_convert_fusion.1
  231.1 19.1 %to_heads_192.1.recv_ref = bf16[16,192,128]{2,1,0:T(8,128)(2,1)} custom-call(bf16[12,192,128]{2,1,0:T(8,128)(2,1)} %copy.106.send_ref), custom_call_target="tpu_custom_call" | custom-call | flops 48000000000 | bytes 1179648 | tf_op jit(solution)/shard_map/to_heads_192/pallas_call | solution.py:122
  250.2 56.4 %attend_back.1.send_ref = bf16[16,576,128]{2,1,0:T(8,128)(2,1)} custom-call(s32[4]{0:T(128)} %pad_add_fusion.meta_ref, s32[32]{0:T(128)} %order_ref.3, bf16[16,192,128]{2,1,0:T(8,128)(2,1)} %to_heads_192.1.recv_ref, bf16[6144,128]{1,0:T(8,128)(2,1)} %get-tuple-element.45.qa_ref, bf16[6144,128]{1,0:T(8,128)(2,1)} %get-tuple-element.46.ka_ref, ...), custom_call_target="tpu_custom_call" | custom-call | flops 77309411328 | bytes 12582912 | tf_op jit(solution)/shard_map/attend_back/pallas_call | solution.py:464
  306.7 68.8 %to_rows_576.1 = bf16[12,576,128]{2,1,0:T(8,128)(2,1)} custom-call(bf16[16,576,128]{2,1,0:T(8,128)(2,1)} %attend_back.1.send_ref), custom_call_target="tpu_custom_call" | custom-call | flops 143999991808 | bytes 4718592 | tf_op jit(solution)/shard_map/to_rows_576/pallas_call | solution.py:196
  384.9 3.1 fusion.7
  390.1 6.3 %copy.111 = bf16[768,2560]{1,0:T(8,128)(2,1)} copy(bf16[768,2560]{0,1:T(8,128)(2,1)} %pad_maximum_fusion) | data formatting | bytes 7864320 | tf_op jit(solution)/shard_map/concatenate | solution.py:882
  398.1 137.2 %grad_sum.1 = (bf16[2,2,384,768]{3,2,1,0:T(8,128)(2,1)}, bf16[2,2,96,2560]{3,2,1,0:T(8,128)(2,1)}, bf16[2,2,96,1024]{3,2,1,0:T(8,128)(2,1)}) custom-call(bf16[2,2,2,384,768]{4,3,2,1,0:T(8,128)(2,1)} %bitcast.99, bf16[2,2,2,96,2560]{4,3,2,1,0:T(8,128)(2,1)} %bitcast.82, bf16[2,2,2,96,1024]{4,3,2,1,0:T(8,128)(2,1)} %bitcast.92), custom_call_target="tpu_custom_call" | custom-call | flops 102236160000 | bytes 20447232 | tf_op jit(solution)/shard_map/grad_sum/pallas_call | solution.py:660
  544.8 2.7 copy.115
  553.6 2.9 fusion.56
  556.5 3.0 fusion.31
  559.6 2.7 bitcast_convert_fusion
  562.3 4.4 convert_element_type.198
  (214 shorter events, 100.6 us)
Async XLA Ops:
  7.2 8.1 %copy-start.16 = (f32[384,768]{1,0:T(8,128)S(1)}, f32[384,768]{1,0:T(8,128)}, u32[]{:S(2)}) copy-start(f32[384,768]{1,0:T(8,128)} %param.25) | copy-start | bytes 3538948
  7.2 390.9 %reduce-scatter.2.cloned.1.call-start = ((), (), s32[]{:S(2)}) async-start(), calls=%async_computation.1 | async-start | bytes 4866048 | tf_op jit(solution)/shard_map/reduce_scatter | solution.py:698
  19.3 5.0 copy-start.29
  21.9 21.9 %collective-permute-start = (bf16[192,2432]{1,0:T(8,128)(2,1)}, bf16[192,2432]{1,0:T(8,128)(2,1)}, u32[]{:S(2)}, u32[]{:S(2)}) collective-permute-start(bf16[192,2432]{1,0:T(8,128)(2,1)} %constant_dynamic-slice_fusion.3), channel_id=1, source_target_pairs={{0,1},{1,0},{2,3},{3,2},{4,5},{5,4},{6,7},{7,6},{8,9},{9,8},{10,11... | collective-permute-start | bytes 2801672 | tf_op jit(solution)/shard_map/ppermute | solution.py:750
  41.0 8.8 %copy-start.7 = (bf16[768,3072]{1,0:T(8,128)(2,1)}, bf16[768,3072]{1,0:T(8,128)(2,1)S(1)}, u32[]{:S(2)}) copy-start(bf16[768,3072]{1,0:T(8,128)(2,1)S(1)} %get-tuple-element.139) | copy-start | bytes 14155780
  41.0 7.6 %copy-start.6 = (bf16[1536,896]{1,0:T(8,128)(2,1)S(1)}, bf16[1536,896]{1,0:T(8,128)(2,1)}, u32[]{:S(2)}) copy-start(bf16[1536,896]{1,0:T(8,128)(2,1)} %get-tuple-element.39) | copy-start | bytes 8257540
  43.8 9.4 %collective-permute-start.1 = (bf16[192,2432]{1,0:T(8,128)(2,1)}, bf16[192,2432]{1,0:T(8,128)(2,1)S(1)}, u32[]{:S(2)}, u32[]{:S(2)}) collective-permute-start(bf16[192,2432]{1,0:T(8,128)(2,1)} %collective-permute-done), channel_id=1, source_target_pairs={{0,2},{2,0},{4,6},{6,4},{8,10},{10,8},{12,14},{14,12},{16,18},{18,... | collective-permute-start | bytes 2801672 | tf_op jit(solution)/shard_map/ppermute | solution.py:756
  46.0 102.1 %collective-permute-start.2 = (bf16[192,768]{1,0:T(8,128)(2,1)}, bf16[192,768]{1,0:T(8,128)(2,1)}, u32[]{:S(2)}, u32[]{:S(2)}) collective-permute-start(bf16[192,768]{1,0:T(8,128)(2,1)} %constant_dynamic-slice_fusion.2), channel_id=1, source_target_pairs={{0,1},{1,0},{2,3},{3,2},{4,5},{5,4},{6,7},{7,6},{8,9},{9,8},{10,11... | collective-permute-start | bytes 884744 | tf_op jit(solution)/shard_map/ppermute | solution.py:750
  48.3 99.8 %collective-permute-start.3 = (bf16[192,3072]{1,0:T(8,128)(2,1)}, bf16[192,3072]{1,0:T(8,128)(2,1)}, u32[]{:S(2)}, u32[]{:S(2)}) collective-permute-start(bf16[192,3072]{1,0:T(8,128)(2,1)} %constant_dynamic-slice_fusion.1), channel_id=1, source_target_pairs={{0,1},{1,0},{2,3},{3,2},{4,5},{5,4},{6,7},{7,6},{8,9},{9,8},{10,11... | collective-permute-start | bytes 3538952 | tf_op jit(solution)/shard_map/ppermute | solution.py:750
  49.8 98.3 %collective-permute-start.4 = (bf16[768,896]{1,0:T(8,128)(2,1)}, bf16[768,896]{1,0:T(8,128)(2,1)}, u32[]{:S(2)}, u32[]{:S(2)}) collective-permute-start(bf16[768,896]{1,0:T(8,128)(2,1)} %constant_dynamic-slice_fusion), channel_id=1, source_target_pairs={{0,1},{1,0},{2,3},{3,2},{4,5},{5,4},{6,7},{7,6},{8,9},{9,8},{10,11... | collective-permute-start | bytes 4128776 | tf_op jit(solution)/shard_map/ppermute | solution.py:750
  148.1 39.4 %collective-permute-start.7 = (bf16[768,896]{1,0:T(8,128)(2,1)}, bf16[768,896]{1,0:T(8,128)(2,1)S(1)}, u32[]{:S(2)}, u32[]{:S(2)}) collective-permute-start(bf16[768,896]{1,0:T(8,128)(2,1)} %collective-permute-done.4), channel_id=1, source_target_pairs={{0,2},{2,0},{4,6},{6,4},{8,10},{10,8},{12,14},{14,12},{16,18},{18,... | collective-permute-start | bytes 4128776 | tf_op jit(solution)/shard_map/ppermute | solution.py:756
  148.9 37.1 %collective-permute-start.6 = (bf16[192,3072]{1,0:T(8,128)(2,1)}, bf16[192,3072]{1,0:T(8,128)(2,1)}, u32[]{:S(2)}, u32[]{:S(2)}) collective-permute-start(bf16[192,3072]{1,0:T(8,128)(2,1)} %collective-permute-done.3), channel_id=1, source_target_pairs={{0,2},{2,0},{4,6},{6,4},{8,10},{10,8},{12,14},{14,12},{16,18},{18,... | collective-permute-start | bytes 3538952 | tf_op jit(solution)/shard_map/ppermute | solution.py:756
  172.5 9.3 %collective-permute-start.5 = (bf16[192,768]{1,0:T(8,128)(2,1)}, bf16[192,768]{1,0:T(8,128)(2,1)}, u32[]{:S(2)}, u32[]{:S(2)}) collective-permute-start(bf16[192,768]{1,0:T(8,128)(2,1)} %collective-permute-done.2), channel_id=1, source_target_pairs={{0,2},{2,0},{4,6},{6,4},{8,10},{10,8},{12,14},{14,12},{16,18},{18,... | collective-permute-start | bytes 884744 | tf_op jit(solution)/shard_map/ppermute | solution.py:756
  177.0 6.5 %copy-start.19 = (bf16[1,384,768]{2,1,0:T(8,128)(2,1)S(1)}, bf16[1,384,768]{2,1,0:T(8,128)(2,1)}, u32[]{:S(2)}) copy-start(bf16[1,384,768]{2,1,0:T(8,128)(2,1)} %param.19) | copy-start | bytes 1769476
  177.1 6.5 %copy-start.32 = (f32[768]{0:T(1024)S(1)}, f32[768]{0:T(1024)}, u32[]{:S(2)}) copy-start(f32[768]{0:T(1024)} %get-tuple-element.125) | copy-start | bytes 9220
  179.2 6.9 %copy-start.8 = (bf16[768,3072]{1,0:T(8,128)(2,1)S(1)}, bf16[768,3072]{1,0:T(8,128)(2,1)}, u32[]{:S(2)}) copy-start(bf16[768,3072]{1,0:T(8,128)(2,1)} %constant_dynamic-update-slice_fusion.4) | copy-start | bytes 14155780
  183.6 3.9 copy-start.4
  188.2 13.6 %copy-start.31 = (f32[768]{0:T(1024)S(1)}, f32[768]{0:T(1024)}, u32[]{:S(2)}) copy-start(f32[768]{0:T(1024)} %get-tuple-element.122) | copy-start | bytes 9220
  250.2 312.1 %all-gather.2.cloned.1.call-start = ((), (), s32[]{:S(2)}) async-start(), calls=%async_computation.2 | async-start | bytes 2506752 | tf_op jit(solution)/shard_map/all_gather | solution.py:701
  380.5 4.4 copy-start.10
  383.0 5.0 copy-start.14
  390.1 6.3 %copy-start.5 = (bf16[768,1024]{0,1:T(8,128)(2,1)S(1)}, bf16[768,1024]{0,1:T(8,128)(2,1)}, u32[]{:S(2)}) copy-start(bf16[768,1024]{0,1:T(8,128)(2,1)} %fusion.21) | copy-start | bytes 4718596
  544.8 4.1 copy-start.18
  549.2 4.4 copy-start.11
  (21 other events, 46.7 us)
Sparse Core Ops, SparseCore 0:
  250.3 143.3 reduce-scatter.1
  398.2 57.5 all-gather.1

commit v4 on v3

--- a/solution.py
+++ b/solution.py
@@ -482,8 +482,11 @@
     )(meta, order, recv, qa, ka, va, sums)
 
 
-PART_ORDERS = (("x", "z", "wa"), ("wa", "x", "z"), ("z", "wa", "x"))
-GATHER_ORDERS = (("x", "z"), ("z", "x"), ("z", "x"))
+PART_ORDERS = (("x", "z"), ("z", "x"), ("wa", "x", "z"), ("z", "wa", "x"))
+GATHER_ORDERS = (("z", "x"), ("z", "x"), ("z", "x"), ("z", "x"))
+PARTS = 4
+EARLY = 2
+STAGES = sum(len(order) for order in PART_ORDERS)
 SIZES = {"wa": 2, "x": 2, "z": 4}
 
 
@@ -508,8 +511,13 @@
 
 
 def grad_sum_kernel(*refs):
-    g_refs, out_refs, core_bufs, bufs = refs[:3], refs[3:6], refs[6:9], refs[9:18]
-    send_sem, recv_sem = refs[18:]
+    refs = list(refs)
+    sizes = (PARTS, PARTS, PARTS - EARLY, STAGES)
+    g_refs, out_refs, core_bufs, bufs = (
+        [refs.pop(0) for _ in range(number)] for number in sizes
+    )
+    core_bufs = [None] * EARLY + core_bufs
+    send_sem, recv_sem = refs
     links = Links()
     core, x, z, wa = (links.at[name] for name in ("core", "x", "z", "wa"))
     barrier = pltpu.get_barrier_semaphore()
@@ -548,8 +556,8 @@
             at[axis] = value
             held = held | {axis}
         return g_refs[part].at[
-            pl.ds(at["wa"], 1) if "wa" in held else pl.ds(0, 2),
-            core,
+            pl.ds(0, 1) if part < EARLY else pl.ds(at["wa"], 1) if "wa" in held else pl.ds(0, 2),
+            0 if part < EARLY else core,
             pl.ds(at["x"], 1) if "x" in held else pl.ds(0, 2),
             *z_share(g_refs[part], at["z"] if "z" in held else None),
         ]
@@ -571,13 +579,16 @@
 
     core_copies = [
         remote(g_refs[part].at[:, 1 - core], core_bufs[part], links.peer("core", 1 - core))
-        for part in range(3)
+        if part >= EARLY
+        else None
+        for part in range(PARTS)
     ]
+    first_buf = [sum(len(order) for order in PART_ORDERS[:part]) for part in range(PARTS)]
 
     def begin(part, stage):
         axis = PART_ORDERS[part][stage]
         held = set(PART_ORDERS[part][:stage])
-        buf = bufs[part * 3 + stage]
+        buf = bufs[first_buf[part] + stage]
         copies = []
         for step in range(1, SIZES[axis]):
             value = lax.rem(links.at[axis] + step, SIZES[axis])
@@ -587,22 +598,24 @@
         return copies
 
     flying = {}
-    for part in range(3):
-        core_copies[part].wait()
-        add_into(slab(part, set()), [core_bufs[part]])
+    for part in range(PARTS):
+        if part >= EARLY:
+            core_copies[part].wait()
+            add_into(slab(part, set()), [core_bufs[part]])
         flying[part] = begin(part, 0)
     for stage in range(3):
-        for part in range(3):
-            axis = PART_ORDERS[part][stage]
+        for part in range(PARTS):
+            order = PART_ORDERS[part]
+            if stage >= len(order):
+                continue
             for copy in flying[part]:
                 copy.wait()
-            buf = bufs[part * 3 + stage]
+            buf = bufs[first_buf[part] + stage]
             add_into(
-                slab(part, set(PART_ORDERS[part][: stage + 1])),
-                [buf.at[step] for step in range(SIZES[axis] - 1)],
+                slab(part, set(order[: stage + 1])),
+                [buf.at[step] for step in range(SIZES[order[stage]] - 1)],
             )
-            if stage < 2:
-                flying[part] = begin(part, stage + 1)
+            flying[part] = begin(part, stage + 1) if stage + 1 < len(order) else None
 
     def out_slab(part, held):
         return out_refs[part].at[
@@ -619,11 +632,11 @@
             for step in range(1, SIZES[axis])
         ]
 
-    for part in range(3):
+    for part in range(PARTS):
         out_slab(part, {"x", "z"})[...] = slab(part, {"wa", "x", "z"})[0]
         flying[part] = spread(part, 0)
     for stage in range(2):
-        for part in range(3):
+        for part in range(PARTS):
             for copy in flying[part]:
                 copy.wait()
             if stage == 0:
@@ -631,7 +644,7 @@
             else:
                 block = out_slab(part, set())
                 flying[part] = [remote(block, block, links.peer("core", 1 - core))]
-    for part in range(3):
+    for part in range(PARTS):
         for copy in flying[part]:
             copy.wait()
 
@@ -640,8 +653,9 @@
     bufs, core_bufs, outs, given = [], [], [], []
     for part, grad in enumerate(grads):
         rows, width = grad.shape
-        piece = rows // 8
-        shape = {"wa": 2, "x": 2, "z": 4}
+        early = part < EARLY
+        piece = rows // 2 if early else rows // 8
+        shape = {"wa": 1 if early else 2, "x": 2, "z": 4}
         for axis in PART_ORDERS[part]:
             shape[axis] //= SIZES[axis]
             share = (
@@ -652,21 +666,23 @@
             bufs.append(
                 pltpu.VMEM((SIZES[axis] - 1, shape["wa"], shape["x"], *share), low_type)
             )
-        core_bufs.append(pltpu.VMEM((2, 2, piece, width), low_type))
+        if not early:
+            core_bufs.append(pltpu.VMEM((2, 2, piece, width), low_type))
         outs.append(jax.ShapeDtypeStruct((2, 2, piece, width), low_type))
-        given.append(grad.reshape(2, 2, 2, piece, width))
+        lead = (1, 1) if early else (2, 2)
+        given.append(grad.reshape(*lead, 2, piece, width))
     vmem = pl.BlockSpec(memory_space=pltpu.VMEM)
     size = sum(grad.size for grad in grads)
     sums = pl.pallas_call(
         grad_sum_kernel,
         out_shape=tuple(outs),
-        in_specs=[vmem] * 3,
-        out_specs=(vmem,) * 3,
+        in_specs=[vmem] * PARTS,
+        out_specs=(vmem,) * PARTS,
         scratch_shapes=[
             *core_bufs,
             *bufs,
-            pltpu.SemaphoreType.DMA((40,)),
-            pltpu.SemaphoreType.DMA((40,)),
+            pltpu.SemaphoreType.DMA((48,)),
+            pltpu.SemaphoreType.DMA((48,)),
         ],
         compiler_params=pltpu.CompilerParams(
             collective_id=collective_id, has_side_effects=True, vmem_limit_bytes=VMEM_BYTES
@@ -859,13 +875,34 @@
     )
     up_block = grad_wup.astype(low_type)
     down_block = grad_wdown.astype(low_type)
+    def add_low(mine, given):
+        return (mine.astype(jnp.float32) + given.astype(jnp.float32)).astype(low_type)
+
+    def core_halves(block):
+        view = block.reshape(2, 2, -1, block.shape[1])
+        keep = lax.dynamic_index_in_dim(view, core, 1, keepdims=False)
+        give = lax.dynamic_index_in_dim(view, 1 - core, 1, keepdims=False)
+        return keep, lax.ppermute(give, "ctx", [(k, k ^ 1) for k in range(count)])
+
+    def wa_halves(block):
+        keep = lax.dynamic_index_in_dim(block, wa, 0, keepdims=False)
+        give = lax.dynamic_index_in_dim(block, 1 - wa, 0, keepdims=False)
+        return keep, lax.ppermute(give, "wa", [(0, 1), (1, 0)])
+
     context_back, down_block, out_block, up_block = lax.optimization_barrier(
         (context_back, down_block, out_block, up_block)
     )
-    up_sum = reduce_shards(up_block)
-
-    back_at_head = to_heads(context_back, count, 2)
-    grads_out = attend_back(meta, block_order, back_at_head, qa, ka, va, sums)
+    if direct:
+        halves = [core_halves(block) for block in (up_block, down_block)]
+        back_at_head = to_heads(context_back, count, 2)
+        back_at_head, halves = lax.optimization_barrier((back_at_head, halves))
+        halves = [wa_halves(add_low(*pair)) for pair in halves]
+        grads_out = attend_back(meta, block_order, back_at_head, qa, ka, va, sums)
+        grads_out, halves = lax.optimization_barrier((grads_out, halves))
+        early = [add_low(*pair) for pair in halves]
+    else:
+        back_at_head = to_heads(context_back, count, 2)
+        grads_out = attend_back(meta, block_order, back_at_head, qa, ka, va, sums)
     grads_in = to_rows(grads_out, count, 3)
 
     d_pair = grads_in[:, :tok_rows, :].transpose(1, 0, 2).reshape(tok_rows, 2 * width)
@@ -887,10 +924,10 @@
         axis=1,
     )
     if direct:
-        down_sum, last_sum, out_sum = grad_sum((down_block, last_block, out_block), 4)
+        up_sum, down_sum, last_sum, out_sum = grad_sum((*early, last_block, out_block), 4)
     else:
-        down_sum, last_sum, out_sum = (
-            reduce_shards(block) for block in (down_block, last_block, out_block)
+        up_sum, down_sum, last_sum, out_sum = (
+            reduce_shards(block) for block in (up_block, down_block, last_block, out_block)
         )
     d_input = (
         d_hone

time: 585 us -> 593 us (1.014)
  between operations: 16 us -> 2.32 us
  Pallas kernels: 390 us -> 399 us
  other arithmetic: 37.7 us -> 44.8 us
    pallas_call x2, Pallas kernels: 92.3 us -> 82.5 us  [to_rows(): pl.pallas_call(partial(to_rows_kernel, count), out_shape=jax.ShapeDtypeSt...]
    squeeze x0 -> x4, local copies, waits for them, and re-layouts: none -> 9.43 us  [the longest x2 6.69 us: core_halves(): give = lax.dynamic_index_in_dim(view, 1 - core, 1, keepdims=False)]
    pallas_call x1, Pallas kernels: 56.4 us -> 65.6 us  [attend_back(): pl.pallas_call(attend_back_kernel, out_shape=jax.ShapeDtypeStruct((count,...]
    convert_element_type x0 -> x4, other arithmetic: none -> 8.22 us  [add_low(): (mine.astype(jnp.float32) + given.astype(jnp.float32)).astype(low_type)]
    unnamed x75 -> x83, local copies, waits for them, and re-layouts: 13.5 us -> 14.4 us
  transfers between devices with their start and end apart: 10 -> 12, of which waited for: 1 -> 1; matrix products, arithmetic and copies ran while one was open for 16% -> 9% of each run, Pallas kernels for 65% -> 34%
where the time goes in v4:
time: 593 us; the launch traced here: 585 us
  Pallas kernels  399 us (67%)
  local copies, waits for them, and re-layouts  78 us (13%)
  matrix products  48.8 us (8%)
  other arithmetic  44.8 us (8%)
  starting transfers between devices  9.46 us (2%)
    pallas_call x1, Pallas kernels, grad_sum(): pl.pallas_call(grad_sum_kernel, out_shape=tuple(outs), in_specs=[vmem] *...  142 us
    pallas_call x2, Pallas kernels, to_rows(): pl.pallas_call(partial(to_rows_kernel, count), out_shape=jax.ShapeDtypeSt...  82.5 us
    pallas_call x1, Pallas kernels, attend_back(): pl.pallas_call(attend_back_kernel, out_shape=jax.ShapeDtypeStruct((count,...  65.6 us
    pallas_call x2, Pallas kernels, to_heads(): pl.pallas_call(partial(to_heads_kernel, count), out_shape=jax.ShapeDtypeS...  64.4 us
    pallas_call x1, Pallas kernels, attend(): pl.pallas_call(attend_kernel, out_shape=(jax.ShapeDtypeStruct((count, row...  40 us
    unnamed x83, local copies, waits for them, and re-layouts  14.4 us
    dot_general x1, matrix products, body(): jnp.dot(norm_low, up_weight, preferred_element_type=jnp.float32) + up_bias  13.6 us
  transfers between devices with their start and end apart: 12, of which 1 were waited for; matrix products, arithmetic and copies ran while one was open for 9% of the time, Pallas kernels for 34%

profile of v4, /device:TPU:9, one launch (start us, length us, event | category | flops | bytes accessed | tf_op | source)
XLA Modules:
  0.0 585.2 jit_solution(8529316327192496379)
XLA Ops:
  31.5 2.9 constant_dynamic-update-slice_fusion.5
  34.4 2.6 collective-permute-done
  51.1 3.2 slice.127.wkv_ref
  56.3 5.1 project.1.send_ref
  61.4 45.4 %to_heads_576.1.recv_ref = bf16[16,576,128]{2,1,0:T(8,128)(2,1)} custom-call(bf16[12,576,128]{2,1,0:T(8,128)(2,1)} %project.1.send_ref), custom_call_target="tpu_custom_call" | custom-call | flops 143999991808 | bytes 3538944 | tf_op jit(solution)/shard_map/to_heads_576/pallas_call | solution.py:122
  106.8 40.0 %attend.1 = (bf16[16,192,128]{2,1,0:T(8,128)(2,1)}, bf16[6144,128]{1,0:T(8,128)(2,1)}, bf16[6144,128]{1,0:T(8,128)(2,1)}, bf16[6144,128]{1,0:T(8,128)(2,1)}, f32[6144,128]{1,0:T(8,128)}) custom-call(s32[4]{0:T(128)} %pad_add_fusion.meta_ref, s32[32]{0:T(128)} %order_ref.3, bf16[16,576,128]{2,1,0:T(8,128)(2,1)} %to_heads_576.1.recv_ref), custom_call_target="tpu_custom_call" | custom-call | flops 38654705664 | bytes 9437184 | tf_op jit(solution)/shard_map/attend/pallas_call | solution.py:335
  147.7 23.5 %to_rows_192.1 = bf16[12,192,128]{2,1,0:T(8,128)(2,1)} custom-call(bf16[16,192,128]{2,1,0:T(8,128)(2,1)} %get-tuple-element.51.send_ref), custom_call_target="tpu_custom_call" | custom-call | flops 48000000000 | bytes 1572864 | tf_op jit(solution)/shard_map/to_rows_192/pallas_call | solution.py:196
  177.9 2.7 constant_dynamic-update-slice_fusion.1
  186.8 13.6 %multiply_convert_fusion = (bf16[384,3072]{1,0:T(8,128)(2,1)S(1)}, f32[384,3072]{1,0:T(8,128)S(1)}, f32[384,3072]{1,0:T(8,128)}) fusion(f32[3072]{0:T(1024)S(1)} %bitcast.123, bf16[768,3072]{1,0:T(8,128)(2,1)S(1)} %constant_dynamic-update-slice_fusion.3, f32[384,768]{1,0:T(8,128)S(1)} %get-tuple-element.180, f32[768]{0:T(1024)S(1)} %copy-done.32, ...), kind=kOutput, calls=%fused_computation.10 | convolution fusion | flops 1891270656 | bytes 17716224 | tf_op jit(solution)/shard_map/dot_general | solution.py:826
  205.2 4.7 convolution_convert_fusion.2
  209.9 5.1 fusion.68
  222.0 4.6 convolution_convert_fusion.1
  230.1 5.0 dynamic-slice_bitcast_fusion.2
  239.9 19.0 %to_heads_192.1.recv_ref = bf16[16,192,128]{2,1,0:T(8,128)(2,1)} custom-call(bf16[12,192,128]{2,1,0:T(8,128)(2,1)} %copy.106.send_ref), custom_call_target="tpu_custom_call" | custom-call | flops 48000000000 | bytes 1179648 | tf_op jit(solution)/shard_map/to_heads_192/pallas_call | solution.py:122
  259.0 3.3 add_convert_fusion.1
  268.7 65.6 %attend_back.1.send_ref = bf16[16,576,128]{2,1,0:T(8,128)(2,1)} custom-call(s32[4]{0:T(128)} %pad_add_fusion.meta_ref, s32[32]{0:T(128)} %order_ref.3, bf16[16,192,128]{2,1,0:T(8,128)(2,1)} %to_heads_192.1.recv_ref, bf16[6144,128]{1,0:T(8,128)(2,1)} %get-tuple-element.59.qa_ref, bf16[6144,128]{1,0:T(8,128)(2,1)} %get-tuple-element.60.ka_ref, ...), custom_call_target="tpu_custom_call" | custom-call | flops 77309411328 | bytes 12582912 | tf_op jit(solution)/shard_map/attend_back/pallas_call | solution.py:464
  335.3 59.0 %to_rows_576.1 = bf16[12,576,128]{2,1,0:T(8,128)(2,1)} custom-call(bf16[16,576,128]{2,1,0:T(8,128)(2,1)} %attend_back.1.send_ref), custom_call_target="tpu_custom_call" | custom-call | flops 143999991808 | bytes 4718592 | tf_op jit(solution)/shard_map/to_rows_576/pallas_call | solution.py:196
  397.1 3.8 fusion.56
  403.0 3.1 fusion.7
  408.2 6.4 %copy.111 = bf16[768,2560]{1,0:T(8,128)(2,1)} copy(bf16[768,2560]{0,1:T(8,128)(2,1)} %pad_maximum_fusion) | data formatting | bytes 7864320 | tf_op jit(solution)/shard_map/concatenate | solution.py:919
  418.0 141.6 %grad_sum.1 = (bf16[2,2,96,3072]{3,2,1,0:T(8,128)(2,1)}, bf16[2,2,384,768]{3,2,1,0:T(8,128)(2,1)}, bf16[2,2,96,2560]{3,2,1,0:T(8,128)(2,1)}, bf16[2,2,96,1024]{3,2,1,0:T(8,128)(2,1)}) custom-call(bf16[1,1,2,96,3072]{4,3,2,1,0:T(8,128)(2,1)} %bitcast.119, bf16[1,1,2,384,768]{4,3,2,1,0:T(8,128)(2,1)} %bitcast.120, bf16[2,2,2,96,2560]{4,3,2,1,0:T(8,128)(2,1)} %bitcast.108, ...), custom_call_target="tpu_custom_call" | custom-call | flops 78643200000 | bytes 15728640 | tf_op jit(solution)/shard_map/grad_sum/pallas_call | solution.py:676
  567.5 3.0 fusion.31
  577.1 4.6 bitcast_convert_fusion.1
  582.3 2.7 bitcast_convert_fusion
  (234 shorter events, 112.4 us)
Async XLA Ops:
  0.7 8.0 %copy-start.17 = (f32[384,768]{1,0:T(8,128)S(1)}, f32[384,768]{1,0:T(8,128)}, u32[]{:S(2)}) copy-start(f32[384,768]{1,0:T(8,128)} %param.25) | copy-start | bytes 3538948
  12.6 5.1 copy-start.31
  15.2 21.9 %collective-permute-start = (bf16[192,2432]{1,0:T(8,128)(2,1)}, bf16[192,2432]{1,0:T(8,128)(2,1)}, u32[]{:S(2)}, u32[]{:S(2)}) collective-permute-start(bf16[192,2432]{1,0:T(8,128)(2,1)} %constant_dynamic-slice_fusion.3), channel_id=1, source_target_pairs={{0,1},{1,0},{2,3},{3,2},{4,5},{5,4},{6,7},{7,6},{8,9},{9,8},{10,11... | collective-permute-start | bytes 2801672 | tf_op jit(solution)/shard_map/ppermute | solution.py:766
  34.4 8.7 %copy-start.8 = (bf16[768,3072]{1,0:T(8,128)(2,1)}, bf16[768,3072]{1,0:T(8,128)(2,1)S(1)}, u32[]{:S(2)}) copy-start(bf16[768,3072]{1,0:T(8,128)(2,1)S(1)} %get-tuple-element.161) | copy-start | bytes 14155780
  34.4 7.5 %copy-start.5 = (bf16[1536,896]{1,0:T(8,128)(2,1)S(1)}, bf16[1536,896]{1,0:T(8,128)(2,1)}, u32[]{:S(2)}) copy-start(bf16[1536,896]{1,0:T(8,128)(2,1)} %get-tuple-element.50) | copy-start | bytes 8257540
  37.1 9.6 %collective-permute-start.1 = (bf16[192,2432]{1,0:T(8,128)(2,1)}, bf16[192,2432]{1,0:T(8,128)(2,1)S(1)}, u32[]{:S(2)}, u32[]{:S(2)}) collective-permute-start(bf16[192,2432]{1,0:T(8,128)(2,1)} %collective-permute-done), channel_id=1, source_target_pairs={{0,2},{2,0},{4,6},{6,4},{8,10},{10,8},{12,14},{14,12},{16,18},{18,... | collective-permute-start | bytes 2801672 | tf_op jit(solution)/shard_map/ppermute | solution.py:772
  39.4 107.5 %collective-permute-start.2 = (bf16[192,768]{1,0:T(8,128)(2,1)}, bf16[192,768]{1,0:T(8,128)(2,1)}, u32[]{:S(2)}, u32[]{:S(2)}) collective-permute-start(bf16[192,768]{1,0:T(8,128)(2,1)} %constant_dynamic-slice_fusion.2), channel_id=1, source_target_pairs={{0,1},{1,0},{2,3},{3,2},{4,5},{5,4},{6,7},{7,6},{8,9},{9,8},{10,11... | collective-permute-start | bytes 884744 | tf_op jit(solution)/shard_map/ppermute | solution.py:766
  41.7 105.1 %collective-permute-start.3 = (bf16[192,3072]{1,0:T(8,128)(2,1)}, bf16[192,3072]{1,0:T(8,128)(2,1)}, u32[]{:S(2)}, u32[]{:S(2)}) collective-permute-start(bf16[192,3072]{1,0:T(8,128)(2,1)} %constant_dynamic-slice_fusion.1), channel_id=1, source_target_pairs={{0,1},{1,0},{2,3},{3,2},{4,5},{5,4},{6,7},{7,6},{8,9},{9,8},{10,11... | collective-permute-start | bytes 3538952 | tf_op jit(solution)/shard_map/ppermute | solution.py:766
  43.1 103.7 %collective-permute-start.4 = (bf16[768,896]{1,0:T(8,128)(2,1)}, bf16[768,896]{1,0:T(8,128)(2,1)}, u32[]{:S(2)}, u32[]{:S(2)}) collective-permute-start(bf16[768,896]{1,0:T(8,128)(2,1)} %constant_dynamic-slice_fusion), channel_id=1, source_target_pairs={{0,1},{1,0},{2,3},{3,2},{4,5},{5,4},{6,7},{7,6},{8,9},{9,8},{10,11... | collective-permute-start | bytes 4128776 | tf_op jit(solution)/shard_map/ppermute | solution.py:766
  146.8 39.3 %collective-permute-start.7 = (bf16[768,896]{1,0:T(8,128)(2,1)}, bf16[768,896]{1,0:T(8,128)(2,1)S(1)}, u32[]{:S(2)}, u32[]{:S(2)}) collective-permute-start(bf16[768,896]{1,0:T(8,128)(2,1)} %collective-permute-done.4), channel_id=1, source_target_pairs={{0,2},{2,0},{4,6},{6,4},{8,10},{10,8},{12,14},{14,12},{16,18},{18,... | collective-permute-start | bytes 4128776 | tf_op jit(solution)/shard_map/ppermute | solution.py:772
  147.7 37.1 %collective-permute-start.6 = (bf16[192,3072]{1,0:T(8,128)(2,1)}, bf16[192,3072]{1,0:T(8,128)(2,1)}, u32[]{:S(2)}, u32[]{:S(2)}) collective-permute-start(bf16[192,3072]{1,0:T(8,128)(2,1)} %collective-permute-done.3), channel_id=1, source_target_pairs={{0,2},{2,0},{4,6},{6,4},{8,10},{10,8},{12,14},{14,12},{16,18},{18,... | collective-permute-start | bytes 3538952 | tf_op jit(solution)/shard_map/ppermute | solution.py:772
  171.2 9.3 %collective-permute-start.5 = (bf16[192,768]{1,0:T(8,128)(2,1)}, bf16[192,768]{1,0:T(8,128)(2,1)}, u32[]{:S(2)}, u32[]{:S(2)}) collective-permute-start(bf16[192,768]{1,0:T(8,128)(2,1)} %collective-permute-done.2), channel_id=1, source_target_pairs={{0,2},{2,0},{4,6},{6,4},{8,10},{10,8},{12,14},{14,12},{16,18},{18,... | collective-permute-start | bytes 884744 | tf_op jit(solution)/shard_map/ppermute | solution.py:772
  175.7 6.5 %copy-start.21 = (bf16[1,384,768]{2,1,0:T(8,128)(2,1)S(1)}, bf16[1,384,768]{2,1,0:T(8,128)(2,1)}, u32[]{:S(2)}) copy-start(bf16[1,384,768]{2,1,0:T(8,128)(2,1)} %param.19) | copy-start | bytes 1769476
  175.7 6.5 %copy-start.34 = (f32[768]{0:T(1024)S(1)}, f32[768]{0:T(1024)}, u32[]{:S(2)}) copy-start(f32[768]{0:T(1024)} %get-tuple-element.147) | copy-start | bytes 9220
  177.9 6.9 %copy-start.9 = (bf16[768,3072]{1,0:T(8,128)(2,1)S(1)}, bf16[768,3072]{1,0:T(8,128)(2,1)}, u32[]{:S(2)}) copy-start(bf16[768,3072]{1,0:T(8,128)(2,1)} %constant_dynamic-update-slice_fusion.4) | copy-start | bytes 14155780
  186.8 13.6 %copy-start.33 = (f32[768]{0:T(1024)S(1)}, f32[768]{0:T(1024)}, u32[]{:S(2)}) copy-start(f32[768]{0:T(1024)} %get-tuple-element.144) | copy-start | bytes 9220
  235.1 23.9 %collective-permute-start.8 = (bf16[2,192,3072]{2,1,0:T(8,128)(2,1)}, bf16[2,192,3072]{2,1,0:T(8,128)(2,1)}, u32[]{:S(2)}, u32[]{:S(2)}) collective-permute-start(bf16[2,192,3072]{2,1,0:T(8,128)(2,1)} %get-tuple-element.165), channel_id=1, source_target_pairs={{0,2},{2,0},{4,6},{6,4},{8,10},{10,8},{12,14},{14,12},{16,18},{18,... | collective-permute-start | bytes 7077896 | tf_op jit(solution)/shard_map/ppermute | solution.py:885
  236.9 22.1 %collective-permute-start.9 = (bf16[2,768,768]{2,1,0:T(8,128)(2,1)}, bf16[2,768,768]{2,1,0:T(8,128)(2,1)}, u32[]{:S(2)}, u32[]{:S(2)}) collective-permute-start(bf16[2,768,768]{2,1,0:T(8,128)(2,1)} %get-tuple-element.163), channel_id=1, source_target_pairs={{0,2},{2,0},{4,6},{6,4},{8,10},{10,8},{12,14},{14,12},{16,18},{18,... | collective-permute-start | bytes 7077896 | tf_op jit(solution)/shard_map/ppermute | solution.py:885
  263.8 70.4 %collective-permute-start.10 = (bf16[192,3072]{1,0:T(8,128)(2,1)}, bf16[192,3072]{1,0:T(8,128)(2,1)S(1)}, u32[]{:S(2)}, u32[]{:S(2)}) collective-permute-start(bf16[192,3072]{1,0:T(8,128)(2,1)} %get-tuple-element.173), channel_id=1, source_target_pairs={{0,1},{1,0},{2,3},{3,2},{4,5},{5,4},{6,7},{7,6},{8,9},{9,8},{10,11... | collective-permute-start | bytes 3538952 | tf_op jit(solution)/shard_map/ppermute | solution.py:890
  267.4 66.8 %collective-permute-start.11 = (bf16[768,768]{1,0:T(8,128)(2,1)S(1)}, bf16[768,768]{1,0:T(8,128)(2,1)S(1)}, u32[]{:S(2)}, u32[]{:S(2)}) collective-permute-start(bf16[768,768]{1,0:T(8,128)(2,1)S(1)} %get-tuple-element.171), channel_id=1, source_target_pairs={{0,1},{1,0},{2,3},{3,2},{4,5},{5,4},{6,7},{7,6},{8,9},{9,8},{10,11... | collective-permute-start | bytes 3538952 | tf_op jit(solution)/shard_map/ppermute | solution.py:890
  334.2 60.1 %copy-start.13 = (bf16[192,3072]{1,0:T(8,128)(2,1)}, bf16[192,3072]{1,0:T(8,128)(2,1)S(1)}, u32[]{:S(2)}) copy-start(bf16[192,3072]{1,0:T(8,128)(2,1)S(1)} %collective-permute-done.10) | copy-start | bytes 3538948
  408.2 6.4 %copy-start.6 = (bf16[192,3072]{1,0:T(8,128)(2,1)S(1)}, bf16[192,3072]{1,0:T(8,128)(2,1)}, u32[]{:S(2)}) copy-start(bf16[192,3072]{1,0:T(8,128)(2,1)} %get-tuple-element.68) | copy-start | bytes 3538948
  408.2 6.4 %copy-start.14 = (bf16[192,3072]{1,0:T(8,128)(2,1)S(1)}, bf16[192,3072]{1,0:T(8,128)(2,1)}, u32[]{:S(2)}) copy-start(bf16[192,3072]{1,0:T(8,128)(2,1)} %copy-done.13) | copy-start | bytes 3538948
  577.1 5.3 copy-start.11
  (28 other events, 65.9 us)

commit v5 on v4

--- a/solution.py
+++ b/solution.py
@@ -213,17 +213,17 @@
     )(send)
 
 
-def project_kernel(x_ref, wq_ref, wkv_ref, bq_ref, bkv_ref, out_ref):
-    rows = x_ref.shape[0]
+def project_kernel(x_ref, pack_ref, bq_ref, bkv_ref, out_ref):
+    rows, width = x_ref.shape
     half = rows // 2
     step = 4
     for base in range(0, HEADS, step):
         cols = slice(base * LANES, (base + step) * LANES)
-        both = (dot_nn(x_ref[...], wkv_ref[:, cols]) + bkv_ref[:, cols]).astype(low_type)
+        both = (dot_nn(x_ref[...], pack_ref[:, width + cols.start : width + cols.stop]) + bkv_ref[:, cols]).astype(low_type)
         for at in range(step):
             out_ref[base + at, 0:rows, :] = both[:, at * LANES : (at + 1) * LANES]
         cols = slice(base * HEAD_DIM, (base + step) * HEAD_DIM)
-        query = ((dot_nn(x_ref[...], wq_ref[:, cols]) + bq_ref[:, cols]) * 0.125).astype(low_type)
+        query = ((dot_nn(x_ref[...], pack_ref[:, cols]) + bq_ref[:, cols]) * 0.125).astype(low_type)
         for at in range(step):
             lanes = slice(at * HEAD_DIM, (at + 1) * HEAD_DIM)
             out_ref[base + at, rows : rows + half, :] = jnp.concatenate(
@@ -231,17 +231,17 @@
             )
 
 
-def project(x, wq, wkv, bq, bkv):
+def project(x, pack, bq, bkv):
     rows = x.shape[0]
     vmem = pl.BlockSpec(memory_space=pltpu.VMEM)
     return pl.pallas_call(
         project_kernel,
         out_shape=jax.ShapeDtypeStruct((HEADS, rows + rows // 2, LANES), low_type),
-        in_specs=[vmem] * 5,
+        in_specs=[vmem] * 4,
         out_specs=vmem,
         compiler_params=pltpu.CompilerParams(vmem_limit_bytes=VMEM_BYTES),
         name="project",
-    )(x, wq, wkv, bq, bkv)
+    )(x, pack, bq, bkv)
 
 
 def tile_range(meta_ref, first, last, total):
@@ -482,10 +482,10 @@
     )(meta, order, recv, qa, ka, va, sums)
 
 
-PART_ORDERS = (("x", "z"), ("z", "x"), ("wa", "x", "z"), ("z", "wa", "x"))
-GATHER_ORDERS = (("z", "x"), ("z", "x"), ("z", "x"), ("z", "x"))
-PARTS = 4
-EARLY = 2
+PART_ORDERS = (("x", "z"), ("x", "z"), ("wa", "x", "z"), ("wa", "x", "z"))
+GATHER_ORDERS = (("z", "x"), ("z", "x"), ("z", "x"), ("x", "z"))
+PARTS = len(PART_ORDERS)
+EARLY = sum(len(order) == 2 for order in PART_ORDERS)
 STAGES = sum(len(order) for order in PART_ORDERS)
 SIZES = {"wa": 2, "x": 2, "z": 4}
 
@@ -597,26 +597,6 @@
             )
         return copies
 
-    flying = {}
-    for part in range(PARTS):
-        if part >= EARLY:
-            core_copies[part].wait()
-            add_into(slab(part, set()), [core_bufs[part]])
-        flying[part] = begin(part, 0)
-    for stage in range(3):
-        for part in range(PARTS):
-            order = PART_ORDERS[part]
-            if stage >= len(order):
-                continue
-            for copy in flying[part]:
-                copy.wait()
-            buf = bufs[first_buf[part] + stage]
-            add_into(
-                slab(part, set(order[: stage + 1])),
-                [buf.at[step] for step in range(SIZES[order[stage]] - 1)],
-            )
-            flying[part] = begin(part, stage + 1) if stage + 1 < len(order) else None
-
     def out_slab(part, held):
         return out_refs[part].at[
             core,
@@ -632,21 +612,42 @@
             for step in range(1, SIZES[axis])
         ]
 
+    def start_gather(part, stage):
+        if stage < 2:
+            return spread(part, stage)
+        block = out_slab(part, set())
+        return [remote(block, block, links.peer("core", 1 - core))]
+
+    flying, passed = {}, {}
     for part in range(PARTS):
-        out_slab(part, {"x", "z"})[...] = slab(part, {"wa", "x", "z"})[0]
-        flying[part] = spread(part, 0)
-    for stage in range(2):
+        passed[part] = 0 if part >= EARLY else 1
+        flying[part] = begin(part, 0) if part < EARLY else [core_copies[part]]
+    while any(flying.values()):
         for part in range(PARTS):
+            if not flying[part]:
+                continue
+            order = PART_ORDERS[part]
             for copy in flying[part]:
                 copy.wait()
-            if stage == 0:
-                flying[part] = spread(part, 1)
+            step = passed[part]
+            passed[part] += 1
+            if step == 0:
+                add_into(slab(part, set()), [core_bufs[part]])
+            elif step <= len(order):
+                buf = bufs[first_buf[part] + step - 1]
+                add_into(
+                    slab(part, set(order[:step])),
+                    [buf.at[at] for at in range(SIZES[order[step - 1]] - 1)],
+                )
+            if step < len(order):
+                flying[part] = begin(part, step)
+            elif step == len(order):
+                out_slab(part, {"x", "z"})[...] = slab(part, {"wa", "x", "z"})[0]
+                flying[part] = start_gather(part, 0)
+            elif step <= len(order) + 2:
+                flying[part] = start_gather(part, step - len(order))
             else:
-                block = out_slab(part, set())
-                flying[part] = [remote(block, block, links.peer("core", 1 - core))]
-    for part in range(PARTS):
-        for copy in flying[part]:
-            copy.wait()
+                flying[part] = None
 
 
 def grad_sum(grads, collective_id):
@@ -681,8 +682,8 @@
         scratch_shapes=[
             *core_bufs,
             *bufs,
-            pltpu.SemaphoreType.DMA((48,)),
-            pltpu.SemaphoreType.DMA((48,)),
+            pltpu.SemaphoreType.DMA((16 * PARTS,)),
+            pltpu.SemaphoreType.DMA((16 * PARTS,)),
         ],
         compiler_params=pltpu.CompilerParams(
             collective_id=collective_id, has_side_effects=True, vmem_limit_bytes=VMEM_BYTES
@@ -695,19 +696,9 @@
     return [part.reshape(-1, part.shape[-1]) for part in sums]
 
 
-def pack_columns(vectors, rows):
-    columns = jnp.stack([vec.astype(low_type) for vec in vectors], axis=1)
-    return jnp.pad(columns, ((0, 0), (0, LANES - len(vectors))))
-
-
 def column_sums(terms, lanes):
     block = jnp.stack([jnp.sum(term, axis=0) for term in terms], axis=1).astype(low_type)
     return jnp.pad(block, ((0, 0), (0, lanes - len(terms))))
-
-
-def rows_of_columns(block, wanted):
-    pick = jnp.eye(LANES, 8, dtype=low_type)
-    return jnp.einsum("fk,kj->jf", block, pick, preferred_element_type=jnp.float32)[:wanted]
 
 
 def reduce_shards(grad):
@@ -783,37 +774,49 @@
         ],
         axis=2,
     ).reshape(shard, 2 * width)
-    vectors = pack_columns(
-        [b_query, b_value, b_out, gain_one, shift_one, gain_two, shift_two, b_down], shard
-    )
-    first_shard = jnp.concatenate([w_query.astype(low_type), pair, vectors], axis=1)
+    own_vectors = jnp.concatenate(
+        [b_query, b_value, b_out, gain_one, shift_one, gain_two, shift_two, b_down, b_up]
+    ).astype(low_type)
+    if direct:
+        other_vectors = lax.ppermute(own_vectors, "wa", [(0, 1), (1, 0)])
+        flat_vectors = jnp.where(
+            wa == 0,
+            jnp.stack([own_vectors, other_vectors]),
+            jnp.stack([other_vectors, own_vectors]),
+        )
+    else:
+        flat_vectors = lax.all_gather(own_vectors, "wa", axis=0)
+    flat_vectors = flat_vectors.astype(jnp.float32)
+
+    def vector(index):
+        return flat_vectors[:, index * shard : (index + 1) * shard].reshape(-1)
+
+    first_shard = jnp.concatenate([w_query.astype(low_type), pair], axis=1)
     fetched = fetch_half(first_shard)
     later_shards = (
         w_out.astype(low_type),
         w_up.astype(low_type),
-        jnp.concatenate([w_down.astype(low_type), pack_columns([b_up], 4 * shard)], axis=1),
+        w_down.astype(low_type),
     )
     later_fetched = tuple(fetch_half(block, fetched) for block in later_shards)
     first_pack = gather_rows(first_shard, fetched)
     query_weight = first_pack[:, :width]
     pair_weight = first_pack[:, width : 3 * width]
-    vector_rows = rows_of_columns(first_pack[:, 3 * width :], 8)
     query_bias, value_bias, out_bias, gain_first, shift_first, gain_second, shift_second, down_bias = (
-        vector_rows[index] for index in range(8)
-    )
+        vector(index) for index in range(8)
+    )
+    up_bias = flat_vectors[:, 8 * shard :].reshape(-1)
     pair_bias = jnp.stack(
         [jnp.zeros((HEADS, HEAD_DIM), jnp.float32), value_bias.reshape(HEADS, HEAD_DIM)], axis=1
     ).reshape(1, 2 * width)
 
-    packed = project(inputs, query_weight, pair_weight, query_bias[None, :], pair_bias)
+    packed = project(inputs, first_pack, query_bias[None, :], pair_bias)
     at_head = to_heads(packed, count, 0)
     context_out, qa, ka, va, sums = attend(meta, block_order, at_head)
     context_out, later_fetched = lax.optimization_barrier((context_out, later_fetched))
-    out_weight, up_weight, down_pack = (
+    out_weight, up_weight, down_weight = (
         gather_rows(block, half_block) for block, half_block in zip(later_shards, later_fetched)
     )
-    down_weight = down_pack[:, :width]
-    up_bias = rows_of_columns(down_pack[:, width:], 1)[0]
     context_in = to_rows(context_out, count, 1)
     context_low = (
         context_in.reshape(HEADS, half, 2, HEAD_DIM).transpose(2, 1, 0, 3).reshape(tok_rows, width)
@@ -913,15 +916,15 @@
         .reshape(tok_rows, width)
         * jnp.asarray(0.125, low_type)
     )
-    d_all = jnp.concatenate([d_queries, d_pair], axis=1)
+    d_all = jnp.concatenate(
+        [d_queries, d_pair, jnp.zeros((tok_rows, lanes), low_type)], axis=1
+    )
     grad_all = jnp.einsum("tc,td->cd", inputs, d_all, preferred_element_type=jnp.float32)
     d_values = d_pair.reshape(tok_rows, HEADS, 2, HEAD_DIM)[:, :, 1, :].reshape(tok_rows, width)
-    last_block = jnp.concatenate(
-        [
-            grad_all.astype(low_type),
-            column_sums([d_queries.astype(jnp.float32), d_values.astype(jnp.float32)], lanes),
-        ],
-        axis=1,
+    last_block = lax.dynamic_update_slice(
+        grad_all.astype(low_type),
+        column_sums([d_queries.astype(jnp.float32), d_values.astype(jnp.float32)], lanes),
+        (0, 3 * width),
     )
     if direct:
         up_sum, down_sum, last_sum, out_sum = grad_sum((*early, last_block, out_block), 4)

time: 593 us -> 609 us (1.027)
  local copies, waits for them, and re-layouts: 78 us -> 104 us
  Pallas kernels: 399 us -> 391 us
  other arithmetic: 44.8 us -> 38 us
  matrix products: 48.8 us -> 55.4 us
    unnamed x83 -> x132, local copies, waits for them, and re-layouts: 14.4 us -> 35 us
    pallas_call x1, Pallas kernels: 142 us -> 129 us  [grad_sum(): pl.pallas_call(grad_sum_kernel, out_shape=tuple(outs), in_specs=[vmem] *...]
    convert_element_type x11 -> x2, other arithmetic: 8.2 us -> 0.94 us  [the longest x1 0.88 us: body(): flat_vectors = flat_vectors.astype(jnp.float32)]
    slice x3 -> x2, local copies, waits for them, and re-layouts: 6.81 us -> 0.62 us  [the longest x1 0.62 us: vector(): return flat_vectors[:, index * shard:(index + 1) * shard].reshape(-1)]
  transfers between devices with their start and end apart: 12 -> 13, of which waited for: 1 -> 0; matrix products, arithmetic and copies ran while one was open for 9% -> 16% of each run, Pallas kernels for 34% -> 34%
where the time goes in v5:
time: 609 us; the launch traced here: 601 us
  Pallas kernels  391 us (64%)
  local copies, waits for them, and re-layouts  104 us (17%)
  matrix products  55.4 us (9%)
  other arithmetic  38 us (6%)
  starting transfers between devices  9.33 us (2%)
    pallas_call x1, Pallas kernels, grad_sum(): pl.pallas_call(grad_sum_kernel, out_shape=tuple(outs), in_specs=[vmem] *...  129 us
    pallas_call x2, Pallas kernels, to_rows(): pl.pallas_call(partial(to_rows_kernel, count), out_shape=jax.ShapeDtypeSt...  82.5 us
    pallas_call x1, Pallas kernels, attend_back(): pl.pallas_call(attend_back_kernel, out_shape=jax.ShapeDtypeStruct((count,...  68.6 us
    pallas_call x2, Pallas kernels, to_heads(): pl.pallas_call(partial(to_heads_kernel, count), out_shape=jax.ShapeDtypeS...  64.7 us
    pallas_call x1, Pallas kernels, attend(): pl.pallas_call(attend_kernel, out_shape=(jax.ShapeDtypeStruct((count, row...  41.8 us
    unnamed x132, local copies, waits for them, and re-layouts  35 us
    dot_general x1, matrix products, body(): jnp.dot(norm_low, up_weight, preferred_element_type=jnp.float32) + up_bias  13.7 us
  transfers between devices with their start and end apart: 13, of which 0 were waited for; matrix products, arithmetic and copies ran while one was open for 16% of the time, Pallas kernels for 34%

profile of v5, /device:TPU:9, one launch (start us, length us, event | category | flops | bytes accessed | tf_op | source)
XLA Modules:
  0.0 600.6 jit_solution(10769443455452325936)
XLA Ops:
  30.8 2.8 constant_dynamic-update-slice_fusion.14
  39.6 4.8 constant_dynamic-update-slice_fusion.11
  71.3 5.0 project.1.send_ref
  76.3 45.6 %to_heads_576.1.recv_ref = bf16[16,576,128]{2,1,0:T(8,128)(2,1)} custom-call(bf16[12,576,128]{2,1,0:T(8,128)(2,1)} %project.1.send_ref), custom_call_target="tpu_custom_call" | custom-call | flops 143999991808 | bytes 3538944 | tf_op jit(solution)/shard_map/to_heads_576/pallas_call | solution.py:122
  121.9 41.8 %attend.1 = (bf16[16,192,128]{2,1,0:T(8,128)(2,1)}, bf16[6144,128]{1,0:T(8,128)(2,1)}, bf16[6144,128]{1,0:T(8,128)(2,1)}, bf16[6144,128]{1,0:T(8,128)(2,1)}, f32[6144,128]{1,0:T(8,128)}) custom-call(s32[4]{0:T(128)} %pad_add_fusion.meta_ref, s32[32]{0:T(128)} %order_ref.3, bf16[16,576,128]{2,1,0:T(8,128)(2,1)} %to_heads_576.1.recv_ref), custom_call_target="tpu_custom_call" | custom-call | flops 38654705664 | bytes 9437184 | tf_op jit(solution)/shard_map/attend/pallas_call | solution.py:335
  164.7 23.5 %to_rows_192.1 = bf16[12,192,128]{2,1,0:T(8,128)(2,1)} custom-call(bf16[16,192,128]{2,1,0:T(8,128)(2,1)} %get-tuple-element.51.send_ref), custom_call_target="tpu_custom_call" | custom-call | flops 48000000000 | bytes 1572864 | tf_op jit(solution)/shard_map/to_rows_192/pallas_call | solution.py:196
  203.6 13.7 %multiply_convert_fusion = (bf16[384,3072]{1,0:T(8,128)(2,1)S(1)}, f32[384,3072]{1,0:T(8,128)S(1)}, f32[384,3072]{1,0:T(8,128)S(1)}) fusion(f32[3072]{0:T(1024)S(1)} %copy-done.32, bf16[768,3072]{1,0:T(8,128)(2,1)} %constant_dynamic-update-slice_fusion.12, f32[384,768]{1,0:T(8,128)S(1)} %get-tuple-element.182, f32[768]{0:T(1024)S(1)} %copy-done.35, ...), kind=kOutput, calls=%fused_computation.8 | convolution fusion | flops 1891270656 | bytes 17716224 | tf_op jit(solution)/shard_map/dot_general | solution.py:829
  218.5 4.5 fusion.49
  225.6 6.5 %fusion.40 = (bf16[3072]{0:T(1024)(128)(2,1)S(1)}, bf16[384,3072]{1,0:T(8,128)(2,1)S(1)}) fusion(f32[384,3072]{1,0:T(8,128)S(1)} %get-tuple-element.155, f32[384,3072]{1,0:T(8,128)S(1)} %get-tuple-element.183, bf16[384,768]{1,0:T(8,128)(2,1)S(1)} %get-tuple-element.145, bf16[3072,768]{1,0:T(8,128)(2,1)} %constant_dynamic-update-slice_fusion.9), kind=kOutput, calls=%fused_computation.147 | convolution fusion | flops 1829630976 | bytes 17111040 | tf_op jit(solution)/shard_map/td,fd->tf/dot_general | solution.py:840
  232.2 4.6 convolution_convert_fusion.1
  236.8 4.8 multiply_reduce_fusion
  241.6 4.7 convolution_convert_fusion.2
  252.6 5.1 dynamic-slice_bitcast_fusion
  263.6 19.0 %to_heads_192.1.recv_ref = bf16[16,192,128]{2,1,0:T(8,128)(2,1)} custom-call(bf16[12,192,128]{2,1,0:T(8,128)(2,1)} %copy.89.send_ref), custom_call_target="tpu_custom_call" | custom-call | flops 48000000000 | bytes 1179648 | tf_op jit(solution)/shard_map/to_heads_192/pallas_call | solution.py:122
  282.7 2.9 add_convert_fusion
  292.4 68.6 %attend_back.1.send_ref = bf16[16,576,128]{2,1,0:T(8,128)(2,1)} custom-call(s32[4]{0:T(128)} %pad_add_fusion.meta_ref, s32[32]{0:T(128)} %order_ref.3, bf16[16,192,128]{2,1,0:T(8,128)(2,1)} %to_heads_192.1.recv_ref, bf16[6144,128]{1,0:T(8,128)(2,1)} %get-tuple-element.59.qa_ref, bf16[6144,128]{1,0:T(8,128)(2,1)} %get-tuple-element.60.ka_ref, ...), custom_call_target="tpu_custom_call" | custom-call | flops 77309411328 | bytes 12582912 | tf_op jit(solution)/shard_map/attend_back/pallas_call | solution.py:464
  362.1 59.0 %to_rows_576.1 = bf16[12,576,128]{2,1,0:T(8,128)(2,1)} custom-call(bf16[16,576,128]{2,1,0:T(8,128)(2,1)} %attend_back.1.send_ref), custom_call_target="tpu_custom_call" | custom-call | flops 143999991808 | bytes 4718592 | tf_op jit(solution)/shard_map/to_rows_576/pallas_call | solution.py:196
  426.2 6.2 %fusion.6 = bf16[768,2560]{1,0:T(8,128)(2,1)S(1)} fusion(bf16[384,1536]{0,1:T(8,128)(2,1)S(1)} %bitcast.120, bf16[384,768]{0,1:T(8,128)(2,1)S(1)} %mul.265, bf16[2560]{0:T(1024)(128)(2,1)S(1)} %copy-done.34, bf16[1,384,768]{2,1,0:T(8,128)(2,1)} %param.19), kind=kOutput, calls=%fused_computation.22 | convolution fusion | flops 1517813760 | bytes 6296576 | tf_op jit(solution)/shard_map/tc,td->cd/dot_general | solution.py:922
  436.9 128.8 %grad_sum.1 = (bf16[2,2,96,3072]{3,2,1,0:T(8,128)(2,1)}, bf16[2,2,384,768]{3,2,1,0:T(8,128)(2,1)}, bf16[2,2,96,2560]{3,2,1,0:T(8,128)(2,1)}, bf16[2,2,96,1024]{3,2,1,0:T(8,128)(2,1)}) custom-call(bf16[1,1,2,96,3072]{4,3,2,1,0:T(8,128)(2,1)} %bitcast.126, bf16[1,1,2,384,768]{4,3,2,1,0:T(8,128)(2,1)} %bitcast.125, bf16[2,2,2,96,2560]{4,3,2,1,0:T(8,128)(2,1)} %bitcast.132, ...), custom_call_target="tpu_custom_call" | custom-call | flops 78643200000 | bytes 15728640 | tf_op jit(solution)/shard_map/grad_sum/pallas_call | solution.py:677
  576.5 3.0 copy.100
  579.6 3.3 fusion.46
  588.1 4.4 bitcast_convert_fusion
  592.5 2.9 bitcast_convert_fusion.1
  597.0 3.3 fusion.20
  (282 shorter events, 129.0 us)
Async XLA Ops:
  4.1 21.7 %copy-start.2 = (bf16[384,1536]{1,0:T(8,128)(2,1)}, bf16[384,1536]{1,0:T(8,128)(2,1)S(1)}, u32[]{:S(2)}) copy-start(bf16[384,1536]{1,0:T(8,128)(2,1)S(1)} %copy.84) | copy-start | bytes 3538948
  4.2 13.9 %copy-start.33 = (f32[1536]{0:T(1024)S(1)}, f32[1536]{0:T(1024)}, u32[]{:S(2)}) copy-start(f32[1536]{0:T(1024)} %param.33) | copy-start | bytes 18436
  4.2 20.6 %copy-start.49 = (s32[1,3]{1,0:T(1,128)S(1)}, s32[1,3]{1,0:T(1,128)}, u32[]{:S(2)}) copy-start(s32[1,3]{1,0:T(1,128)} %param.21) | copy-start | bytes 40
  4.2 20.7 %copy-start.50 = (s32[32]{0:T(128)S(1)}, s32[32]{0:T(128)}, u32[]{:S(2)}) copy-start(s32[32]{0:T(128)} %order_ref.3) | copy-start | bytes 388
  4.3 21.6 %copy-start.6 = (bf16[384,768]{1,0:T(8,128)(2,1)}, bf16[384,768]{1,0:T(8,128)(2,1)S(1)}, u32[]{:S(2)}) copy-start(bf16[384,768]{1,0:T(8,128)(2,1)S(1)} %convert_element_type.174) | copy-start | bytes 1769476
  5.3 54.8 %collective-permute-start = (bf16[192,2304]{1,0:T(8,128)(2,1)}, bf16[192,2304]{1,0:T(8,128)(2,1)}, u32[]{:S(2)}, u32[]{:S(2)}) collective-permute-start(bf16[192,2304]{1,0:T(8,128)(2,1)} %fusion.31), channel_id=1, source_target_pairs={{0,1},{1,0},{2,3},{3,2},{4,5},{5,4},{6,7},{7,6},{8,9},{9,8},{10,11... | collective-permute-start | bytes 2654216 | tf_op jit(solution)/shard_map/ppermute | solution.py:757
  18.7 27.0 %collective-permute-start.2 = (bf16[4608]{0:T(1024)(128)(2,1)}, bf16[4608]{0:T(1024)(128)(2,1)S(1)}, u32[]{:S(2)}, u32[]{:S(2)}) collective-permute-start(bf16[4608]{0:T(1024)(128)(2,1)} %get-tuple-element.158), channel_id=1, source_target_pairs={{0,1},{1,0},{2,3},{3,2},{4,5},{5,4},{6,7},{7,6},{8,9},{9,8},{10,11... | collective-permute-start | bytes 27656 | tf_op jit(solution)/shard_map/ppermute | solution.py:781
  60.1 9.4 %collective-permute-start.1 = (bf16[192,2304]{1,0:T(8,128)(2,1)}, bf16[192,2304]{1,0:T(8,128)(2,1)S(1)}, u32[]{:S(2)}, u32[]{:S(2)}) collective-permute-start(bf16[192,2304]{1,0:T(8,128)(2,1)} %collective-permute-done), channel_id=1, source_target_pairs={{0,2},{2,0},{4,6},{6,4},{8,10},{10,8},{12,14},{14,12},{16,18},{18,... | collective-permute-start | bytes 2654216 | tf_op jit(solution)/shard_map/ppermute | solution.py:763
  63.7 100.1 %collective-permute-start.4 = (bf16[192,3072]{1,0:T(8,128)(2,1)}, bf16[192,3072]{1,0:T(8,128)(2,1)}, u32[]{:S(2)}, u32[]{:S(2)}) collective-permute-start(bf16[192,3072]{1,0:T(8,128)(2,1)} %constant_dynamic-slice_fusion.1), channel_id=1, source_target_pairs={{0,1},{1,0},{2,3},{3,2},{4,5},{5,4},{6,7},{7,6},{8,9},{9,8},{10,11... | collective-permute-start | bytes 3538952 | tf_op jit(solution)/shard_map/ppermute | solution.py:757
  66.0 97.8 %collective-permute-start.5 = (bf16[768,768]{1,0:T(8,128)(2,1)}, bf16[768,768]{1,0:T(8,128)(2,1)}, u32[]{:S(2)}, u32[]{:S(2)}) collective-permute-start(bf16[768,768]{1,0:T(8,128)(2,1)} %constant_dynamic-slice_fusion), channel_id=1, source_target_pairs={{0,1},{1,0},{2,3},{3,2},{4,5},{5,4},{6,7},{7,6},{8,9},{9,8},{10,11... | collective-permute-start | bytes 3538952 | tf_op jit(solution)/shard_map/ppermute | solution.py:757
  67.0 96.8 %collective-permute-start.3 = (bf16[192,768]{1,0:T(8,128)(2,1)}, bf16[192,768]{1,0:T(8,128)(2,1)}, u32[]{:S(2)}, u32[]{:S(2)}) collective-permute-start(bf16[192,768]{1,0:T(8,128)(2,1)} %constant_dynamic-slice_fusion.2), channel_id=1, source_target_pairs={{0,1},{1,0},{2,3},{3,2},{4,5},{5,4},{6,7},{7,6},{8,9},{9,8},{10,11... | collective-permute-start | bytes 884744 | tf_op jit(solution)/shard_map/ppermute | solution.py:757
  163.8 53.6 %collective-permute-start.8 = (bf16[768,768]{1,0:T(8,128)(2,1)}, bf16[768,768]{1,0:T(8,128)(2,1)S(1)}, u32[]{:S(2)}, u32[]{:S(2)}) collective-permute-start(bf16[768,768]{1,0:T(8,128)(2,1)} %collective-permute-done.5), channel_id=1, source_target_pairs={{0,2},{2,0},{4,6},{6,4},{8,10},{10,8},{12,14},{14,12},{16,18},{18,... | collective-permute-start | bytes 3538952 | tf_op jit(solution)/shard_map/ppermute | solution.py:763
  164.6 32.6 %collective-permute-start.6 = (bf16[192,768]{1,0:T(8,128)(2,1)}, bf16[192,768]{1,0:T(8,128)(2,1)}, u32[]{:S(2)}, u32[]{:S(2)}) collective-permute-start(bf16[192,768]{1,0:T(8,128)(2,1)} %collective-permute-done.3), channel_id=1, source_target_pairs={{0,2},{2,0},{4,6},{6,4},{8,10},{10,8},{12,14},{14,12},{16,18},{18,... | collective-permute-start | bytes 884744 | tf_op jit(solution)/shard_map/ppermute | solution.py:763
  188.2 13.1 %collective-permute-start.7 = (bf16[192,3072]{1,0:T(8,128)(2,1)}, bf16[192,3072]{1,0:T(8,128)(2,1)}, u32[]{:S(2)}, u32[]{:S(2)}) collective-permute-start(bf16[192,3072]{1,0:T(8,128)(2,1)} %collective-permute-done.4), channel_id=1, source_target_pairs={{0,2},{2,0},{4,6},{6,4},{8,10},{10,8},{12,14},{14,12},{16,18},{18,... | collective-permute-start | bytes 3538952 | tf_op jit(solution)/shard_map/ppermute | solution.py:763
  192.7 6.2 %copy-start.24 = (bf16[1,384,768]{2,1,0:T(8,128)(2,1)S(1)}, bf16[1,384,768]{2,1,0:T(8,128)(2,1)}, u32[]{:S(2)}) copy-start(bf16[1,384,768]{2,1,0:T(8,128)(2,1)} %param.19) | copy-start | bytes 1769476
  192.7 6.2 %copy-start.37 = (f32[768]{0:T(1024)S(1)}, f32[768]{0:T(1024)}, u32[]{:S(2)}) copy-start(f32[768]{0:T(1024)} %add.209) | copy-start | bytes 9220
  257.7 25.0 %collective-permute-start.10 = (bf16[2,768,768]{2,1,0:T(8,128)(2,1)}, bf16[2,768,768]{2,1,0:T(8,128)(2,1)}, u32[]{:S(2)}, u32[]{:S(2)}) collective-permute-start(bf16[2,768,768]{2,1,0:T(8,128)(2,1)} %get-tuple-element.162), channel_id=1, source_target_pairs={{0,2},{2,0},{4,6},{6,4},{8,10},{10,8},{12,14},{14,12},{16,18},{18,... | collective-permute-start | bytes 7077896 | tf_op jit(solution)/shard_map/ppermute | solution.py:888
  259.5 23.2 %collective-permute-start.9 = (bf16[2,192,3072]{2,1,0:T(8,128)(2,1)}, bf16[2,192,3072]{2,1,0:T(8,128)(2,1)}, u32[]{:S(2)}, u32[]{:S(2)}) collective-permute-start(bf16[2,192,3072]{2,1,0:T(8,128)(2,1)} %get-tuple-element.164), channel_id=1, source_target_pairs={{0,2},{2,0},{4,6},{6,4},{8,10},{10,8},{12,14},{14,12},{16,18},{18,... | collective-permute-start | bytes 7077896 | tf_op jit(solution)/shard_map/ppermute | solution.py:888
  287.2 73.8 %collective-permute-start.12 = (bf16[768,768]{1,0:T(8,128)(2,1)}, bf16[768,768]{1,0:T(8,128)(2,1)S(1)}, u32[]{:S(2)}, u32[]{:S(2)}) collective-permute-start(bf16[768,768]{1,0:T(8,128)(2,1)} %get-tuple-element.168), channel_id=1, source_target_pairs={{0,1},{1,0},{2,3},{3,2},{4,5},{5,4},{6,7},{7,6},{8,9},{9,8},{10,11... | collective-permute-start | bytes 3538952 | tf_op jit(solution)/shard_map/ppermute | solution.py:893
  290.9 70.1 %collective-permute-start.11 = (bf16[192,3072]{1,0:T(8,128)(2,1)S(1)}, bf16[192,3072]{1,0:T(8,128)(2,1)S(1)}, u32[]{:S(2)}, u32[]{:S(2)}) collective-permute-start(bf16[192,3072]{1,0:T(8,128)(2,1)S(1)} %get-tuple-element.170), channel_id=1, source_target_pairs={{0,1},{1,0},{2,3},{3,2},{4,5},{5,4},{6,7},{7,6},{8,9},{9,8},{10,11... | collective-permute-start | bytes 3538952 | tf_op jit(solution)/shard_map/ppermute | solution.py:893
  361.0 60.1 %copy-start.17 = (bf16[768,768]{1,0:T(8,128)(2,1)}, bf16[768,768]{1,0:T(8,128)(2,1)S(1)}, u32[]{:S(2)}) copy-start(bf16[768,768]{1,0:T(8,128)(2,1)S(1)} %collective-permute-done.12) | copy-start | bytes 3538948
  426.2 6.2 %copy-start.15 = (bf16[384,768]{0,1:T(8,128)(2,1)}, bf16[384,768]{0,1:T(8,128)(2,1)S(1)}, u32[]{:S(2)}) copy-start(bf16[384,768]{0,1:T(8,128)(2,1)S(1)} %mul.265) | copy-start | bytes 1769476
  426.2 6.3 %copy-start.8 = (bf16[768,768]{1,0:T(8,128)(2,1)S(1)}, bf16[768,768]{1,0:T(8,128)(2,1)}, u32[]{:S(2)}) copy-start(bf16[768,768]{1,0:T(8,128)(2,1)} %get-tuple-element.70) | copy-start | bytes 3538948
  426.2 6.3 %copy-start.18 = (bf16[768,768]{1,0:T(8,128)(2,1)S(1)}, bf16[768,768]{1,0:T(8,128)(2,1)}, u32[]{:S(2)}) copy-start(bf16[768,768]{1,0:T(8,128)(2,1)} %copy-done.17) | copy-start | bytes 3538948
  (44 other events, 128.5 us)

commit v6 on v5

--- a/solution.py
+++ b/solution.py
@@ -213,17 +213,23 @@
     )(send)
 
 
-def project_kernel(x_ref, pack_ref, bq_ref, bkv_ref, out_ref):
+def project_kernel(x_ref, pack_ref, vec_ref, out_ref):
     rows, width = x_ref.shape
     half = rows // 2
     step = 4
     for base in range(0, HEADS, step):
         cols = slice(base * LANES, (base + step) * LANES)
-        both = (dot_nn(x_ref[...], pack_ref[:, width + cols.start : width + cols.stop]) + bkv_ref[:, cols]).astype(low_type)
+        both = dot_nn(x_ref[...], pack_ref[:, width + cols.start : width + cols.stop])
+        bias = vec_ref[1:2, base * HEAD_DIM : (base + step) * HEAD_DIM]
+        blank = jnp.zeros((1, HEAD_DIM), jnp.float32)
+        shifts = []
+        for at in range(step):
+            shifts += [blank, bias[:, at * HEAD_DIM : (at + 1) * HEAD_DIM]]
+        both = (both + jnp.concatenate(shifts, axis=1)).astype(low_type)
         for at in range(step):
             out_ref[base + at, 0:rows, :] = both[:, at * LANES : (at + 1) * LANES]
         cols = slice(base * HEAD_DIM, (base + step) * HEAD_DIM)
-        query = ((dot_nn(x_ref[...], pack_ref[:, cols]) + bq_ref[:, cols]) * 0.125).astype(low_type)
+        query = ((dot_nn(x_ref[...], pack_ref[:, cols]) + vec_ref[0:1, cols]) * 0.125).astype(low_type)
         for at in range(step):
             lanes = slice(at * HEAD_DIM, (at + 1) * HEAD_DIM)
             out_ref[base + at, rows : rows + half, :] = jnp.concatenate(
@@ -231,17 +237,17 @@
             )
 
 
-def project(x, pack, bq, bkv):
+def project(x, pack, vectors):
     rows = x.shape[0]
     vmem = pl.BlockSpec(memory_space=pltpu.VMEM)
     return pl.pallas_call(
         project_kernel,
         out_shape=jax.ShapeDtypeStruct((HEADS, rows + rows // 2, LANES), low_type),
-        in_specs=[vmem] * 4,
+        in_specs=[vmem] * 3,
         out_specs=vmem,
         compiler_params=pltpu.CompilerParams(vmem_limit_bytes=VMEM_BYTES),
         name="project",
-    )(x, pack, bq, bkv)
+    )(x, pack, vectors)
 
 
 def tile_range(meta_ref, first, last, total):
@@ -775,21 +781,26 @@
         axis=2,
     ).reshape(shard, 2 * width)
     own_vectors = jnp.concatenate(
-        [b_query, b_value, b_out, gain_one, shift_one, gain_two, shift_two, b_down, b_up]
+        [
+            jnp.stack(
+                [b_query, b_value, b_out, gain_one, shift_one, gain_two, shift_two, b_down]
+            ),
+            b_up.reshape(4, shard),
+            jnp.zeros((4, shard), jnp.float32),
+        ],
+        axis=0,
     ).astype(low_type)
     if direct:
         other_vectors = lax.ppermute(own_vectors, "wa", [(0, 1), (1, 0)])
-        flat_vectors = jnp.where(
+        vector_rows = jnp.where(
             wa == 0,
-            jnp.stack([own_vectors, other_vectors]),
-            jnp.stack([other_vectors, own_vectors]),
-        )
+            jnp.concatenate([own_vectors, other_vectors], axis=1),
+            jnp.concatenate([other_vectors, own_vectors], axis=1),
+        ).astype(jnp.float32)
     else:
-        flat_vectors = lax.all_gather(own_vectors, "wa", axis=0)
-    flat_vectors = flat_vectors.astype(jnp.float32)
-
-    def vector(index):
-        return flat_vectors[:, index * shard : (index + 1) * shard].reshape(-1)
+        vector_rows = (
+            lax.all_gather(own_vectors, "wa", axis=1, tiled=True)
+        ).astype(jnp.float32)
 
     first_shard = jnp.concatenate([w_query.astype(low_type), pair], axis=1)
     fetched = fetch_half(first_shard)
@@ -802,15 +813,14 @@
     first_pack = gather_rows(first_shard, fetched)
     query_weight = first_pack[:, :width]
     pair_weight = first_pack[:, width : 3 * width]
-    query_bias, value_bias, out_bias, gain_first, shift_first, gain_second, shift_second, down_bias = (
-        vector(index) for index in range(8)
-    )
-    up_bias = flat_vectors[:, 8 * shard :].reshape(-1)
-    pair_bias = jnp.stack(
-        [jnp.zeros((HEADS, HEAD_DIM), jnp.float32), value_bias.reshape(HEADS, HEAD_DIM)], axis=1
-    ).reshape(1, 2 * width)
-
-    packed = project(inputs, first_pack, query_bias[None, :], pair_bias)
+    out_bias, gain_first, shift_first, gain_second, shift_second, down_bias = (
+        vector_rows[index] for index in range(2, 8)
+    )
+    up_bias = (
+        vector_rows[8:12].reshape(4, width // shard, shard).transpose(1, 0, 2).reshape(-1)
+    )
+
+    packed = project(inputs, first_pack, vector_rows)
     at_head = to_heads(packed, count, 0)
     context_out, qa, ka, va, sums = attend(meta, block_order, at_head)
     context_out, later_fetched = lax.optimization_barrier((context_out, later_fetched))
@@ -916,11 +926,14 @@
         .reshape(tok_rows, width)
         * jnp.asarray(0.125, low_type)
     )
+    d_keys, d_values = (
+        grads_in[:, :tok_rows, low : low + HEAD_DIM].transpose(1, 0, 2).reshape(tok_rows, width)
+        for low in (0, HEAD_DIM)
+    )
     d_all = jnp.concatenate(
-        [d_queries, d_pair, jnp.zeros((tok_rows, lanes), low_type)], axis=1
+        [d_queries, d_keys, d_values, jnp.zeros((tok_rows, lanes), low_type)], axis=1
     )
     grad_all = jnp.einsum("tc,td->cd", inputs, d_all, preferred_element_type=jnp.float32)
-    d_values = d_pair.reshape(tok_rows, HEADS, 2, HEAD_DIM)[:, :, 1, :].reshape(tok_rows, width)
     last_block = lax.dynamic_update_slice(
         grad_all.astype(low_type),
         column_sums([d_queries.astype(jnp.float32), d_values.astype(jnp.float32)], lanes),
@@ -940,15 +953,14 @@
     input_grad = d_input.astype(low_type)[None]
 
     wide_grad = last_sum.astype(jnp.float32)
-    pair_grad = wide_grad[:, width : 3 * width].reshape(shard, HEADS, 2, HEAD_DIM)
     out_grad = out_sum.astype(jnp.float32)
     return (
         activations,
         input_grad,
         wide_grad[:, :width],
         wide_grad[:, 3 * width],
-        pair_grad[:, :, 0, :].reshape(shard, width),
-        pair_grad[:, :, 1, :].reshape(shard, width),
+        wide_grad[:, width : 2 * width],
+        wide_grad[:, 2 * width : 3 * width],
         wide_grad[:, 3 * width + 1],
         out_grad[:, :width],
         out_grad[:, width],

time: 609 us -> 563 us (0.924)
  local copies, waits for them, and re-layouts: 104 us -> 66.9 us
  matrix products: 55.4 us -> 44.5 us
    unnamed x132, local copies, waits for them, and re-layouts: 35 us -> 11.7 us
  transfers between devices with their start and end apart: 13 -> 13, of which waited for: 0 -> 1; matrix products, arithmetic and copies ran while one was open for 16% -> 10% of each run, Pallas kernels for 34% -> 37%
where the time goes in v6:
time: 563 us; the launch traced here: 556 us
  Pallas kernels  392 us (70%)
  local copies, waits for them, and re-layouts  66.9 us (12%)
  matrix products  44.5 us (8%)
  other arithmetic  37.1 us (7%)
  starting transfers between devices  9.68 us (2%)
    pallas_call x1, Pallas kernels, grad_sum(): pl.pallas_call(grad_sum_kernel, out_shape=tuple(outs), in_specs=[vmem] *...  129 us
    pallas_call x2, Pallas kernels, to_rows(): pl.pallas_call(partial(to_rows_kernel, count), out_shape=jax.ShapeDtypeSt...  82.3 us
    pallas_call x1, Pallas kernels, attend_back(): pl.pallas_call(attend_back_kernel, out_shape=jax.ShapeDtypeStruct((count,...  69 us
    pallas_call x2, Pallas kernels, to_heads(): pl.pallas_call(partial(to_heads_kernel, count), out_shape=jax.ShapeDtypeS...  64.6 us
    pallas_call x1, Pallas kernels, attend(): pl.pallas_call(attend_kernel, out_shape=(jax.ShapeDtypeStruct((count, row...  41.9 us
    dot_general x1, matrix products, body(): jnp.dot(norm_low, up_weight, preferred_element_type=jnp.float32) + up_bias  14.6 us
    unnamed x132, local copies, waits for them, and re-layouts  11.7 us
  transfers between devices with their start and end apart: 13, of which 1 were waited for; matrix products, arithmetic and copies ran while one was open for 10% of the time, Pallas kernels for 37%

profile of v6, /device:TPU:9, one launch (start us, length us, event | category | flops | bytes accessed | tf_op | source)
XLA Modules:
  0.0 556.3 jit_solution(6286505245741000276)
XLA Ops:
  9.5 4.6 constant_dynamic-update-slice_fusion.5
  23.2 3.2 collective-permute-done.2
  41.6 5.0 project.1.send_ref
  46.5 45.6 %to_heads_576.1.recv_ref = bf16[16,576,128]{2,1,0:T(8,128)(2,1)} custom-call(bf16[12,576,128]{2,1,0:T(8,128)(2,1)} %project.1.send_ref), custom_call_target="tpu_custom_call" | custom-call | flops 143999991808 | bytes 3538944 | tf_op jit(solution)/shard_map/to_heads_576/pallas_call | solution.py:122
  92.1 41.9 %attend.1 = (bf16[16,192,128]{2,1,0:T(8,128)(2,1)}, bf16[6144,128]{1,0:T(8,128)(2,1)}, bf16[6144,128]{1,0:T(8,128)(2,1)}, bf16[6144,128]{1,0:T(8,128)(2,1)}, f32[6144,128]{1,0:T(8,128)}) custom-call(s32[4]{0:T(128)} %pad_add_fusion.meta_ref, s32[32]{0:T(128)} %order_ref.3, bf16[16,576,128]{2,1,0:T(8,128)(2,1)} %to_heads_576.1.recv_ref), custom_call_target="tpu_custom_call" | custom-call | flops 38654705664 | bytes 9437184 | tf_op jit(solution)/shard_map/attend/pallas_call | solution.py:341
  134.9 23.4 %to_rows_192.1 = bf16[12,192,128]{2,1,0:T(8,128)(2,1)} custom-call(bf16[16,192,128]{2,1,0:T(8,128)(2,1)} %get-tuple-element.51.send_ref), custom_call_target="tpu_custom_call" | custom-call | flops 48000000000 | bytes 1572864 | tf_op jit(solution)/shard_map/to_rows_192/pallas_call | solution.py:196
  165.0 2.5 constant_dynamic-update-slice_fusion.1
  170.3 14.6 %multiply_convert_fusion = (bf16[384,3072]{1,0:T(8,128)(2,1)S(1)}, f32[384,3072]{1,0:T(8,128)}, f32[384,3072]{1,0:T(8,128)}) fusion(f32[3072]{0:T(1024)S(1)} %copy-done.40, bf16[768,3072]{1,0:T(8,128)(2,1)S(1)} %constant_dynamic-update-slice_fusion.3, f32[384,768]{1,0:T(8,128)S(1)} %get-tuple-element.130, f32[768]{0:T(1024)S(1)} %copy-done.43, ...), kind=kOutput, calls=%fused_computation.8 | convolution fusion | flops 1891270656 | bytes 17716224 | tf_op jit(solution)/shard_map/dot_general | solution.py:839
  191.1 5.8 %fusion.43 = (bf16[3072]{0:T(1024)(128)(2,1)S(1)}, bf16[384,3072]{1,0:T(8,128)(2,1)S(1)}) fusion(f32[384,3072]{1,0:T(8,128)} %get-tuple-element.110, f32[384,3072]{1,0:T(8,128)} %get-tuple-element.131, bf16[384,768]{1,0:T(8,128)(2,1)S(1)} %get-tuple-element.100, bf16[3072,768]{1,0:T(8,128)(2,1)S(1)} %constant_dynamic-update-slice_fusion), kind=kOutput, calls=%fused_computation.146 | convolution fusion | flops 1829630976 | bytes 17111040 | tf_op jit(solution)/shard_map/td,fd->tf/dot_general | solution.py:850
  197.0 4.8 convolution_convert_fusion.1
  204.2 4.3 convolution_convert_fusion.2
  213.5 5.1 dynamic-slice_bitcast_fusion
  221.9 2.6 copy.93
  224.5 19.0 %to_heads_192.1.recv_ref = bf16[16,192,128]{2,1,0:T(8,128)(2,1)} custom-call(bf16[12,192,128]{2,1,0:T(8,128)(2,1)} %copy.86.send_ref), custom_call_target="tpu_custom_call" | custom-call | flops 48000000000 | bytes 1179648 | tf_op jit(solution)/shard_map/to_heads_192/pallas_call | solution.py:122
  243.6 2.9 add_convert_fusion
  248.3 2.5 add_convert_fusion.1
  253.3 69.0 %attend_back.1.send_ref = bf16[16,576,128]{2,1,0:T(8,128)(2,1)} custom-call(s32[4]{0:T(128)} %pad_add_fusion.meta_ref, s32[32]{0:T(128)} %order_ref.3, bf16[16,192,128]{2,1,0:T(8,128)(2,1)} %to_heads_192.1.recv_ref, bf16[6144,128]{1,0:T(8,128)(2,1)} %get-tuple-element.59.qa_ref, bf16[6144,128]{1,0:T(8,128)(2,1)} %get-tuple-element.60.ka_ref, ...), custom_call_target="tpu_custom_call" | custom-call | flops 77309411328 | bytes 12582912 | tf_op jit(solution)/shard_map/attend_back/pallas_call | solution.py:470
  323.4 58.8 %to_rows_576.1 = bf16[12,576,128]{2,1,0:T(8,128)(2,1)} custom-call(bf16[16,576,128]{2,1,0:T(8,128)(2,1)} %attend_back.1.send_ref), custom_call_target="tpu_custom_call" | custom-call | flops 143999991808 | bytes 4718592 | tf_op jit(solution)/shard_map/to_rows_576/pallas_call | solution.py:196
  395.6 4.1 fusion.6
  404.2 129.3 %grad_sum.1 = (bf16[2,2,96,3072]{3,2,1,0:T(8,128)(2,1)}, bf16[2,2,384,768]{3,2,1,0:T(8,128)(2,1)}, bf16[2,2,96,2560]{3,2,1,0:T(8,128)(2,1)}, bf16[2,2,96,1024]{3,2,1,0:T(8,128)(2,1)}) custom-call(bf16[1,1,2,96,3072]{4,3,2,1,0:T(8,128)(2,1)} %bitcast.127, bf16[1,1,2,384,768]{4,3,2,1,0:T(8,128)(2,1)} %bitcast.126, bf16[2,2,2,96,2560]{4,3,2,1,0:T(8,128)(2,1)} %bitcast.136, ...), custom_call_target="tpu_custom_call" | custom-call | flops 78643200000 | bytes 15728640 | tf_op jit(solution)/shard_map/grad_sum/pallas_call | solution.py:683
  542.3 2.7 bitcast_convert_fusion
  545.0 2.9 bitcast_convert_fusion.1
  549.6 2.4 copy.89
  552.0 2.5 fusion.8
  (284 shorter events, 93.9 us)
Async XLA Ops:
  4.1 5.4 copy-start.3
  4.3 5.2 copy-start.8
  5.3 24.8 %collective-permute-start = (bf16[192,2304]{1,0:T(8,128)(2,1)}, bf16[192,2304]{1,0:T(8,128)(2,1)}, u32[]{:S(2)}, u32[]{:S(2)}) collective-permute-start(bf16[192,2304]{1,0:T(8,128)(2,1)} %fusion.33), channel_id=1, source_target_pairs={{0,1},{1,0},{2,3},{3,2},{4,5},{5,4},{6,7},{7,6},{8,9},{9,8},{10,11... | collective-permute-start | bytes 2654216 | tf_op jit(solution)/shard_map/ppermute | solution.py:763
  6.9 19.5 %collective-permute-start.2 = (bf16[16,384]{1,0:T(8,128)(2,1)S(1)}, bf16[16,384]{1,0:T(8,128)(2,1)}, u32[]{:S(2)}, u32[]{:S(2)}) collective-permute-start(bf16[16,384]{1,0:T(8,128)(2,1)S(1)} %concatenate.28), channel_id=1, source_target_pairs={{0,1},{1,0},{2,3},{3,2},{4,5},{5,4},{6,7},{7,6},{8,9},{9,8},{10,11... | collective-permute-start | bytes 36872 | tf_op jit(solution)/shard_map/ppermute | solution.py:794
  8.9 8.4 %slice-start = ((s8[4718592]{0:T(1024)(128)(4,1)}), s8[4194304]{0:T(1024)(128)(4,1)S(1)}, s32[]{:S(2)}) async-start(s8[4718592]{0:T(1024)(128)(4,1)} %bitcast.108), calls=%async_computation | async-start | bytes 8388608
  9.5 7.8 %slice-start.1 = ((s8[4718592]{0:T(1024)(128)(4,1)}), s8[524288]{0:T(1024)(128)(4,1)S(1)}, s32[]{:S(2)}) async-start(s8[4718592]{0:T(1024)(128)(4,1)} %bitcast.108), calls=%async_computation.1 | async-start | bytes 1048576
  28.4 6.8 %copy-start.7 = (bf16[1536,768]{1,0:T(8,128)(2,1)S(1)}, bf16[1536,768]{1,0:T(8,128)(2,1)}, u32[]{:S(2)}) copy-start(bf16[1536,768]{1,0:T(8,128)(2,1)} %get-tuple-element.50) | copy-start | bytes 7077892
  30.0 6.5 %copy-start.19 = (bf16[384,768]{1,0:T(8,128)(2,1)S(1)}, bf16[384,768]{1,0:T(8,128)(2,1)}, u32[]{:S(2)}) copy-start(bf16[384,768]{1,0:T(8,128)(2,1)} %get-tuple-element.48) | copy-start | bytes 1769476
  30.0 9.7 %collective-permute-start.1 = (bf16[192,2304]{1,0:T(8,128)(2,1)}, bf16[192,2304]{1,0:T(8,128)(2,1)S(1)}, u32[]{:S(2)}, u32[]{:S(2)}) collective-permute-start(bf16[192,2304]{1,0:T(8,128)(2,1)} %collective-permute-done), channel_id=1, source_target_pairs={{0,2},{2,0},{4,6},{6,4},{8,10},{10,8},{12,14},{14,12},{16,18},{18,... | collective-permute-start | bytes 2654216 | tf_op jit(solution)/shard_map/ppermute | solution.py:769
  33.9 100.1 %collective-permute-start.4 = (bf16[192,3072]{1,0:T(8,128)(2,1)}, bf16[192,3072]{1,0:T(8,128)(2,1)}, u32[]{:S(2)}, u32[]{:S(2)}) collective-permute-start(bf16[192,3072]{1,0:T(8,128)(2,1)} %constant_dynamic-slice_fusion.1), channel_id=1, source_target_pairs={{0,1},{1,0},{2,3},{3,2},{4,5},{5,4},{6,7},{7,6},{8,9},{9,8},{10,11... | collective-permute-start | bytes 3538952 | tf_op jit(solution)/shard_map/ppermute | solution.py:763
  36.3 97.7 %collective-permute-start.5 = (bf16[768,768]{1,0:T(8,128)(2,1)}, bf16[768,768]{1,0:T(8,128)(2,1)}, u32[]{:S(2)}, u32[]{:S(2)}) collective-permute-start(bf16[768,768]{1,0:T(8,128)(2,1)} %constant_dynamic-slice_fusion), channel_id=1, source_target_pairs={{0,1},{1,0},{2,3},{3,2},{4,5},{5,4},{6,7},{7,6},{8,9},{9,8},{10,11... | collective-permute-start | bytes 3538952 | tf_op jit(solution)/shard_map/ppermute | solution.py:763
  37.2 96.8 %collective-permute-start.3 = (bf16[192,768]{1,0:T(8,128)(2,1)}, bf16[192,768]{1,0:T(8,128)(2,1)}, u32[]{:S(2)}, u32[]{:S(2)}) collective-permute-start(bf16[192,768]{1,0:T(8,128)(2,1)} %constant_dynamic-slice_fusion.2), channel_id=1, source_target_pairs={{0,1},{1,0},{2,3},{3,2},{4,5},{5,4},{6,7},{7,6},{8,9},{9,8},{10,11... | collective-permute-start | bytes 884744 | tf_op jit(solution)/shard_map/ppermute | solution.py:763
  134.0 50.9 %collective-permute-start.8 = (bf16[768,768]{1,0:T(8,128)(2,1)}, bf16[768,768]{1,0:T(8,128)(2,1)}, u32[]{:S(2)}, u32[]{:S(2)}) collective-permute-start(bf16[768,768]{1,0:T(8,128)(2,1)} %collective-permute-done.5), channel_id=1, source_target_pairs={{0,2},{2,0},{4,6},{6,4},{8,10},{10,8},{12,14},{14,12},{16,18},{18,... | collective-permute-start | bytes 3538952 | tf_op jit(solution)/shard_map/ppermute | solution.py:769
  134.8 32.7 %collective-permute-start.6 = (bf16[192,768]{1,0:T(8,128)(2,1)}, bf16[192,768]{1,0:T(8,128)(2,1)S(1)}, u32[]{:S(2)}, u32[]{:S(2)}) collective-permute-start(bf16[192,768]{1,0:T(8,128)(2,1)} %collective-permute-done.3), channel_id=1, source_target_pairs={{0,2},{2,0},{4,6},{6,4},{8,10},{10,8},{12,14},{14,12},{16,18},{18,... | collective-permute-start | bytes 884744 | tf_op jit(solution)/shard_map/ppermute | solution.py:769
  158.4 10.3 %collective-permute-start.7 = (bf16[192,3072]{1,0:T(8,128)(2,1)}, bf16[192,3072]{1,0:T(8,128)(2,1)}, u32[]{:S(2)}, u32[]{:S(2)}) collective-permute-start(bf16[192,3072]{1,0:T(8,128)(2,1)} %collective-permute-done.4), channel_id=1, source_target_pairs={{0,2},{2,0},{4,6},{6,4},{8,10},{10,8},{12,14},{14,12},{16,18},{18,... | collective-permute-start | bytes 3538952 | tf_op jit(solution)/shard_map/ppermute | solution.py:769
  162.1 6.6 %slice-start.6 = ((s8[4718592]{0:T(1024)(128)(4,1)}), s8[524288]{0:T(1024)(128)(4,1)S(1)}, s32[]{:S(2)}) async-start(s8[4718592]{0:T(1024)(128)(4,1)} %bitcast.116), calls=%async_computation.6 | async-start | bytes 1048576
  168.7 16.2 %slice-start.4 = ((s8[4718592]{0:T(1024)(128)(4,1)}), s8[4194304]{0:T(1024)(128)(4,1)S(1)}, s32[]{:S(2)}) async-start(s8[4718592]{0:T(1024)(128)(4,1)} %bitcast.114), calls=%async_computation.4 | async-start | bytes 8388608
  170.3 14.6 %slice-start.5 = ((s8[4718592]{0:T(1024)(128)(4,1)}), s8[524288]{0:T(1024)(128)(4,1)S(1)}, s32[]{:S(2)}) async-start(s8[4718592]{0:T(1024)(128)(4,1)} %bitcast.114), calls=%async_computation.5 | async-start | bytes 1048576
  218.6 25.0 %collective-permute-start.10 = (bf16[2,768,768]{2,1,0:T(8,128)(2,1)}, bf16[2,768,768]{2,1,0:T(8,128)(2,1)}, u32[]{:S(2)}, u32[]{:S(2)}) collective-permute-start(bf16[2,768,768]{2,1,0:T(8,128)(2,1)} %get-tuple-element.115), channel_id=1, source_target_pairs={{0,2},{2,0},{4,6},{6,4},{8,10},{10,8},{12,14},{14,12},{16,18},{18,... | collective-permute-start | bytes 7077896 | tf_op jit(solution)/shard_map/ppermute | solution.py:898
  220.4 23.2 %collective-permute-start.9 = (bf16[2,192,3072]{2,1,0:T(8,128)(2,1)}, bf16[2,192,3072]{2,1,0:T(8,128)(2,1)}, u32[]{:S(2)}, u32[]{:S(2)}) collective-permute-start(bf16[2,192,3072]{2,1,0:T(8,128)(2,1)} %get-tuple-element.117), channel_id=1, source_target_pairs={{0,2},{2,0},{4,6},{6,4},{8,10},{10,8},{12,14},{14,12},{16,18},{18,... | collective-permute-start | bytes 7077896 | tf_op jit(solution)/shard_map/ppermute | solution.py:898
  248.1 74.2 %collective-permute-start.12 = (bf16[768,768]{1,0:T(8,128)(2,1)}, bf16[768,768]{1,0:T(8,128)(2,1)S(1)}, u32[]{:S(2)}, u32[]{:S(2)}) collective-permute-start(bf16[768,768]{1,0:T(8,128)(2,1)} %get-tuple-element.122), channel_id=1, source_target_pairs={{0,1},{1,0},{2,3},{3,2},{4,5},{5,4},{6,7},{7,6},{8,9},{9,8},{10,11... | collective-permute-start | bytes 3538952 | tf_op jit(solution)/shard_map/ppermute | solution.py:903
  252.0 70.3 %collective-permute-start.11 = (bf16[192,3072]{1,0:T(8,128)(2,1)S(1)}, bf16[192,3072]{1,0:T(8,128)(2,1)S(1)}, u32[]{:S(2)}, u32[]{:S(2)}) collective-permute-start(bf16[192,3072]{1,0:T(8,128)(2,1)S(1)} %get-tuple-element.124), channel_id=1, source_target_pairs={{0,1},{1,0},{2,3},{3,2},{4,5},{5,4},{6,7},{7,6},{8,9},{9,8},{10,11... | collective-permute-start | bytes 3538952 | tf_op jit(solution)/shard_map/ppermute | solution.py:903
  322.3 59.9 %copy-start.20 = (bf16[768,768]{1,0:T(8,128)(2,1)}, bf16[768,768]{1,0:T(8,128)(2,1)S(1)}, u32[]{:S(2)}) copy-start(bf16[768,768]{1,0:T(8,128)(2,1)S(1)} %collective-permute-done.12) | copy-start | bytes 3538948
  545.0 7.0 %copy-start.2 = (bf16[768,2304]{1,0:T(8,128)(2,1)S(1)}, bf16[768,2304]{1,0:T(8,128)(2,1)}, u32[]{:S(2)}) copy-start(bf16[768,2304]{1,0:T(8,128)(2,1)} %copy-done.1) | copy-start | bytes 10616836
  (54 other events, 148.3 us)

commit v7 on v6

--- a/solution.py
+++ b/solution.py
@@ -41,6 +41,9 @@
 
 
 def owner_of(head, count):
+    if count == 16:
+        line, place = head // 3, head % 3
+        return 4 * line + place + (line % 2) * ((place + 1) // 2)
     return head * count // HEADS
 
 
@@ -703,8 +706,13 @@
 
 
 def column_sums(terms, lanes):
-    block = jnp.stack([jnp.sum(term, axis=0) for term in terms], axis=1).astype(low_type)
-    return jnp.pad(block, ((0, 0), (0, lanes - len(terms))))
+    total = 0.0
+    for index, term in enumerate(terms):
+        place = lax.broadcasted_iota(jnp.int32, (term.shape[0], lanes), 1) == index
+        total = total + jnp.einsum(
+            "td,tk->dk", term, place.astype(low_type), preferred_element_type=jnp.float32
+        )
+    return total.astype(low_type)
 
 
 def reduce_shards(grad):
@@ -747,7 +755,7 @@
     own_blocks = lax.dynamic_slice(block_order, (2 * me,), (2,))
     position = (own_blocks[:, None] * half + jnp.arange(half, dtype=jnp.int32)[None, :]).reshape(-1)
     own_seg = segment_of(position, seq_ends)
-    owns = jnp.any(me == jnp.arange(HEADS, dtype=jnp.int32) * count // HEADS).astype(jnp.int32)
+    owns = jnp.any(me == owner_of(jnp.arange(HEADS, dtype=jnp.int32), count)).astype(jnp.int32)
     meta = jnp.concatenate([seq_ends.astype(jnp.int32), owns[None]])
 
     core = me % 2
@@ -756,10 +764,11 @@
     def fetch_half(shard_block, after=None):
         if not direct:
             return None
-        if after is not None:
-            shard_block, _ = lax.optimization_barrier((shard_block, after))
         size, columns = shard_block.shape
         part = lax.dynamic_slice(shard_block, (core * (size // 2), 0), (size // 2, columns))
+        if after is not None:
+            part = lax.optimization_barrier(part)
+            part, _ = lax.optimization_barrier((part, after))
         return lax.ppermute(part, "wa", [(0, 1), (1, 0)])
 
     def gather_rows(shard_block, fetched):
@@ -936,7 +945,7 @@
     grad_all = jnp.einsum("tc,td->cd", inputs, d_all, preferred_element_type=jnp.float32)
     last_block = lax.dynamic_update_slice(
         grad_all.astype(low_type),
-        column_sums([d_queries.astype(jnp.float32), d_values.astype(jnp.float32)], lanes),
+        column_sums([d_queries, d_values], lanes),
         (0, 3 * width),
     )
     if direct:

time: 563 us -> 561 us (level)
  Pallas kernels: 392 us -> 298 us
  waiting for transfers between devices: 3.25 us -> 41.9 us
  starting transfers between devices: 9.68 us -> 45.2 us
  local copies, waits for them, and re-layouts: 66.9 us -> 78.5 us
    pallas_call x1, Pallas kernels: 69 us -> 4.97 us  [attend_back(): pl.pallas_call(attend_back_kernel, out_shape=jax.ShapeDtypeStruct((count,...]
    ppermute x2, waiting for transfers between devices: 0.01 us -> 41.9 us  [wa_halves(): return (keep, lax.ppermute(give, 'wa', [(0, 1), (1, 0)]))]
    pallas_call x1, Pallas kernels: 41.9 us -> 5.19 us  [attend(): pl.pallas_call(attend_kernel, out_shape=(jax.ShapeDtypeStruct((count, row...]
    ppermute x4, starting transfers between devices: 3.48 us -> 39 us  [gather_rows(): swapped = lax.ppermute(fetched, 'ctx', [(k, k ^ 1) for k in range(count)])]
    unnamed x132 -> x124, local copies, waits for them, and re-layouts: 11.7 us -> 12.6 us
  transfers between devices with their start and end apart: 13 -> 13, of which waited for: 1 -> 2; matrix products, arithmetic and copies ran while one was open for 10% -> 11% of each run, Pallas kernels for 37% -> 18%
where the time goes in v7:
time: 561 us; the launch traced here: 553 us
  Pallas kernels  298 us (53%)
  local copies, waits for them, and re-layouts  78.5 us (14%)
  matrix products  49.7 us (9%)
  starting transfers between devices  45.2 us (8%)
  waiting for transfers between devices  41.9 us (7%)
  other arithmetic  36.8 us (7%)
    pallas_call x1, Pallas kernels, grad_sum(): pl.pallas_call(grad_sum_kernel, out_shape=tuple(outs), in_specs=[vmem] *...  133 us
    pallas_call x2, Pallas kernels, to_rows(): pl.pallas_call(partial(to_rows_kernel, count), out_shape=jax.ShapeDtypeSt...  85.6 us
    pallas_call x2, Pallas kernels, to_heads(): pl.pallas_call(partial(to_heads_kernel, count), out_shape=jax.ShapeDtypeS...  65 us
    ppermute x2, waiting for transfers between devices, wa_halves(): return (keep, lax.ppermute(give, 'wa', [(0, 1), (1, 0)]))  41.9 us
    ppermute x4, starting transfers between devices, gather_rows(): swapped = lax.ppermute(fetched, 'ctx', [(k, k ^ 1) for k in range(count)])  39 us
    unnamed x124, local copies, waits for them, and re-layouts  12.6 us
    dot_general x1, matrix products, body(): jnp.dot(norm_low, up_weight, preferred_element_type=jnp.float32) + up_bias  11.9 us
  transfers between devices with their start and end apart: 13, of which 2 were waited for; matrix products, arithmetic and copies ran while one was open for 11% of the time, Pallas kernels for 18%

profile of v7, /device:TPU:9, one launch (start us, length us, event | category | flops | bytes accessed | tf_op | source)
XLA Modules:
  0.0 553.3 jit_solution(1236062273372353933)
XLA Ops:
  23.8 4.8 constant_dynamic-update-slice_fusion.2
  45.9 5.0 project.1.send_ref
  50.8 45.0 %to_heads_576.1.recv_ref = bf16[16,576,128]{2,1,0:T(8,128)(2,1)} custom-call(bf16[12,576,128]{2,1,0:T(8,128)(2,1)} %project.1.send_ref), custom_call_target="tpu_custom_call" | custom-call | flops 143999991808 | bytes 3538944 | tf_op jit(solution)/shard_map/to_heads_576/pallas_call | solution.py:125
  95.9 5.2 attend.1
  101.1 37.5 %collective-permute-start.8 = (bf16[768,768]{1,0:T(8,128)(2,1)}, bf16[768,768]{1,0:T(8,128)(2,1)}, u32[]{:S(2)}, u32[]{:S(2)}) collective-permute-start(bf16[768,768]{1,0:T(8,128)(2,1)} %collective-permute-done.5), channel_id=1, source_target_pairs={{0,2},{2,0},{4,6},{6,4},{8,10},{10,8},{12,14},{14,12},{16,18},{18,... | collective-permute-start | bytes 3538952 | tf_op jit(solution)/shard_map/ppermute | solution.py:778
  138.7 19.0 %to_rows_192.1 = bf16[12,192,128]{2,1,0:T(8,128)(2,1)} custom-call(bf16[16,192,128]{2,1,0:T(8,128)(2,1)} %get-tuple-element.51.send_ref), custom_call_target="tpu_custom_call" | custom-call | flops 48000000000 | bytes 1572864 | tf_op jit(solution)/shard_map/to_rows_192/pallas_call | solution.py:199
  170.6 11.9 %multiply_convert_fusion = (bf16[384,3072]{1,0:T(8,128)(2,1)S(1)}, f32[384,3072]{1,0:T(8,128)S(1)}, f32[384,3072]{1,0:T(8,128)S(1)}) fusion(f32[3072]{0:T(1024)S(1)} %copy-done.35, bf16[768,3072]{1,0:T(8,128)(2,1)S(1)} %constant_dynamic-update-slice_fusion.3, f32[384,768]{1,0:T(8,128)S(1)} %get-tuple-element.130, f32[768]{0:T(1024)S(1)} %copy-done.38, ...), kind=kOutput, calls=%fused_computation.8 | convolution fusion | flops 1891270656 | bytes 17716224 | tf_op jit(solution)/shard_map/dot_general | solution.py:848
  184.9 4.5 fusion.58
  192.0 6.3 %fusion.50 = (bf16[3072]{0:T(1024)(128)(2,1)S(1)}, bf16[384,3072]{1,0:T(8,128)(2,1)S(1)}) fusion(f32[384,3072]{1,0:T(8,128)S(1)} %get-tuple-element.110, f32[384,3072]{1,0:T(8,128)S(1)} %get-tuple-element.131, bf16[384,768]{1,0:T(8,128)(2,1)S(1)} %get-tuple-element.100, bf16[3072,768]{1,0:T(8,128)(2,1)} %constant_dynamic-update-slice_fusion), kind=kOutput, calls=%fused_computation.164 | convolution fusion | flops 1829630976 | bytes 17111040 | tf_op jit(solution)/shard_map/td,fd->tf/dot_general | solution.py:859
  198.3 4.6 convolution_convert_fusion.1
  205.3 4.5 convolution_convert_fusion.2
  216.1 5.1 dynamic-slice_bitcast_fusion
  227.1 20.0 %to_heads_192.1.recv_ref = bf16[16,192,128]{2,1,0:T(8,128)(2,1)} custom-call(bf16[12,192,128]{2,1,0:T(8,128)(2,1)} %copy.66.send_ref), custom_call_target="tpu_custom_call" | custom-call | flops 48000000000 | bytes 1179648 | tf_op jit(solution)/shard_map/to_heads_192/pallas_call | solution.py:125
  247.1 2.9 add_convert_fusion
  256.8 5.0 attend_back.1.send_ref
  261.8 16.6 %collective-permute-done.12 = bf16[768,768]{1,0:T(8,128)(2,1)S(1)} collective-permute-done((bf16[768,768]{1,0:T(8,128)(2,1)}, bf16[768,768]{1,0:T(8,128)(2,1)S(1)}, u32[]{:S(2)}, u32[]{:S(2)}) %collective-permute-start.12) | collective-permute-done | bytes 1179680 | tf_op jit(solution)/shard_map/ppermute | solution.py:912
  278.4 25.3 %collective-permute-done.11 = bf16[192,3072]{1,0:T(8,128)(2,1)S(1)} collective-permute-done((bf16[192,3072]{1,0:T(8,128)(2,1)S(1)}, bf16[192,3072]{1,0:T(8,128)(2,1)S(1)}, u32[]{:S(2)}, u32[]{:S(2)}) %collective-permute-start.11) | collective-permute-done | bytes 1179680 | tf_op jit(solution)/shard_map/ppermute | solution.py:912
  304.7 66.6 %to_rows_576.1 = bf16[12,576,128]{2,1,0:T(8,128)(2,1)} custom-call(bf16[16,576,128]{2,1,0:T(8,128)(2,1)} %attend_back.1.send_ref), custom_call_target="tpu_custom_call" | custom-call | flops 143999991808 | bytes 4718592 | tf_op jit(solution)/shard_map/to_rows_576/pallas_call | solution.py:199
  371.3 3.2 slice_bitcast_fusion.1
  379.2 2.9 copy.68
  385.0 3.0 add_convert_fusion.3
  389.5 5.9 %fusion.6 = bf16[768,2560]{1,0:T(8,128)(2,1)S(1)} fusion(bf16[384,768]{0,1:T(8,128)(2,1)S(1)} %bitcast.121, bf16[384,768]{0,1:T(8,128)(2,1)S(1)} %bitcast.130, bf16[384,768]{0,1:T(8,128)(2,1)S(1)} %mul.266, bf16[2560]{0:T(1024)(128)(2,1)S(1)} %copy-done.37, bf16[1,384,768]{2,1,0:T(8,128)(2,1)S(1)} %copy-done.25), kind=kOutput, calls=%fused_computation.22 | convolution fusion | flops 1519779840 | bytes 6296576 | tf_op jit(solution)/shard_map/tc,td->cd/dot_general | solution.py:945
  397.8 132.6 %grad_sum.1 = (bf16[2,2,96,3072]{3,2,1,0:T(8,128)(2,1)}, bf16[2,2,384,768]{3,2,1,0:T(8,128)(2,1)}, bf16[2,2,96,2560]{3,2,1,0:T(8,128)(2,1)}, bf16[2,2,96,1024]{3,2,1,0:T(8,128)(2,1)}) custom-call(bf16[1,1,2,96,3072]{4,3,2,1,0:T(8,128)(2,1)} %bitcast.127, bf16[1,1,2,384,768]{4,3,2,1,0:T(8,128)(2,1)} %bitcast.126, bf16[2,2,2,96,2560]{4,3,2,1,0:T(8,128)(2,1)} %bitcast.135, ...), custom_call_target="tpu_custom_call" | custom-call | flops 78643200000 | bytes 15728640 | tf_op jit(solution)/shard_map/grad_sum/pallas_call | solution.py:686
  541.7 2.9 bitcast_convert_fusion.1
  (270 shorter events, 110.2 us)
Async XLA Ops:
  5.2 23.4 %collective-permute-start = (bf16[192,2304]{1,0:T(8,128)(2,1)}, bf16[192,2304]{1,0:T(8,128)(2,1)}, u32[]{:S(2)}, u32[]{:S(2)}) collective-permute-start(bf16[192,2304]{1,0:T(8,128)(2,1)} %fusion.35), channel_id=1, source_target_pairs={{0,1},{1,0},{2,3},{3,2},{4,5},{5,4},{6,7},{7,6},{8,9},{9,8},{10,11... | collective-permute-start | bytes 2654216 | tf_op jit(solution)/shard_map/ppermute | solution.py:772
  6.8 28.4 %collective-permute-start.2 = (bf16[16,384]{1,0:T(8,128)(2,1)S(1)}, bf16[16,384]{1,0:T(8,128)(2,1)}, u32[]{:S(2)}, u32[]{:S(2)}) collective-permute-start(bf16[16,384]{1,0:T(8,128)(2,1)S(1)} %concatenate.28), channel_id=1, source_target_pairs={{0,1},{1,0},{2,3},{3,2},{4,5},{5,4},{6,7},{7,6},{8,9},{9,8},{10,11... | collective-permute-start | bytes 36872 | tf_op jit(solution)/shard_map/ppermute | solution.py:803
  28.6 5.4 copy-start.50
  28.6 14.2 %collective-permute-start.1 = (bf16[192,2304]{1,0:T(8,128)(2,1)}, bf16[192,2304]{1,0:T(8,128)(2,1)}, u32[]{:S(2)}, u32[]{:S(2)}) collective-permute-start(bf16[192,2304]{1,0:T(8,128)(2,1)} %collective-permute-done), channel_id=1, source_target_pairs={{0,2},{2,0},{4,6},{6,4},{8,10},{10,8},{12,14},{14,12},{16,18},{18,... | collective-permute-start | bytes 2654216 | tf_op jit(solution)/shard_map/ppermute | solution.py:778
  38.9 62.2 %collective-permute-start.4 = (bf16[192,3072]{1,0:T(8,128)(2,1)}, bf16[192,3072]{1,0:T(8,128)(2,1)}, u32[]{:S(2)}, u32[]{:S(2)}) collective-permute-start(bf16[192,3072]{1,0:T(8,128)(2,1)} %constant_dynamic-slice_fusion.1), channel_id=1, source_target_pairs={{0,1},{1,0},{2,3},{3,2},{4,5},{5,4},{6,7},{7,6},{8,9},{9,8},{10,11... | collective-permute-start | bytes 3538952 | tf_op jit(solution)/shard_map/ppermute | solution.py:772
  40.1 60.9 %collective-permute-start.5 = (bf16[768,768]{1,0:T(8,128)(2,1)}, bf16[768,768]{1,0:T(8,128)(2,1)}, u32[]{:S(2)}, u32[]{:S(2)}) collective-permute-start(bf16[768,768]{1,0:T(8,128)(2,1)} %constant_dynamic-slice_fusion), channel_id=1, source_target_pairs={{0,1},{1,0},{2,3},{3,2},{4,5},{5,4},{6,7},{7,6},{8,9},{9,8},{10,11... | collective-permute-start | bytes 3538952 | tf_op jit(solution)/shard_map/ppermute | solution.py:772
  40.4 60.7 %collective-permute-start.3 = (bf16[192,768]{1,0:T(8,128)(2,1)}, bf16[192,768]{1,0:T(8,128)(2,1)}, u32[]{:S(2)}, u32[]{:S(2)}) collective-permute-start(bf16[192,768]{1,0:T(8,128)(2,1)} %constant_dynamic-slice_fusion.2), channel_id=1, source_target_pairs={{0,1},{1,0},{2,3},{3,2},{4,5},{5,4},{6,7},{7,6},{8,9},{9,8},{10,11... | collective-permute-start | bytes 884744 | tf_op jit(solution)/shard_map/ppermute | solution.py:772
  101.1 81.4 %collective-permute-start.8 = (bf16[768,768]{1,0:T(8,128)(2,1)}, bf16[768,768]{1,0:T(8,128)(2,1)}, u32[]{:S(2)}, u32[]{:S(2)}) collective-permute-start(bf16[768,768]{1,0:T(8,128)(2,1)} %collective-permute-done.5), channel_id=1, source_target_pairs={{0,2},{2,0},{4,6},{6,4},{8,10},{10,8},{12,14},{14,12},{16,18},{18,... | collective-permute-start | bytes 3538952 | tf_op jit(solution)/shard_map/ppermute | solution.py:778
  138.6 27.5 %collective-permute-start.6 = (bf16[192,768]{1,0:T(8,128)(2,1)}, bf16[192,768]{1,0:T(8,128)(2,1)S(1)}, u32[]{:S(2)}, u32[]{:S(2)}) collective-permute-start(bf16[192,768]{1,0:T(8,128)(2,1)} %collective-permute-done.3), channel_id=1, source_target_pairs={{0,2},{2,0},{4,6},{6,4},{8,10},{10,8},{12,14},{14,12},{16,18},{18,... | collective-permute-start | bytes 884744 | tf_op jit(solution)/shard_map/ppermute | solution.py:778
  157.7 11.4 %collective-permute-start.7 = (bf16[192,3072]{1,0:T(8,128)(2,1)}, bf16[192,3072]{1,0:T(8,128)(2,1)}, u32[]{:S(2)}, u32[]{:S(2)}) collective-permute-start(bf16[192,3072]{1,0:T(8,128)(2,1)} %collective-permute-done.4), channel_id=1, source_target_pairs={{0,2},{2,0},{4,6},{6,4},{8,10},{10,8},{12,14},{14,12},{16,18},{18,... | collective-permute-start | bytes 3538952 | tf_op jit(solution)/shard_map/ppermute | solution.py:778
  160.6 8.6 %slice-start.4 = ((s8[4718592]{0:T(1024)(128)(4,1)}), s8[524288]{0:T(1024)(128)(4,1)S(1)}, s32[]{:S(2)}) async-start(s8[4718592]{0:T(1024)(128)(4,1)} %bitcast.114), calls=%async_computation.4 | async-start | bytes 1048576
  161.4 5.4 copy-start.24
  163.5 5.6 %slice-start.5 = ((s8[4718592]{0:T(1024)(128)(4,1)}), s8[4194304]{0:T(1024)(128)(4,1)S(1)}, s32[]{:S(2)}) async-start(s8[4718592]{0:T(1024)(128)(4,1)} %bitcast.114), calls=%async_computation.5 | async-start | bytes 8388608
  216.1 5.4 slice-start.2
  216.1 5.4 slice-start.3
  221.2 25.9 %collective-permute-start.10 = (bf16[2,768,768]{2,1,0:T(8,128)(2,1)}, bf16[2,768,768]{2,1,0:T(8,128)(2,1)}, u32[]{:S(2)}, u32[]{:S(2)}) collective-permute-start(bf16[2,768,768]{2,1,0:T(8,128)(2,1)} %get-tuple-element.115), channel_id=1, source_target_pairs={{0,2},{2,0},{4,6},{6,4},{8,10},{10,8},{12,14},{14,12},{16,18},{18,... | collective-permute-start | bytes 7077896 | tf_op jit(solution)/shard_map/ppermute | solution.py:907
  223.3 23.8 %collective-permute-start.9 = (bf16[2,192,3072]{2,1,0:T(8,128)(2,1)}, bf16[2,192,3072]{2,1,0:T(8,128)(2,1)}, u32[]{:S(2)}, u32[]{:S(2)}) collective-permute-start(bf16[2,192,3072]{2,1,0:T(8,128)(2,1)} %get-tuple-element.117), channel_id=1, source_target_pairs={{0,2},{2,0},{4,6},{6,4},{8,10},{10,8},{12,14},{14,12},{16,18},{18,... | collective-permute-start | bytes 7077896 | tf_op jit(solution)/shard_map/ppermute | solution.py:907
  251.6 26.8 %collective-permute-start.12 = (bf16[768,768]{1,0:T(8,128)(2,1)}, bf16[768,768]{1,0:T(8,128)(2,1)S(1)}, u32[]{:S(2)}, u32[]{:S(2)}) collective-permute-start(bf16[768,768]{1,0:T(8,128)(2,1)} %get-tuple-element.122), channel_id=1, source_target_pairs={{0,1},{1,0},{2,3},{3,2},{4,5},{5,4},{6,7},{7,6},{8,9},{9,8},{10,11... | collective-permute-start | bytes 3538952 | tf_op jit(solution)/shard_map/ppermute | solution.py:912
  255.4 48.3 %collective-permute-start.11 = (bf16[192,3072]{1,0:T(8,128)(2,1)S(1)}, bf16[192,3072]{1,0:T(8,128)(2,1)S(1)}, u32[]{:S(2)}, u32[]{:S(2)}) collective-permute-start(bf16[192,3072]{1,0:T(8,128)(2,1)S(1)} %get-tuple-element.124), channel_id=1, source_target_pairs={{0,1},{1,0},{2,3},{3,2},{4,5},{5,4},{6,7},{7,6},{8,9},{9,8},{10,11... | collective-permute-start | bytes 3538952 | tf_op jit(solution)/shard_map/ppermute | solution.py:912
  278.4 25.3 %copy-start.18 = (bf16[768,768]{1,0:T(8,128)(2,1)}, bf16[768,768]{1,0:T(8,128)(2,1)S(1)}, u32[]{:S(2)}) copy-start(bf16[768,768]{1,0:T(8,128)(2,1)S(1)} %collective-permute-done.12) | copy-start | bytes 3538948
  378.1 6.5 %copy-start.49 = (pred[256]{0:T(512)(128)(4,1)S(1)}, pred[256]{0:T(512)(128)(4,1)}, u32[]{:S(2)}) copy-start(pred[256]{0:T(512)(128)(4,1)} %iota_compare_fusion.2) | copy-start | bytes 772
  379.2 5.7 %copy-start.11 = (bf16[768,768]{1,0:T(8,128)(2,1)S(1)}, bf16[768,768]{1,0:T(8,128)(2,1)}, u32[]{:S(2)}) copy-start(bf16[768,768]{1,0:T(8,128)(2,1)} %get-tuple-element.70) | copy-start | bytes 3538948
  389.5 5.9 %copy-start.51 = (pred[256]{0:T(512)(128)(4,1)S(1)}, pred[256]{0:T(512)(128)(4,1)}, u32[]{:S(2)}) copy-start(pred[256]{0:T(512)(128)(4,1)} %iota_compare_fusion.1) | copy-start | bytes 772
  541.7 6.9 %copy-start.1 = (bf16[768,2304]{1,0:T(8,128)(2,1)S(1)}, bf16[768,2304]{1,0:T(8,128)(2,1)}, u32[]{:S(2)}) copy-start(bf16[768,2304]{1,0:T(8,128)(2,1)} %copy-done) | copy-start | bytes 10616836
  (50 other events, 124.4 us)

commit v8 on v6

--- a/solution.py
+++ b/solution.py
@@ -250,7 +250,7 @@
     )(x, pack, vectors)
 
 
-def tile_range(meta_ref, first, last, total):
+def tile_range(meta_ref, first, last, total, step):
     end_a, end_b, end_c = meta_ref[0], meta_ref[1], meta_ref[2]
     low = jnp.where(
         first >= end_c, end_c, jnp.where(first >= end_b, end_b, jnp.where(first >= end_a, end_a, 0))
@@ -260,7 +260,7 @@
         total,
         jnp.where(last >= end_b, end_c, jnp.where(last >= end_a, end_b, end_a)),
     )
-    return low // TILE, (high + TILE - 1) // TILE
+    return low // step, (high + step - 1) // step
 
 
 def attend_kernel(meta_ref, order_ref, recv_ref, out_ref, qa_ref, ka_ref, va_ref, sum_ref):
@@ -303,14 +303,17 @@
         def query_step(index, _):
             first = pl.multiple_of(index * TILE, TILE)
             rows = pl.ds(first, TILE)
-            begin, end = tile_range(meta_ref, first, first + TILE - 1, total)
+            begin, end = tile_range(meta_ref, first, first + TILE - 1, total, 2 * TILE)
             query = qa_ref[rows, :]
             sum_ref[rows, :] = jnp.zeros((TILE, LANES), jnp.float32)
 
             def key_step(key_index, _):
-                keys = pl.ds(pl.multiple_of(key_index * TILE, TILE), TILE)
-                expo = jnp.exp(dot_nt(query, ka_ref[keys, :])).astype(low_type)
-                sum_ref[rows, :] += dot_nn(expo, va_ref[keys, :])
+                gained = 0.0
+                for part in range(2):
+                    keys = pl.ds(pl.multiple_of((2 * key_index + part) * TILE, TILE), TILE)
+                    expo = jnp.exp(dot_nt(query, ka_ref[keys, :])).astype(low_type)
+                    gained = gained + dot_nn(expo, va_ref[keys, :])
+                sum_ref[rows, :] += gained
                 return 0
 
             lax.fori_loop(begin, end, key_step, 0)
@@ -426,7 +429,7 @@
         def query_step(index, _):
             first = pl.multiple_of(index * TILE, TILE)
             rows = pl.ds(first, TILE)
-            begin, end = tile_range(meta_ref, first, first + TILE - 1, total)
+            begin, end = tile_range(meta_ref, first, first + TILE - 1, total, TILE)
             query = qb_ref[rows, :]
             given = da_ref[rows, :]
             query_only = jnp.where(lower_tile, query.astype(jnp.float32), 0.0).astype(low_type)
@@ -893,13 +896,13 @@
 
     def core_halves(block):
         view = block.reshape(2, 2, -1, block.shape[1])
-        keep = lax.dynamic_index_in_dim(view, core, 1, keepdims=False)
-        give = lax.dynamic_index_in_dim(view, 1 - core, 1, keepdims=False)
+        keep = jnp.where(core == 0, view[:, 0], view[:, 1])
+        give = jnp.where(core == 0, view[:, 1], view[:, 0])
         return keep, lax.ppermute(give, "ctx", [(k, k ^ 1) for k in range(count)])
 
     def wa_halves(block):
-        keep = lax.dynamic_index_in_dim(block, wa, 0, keepdims=False)
-        give = lax.dynamic_index_in_dim(block, 1 - wa, 0, keepdims=False)
+        keep = jnp.where(wa == 0, block[0], block[1])
+        give = jnp.where(wa == 0, block[1], block[0])
         return keep, lax.ppermute(give, "wa", [(0, 1), (1, 0)])
 
     context_back, down_block, out_block, up_block = lax.optimization_barrier(

time: 563 us -> 559 us (level)
  local copies, waits for them, and re-layouts: 66.9 us -> 57.4 us
  other arithmetic: 37.1 us -> 46.6 us
    squeeze x4 -> x0, local copies, waits for them, and re-layouts: 9.52 us -> none  [the longest x2 6.79 us: core_halves(): give = lax.dynamic_index_in_dim(view, 1 - core, 1, keepdims=False)]
    select_n x0 -> x4, other arithmetic: none -> 9.51 us  [the longest x2 6.78 us: core_halves(): give = jnp.where(core == 0, view[:, 1], view[:, 0])]
  transfers between devices with their start and end apart: 13 -> 13, of which waited for: 1 -> 1; matrix products, arithmetic and copies ran while one was open for 10% -> 10% of each run, Pallas kernels for 37% -> 36%
where the time goes in v8:
time: 559 us; the launch traced here: 553 us
  Pallas kernels  388 us (69%)
  local copies, waits for them, and re-layouts  57.4 us (10%)
  other arithmetic  46.6 us (8%)
  matrix products  44.5 us (8%)
  starting transfers between devices  9.68 us (2%)
    pallas_call x1, Pallas kernels, grad_sum(): pl.pallas_call(grad_sum_kernel, out_shape=tuple(outs), in_specs=[vmem] *...  129 us
    pallas_call x2, Pallas kernels, to_rows(): pl.pallas_call(partial(to_rows_kernel, count), out_shape=jax.ShapeDtypeSt...  82.2 us
    pallas_call x1, Pallas kernels, attend_back(): pl.pallas_call(attend_back_kernel, out_shape=jax.ShapeDtypeStruct((count,...  69 us
    pallas_call x2, Pallas kernels, to_heads(): pl.pallas_call(partial(to_heads_kernel, count), out_shape=jax.ShapeDtypeS...  64.6 us
    pallas_call x1, Pallas kernels, attend(): pl.pallas_call(attend_kernel, out_shape=(jax.ShapeDtypeStruct((count, row...  38.4 us
    dot_general x1, matrix products, body(): jnp.dot(norm_low, up_weight, preferred_element_type=jnp.float32) + up_bias  14.6 us
    unnamed x132, local copies, waits for them, and re-layouts  11.7 us
  transfers between devices with their start and end apart: 13, of which 1 were waited for; matrix products, arithmetic and copies ran while one was open for 10% of the time, Pallas kernels for 36%

profile of v8, /device:TPU:9, one launch (start us, length us, event | category | flops | bytes accessed | tf_op | source)
XLA Modules:
  0.0 552.7 jit_solution(7441919610637475619)
XLA Ops:
  9.5 4.6 constant_dynamic-update-slice_fusion.5
  23.2 3.2 collective-permute-done.2
  41.6 5.0 project.1.send_ref
  46.5 45.6 %to_heads_576.1.recv_ref = bf16[16,576,128]{2,1,0:T(8,128)(2,1)} custom-call(bf16[12,576,128]{2,1,0:T(8,128)(2,1)} %project.1.send_ref), custom_call_target="tpu_custom_call" | custom-call | flops 143999991808 | bytes 3538944 | tf_op jit(solution)/shard_map/to_heads_576/pallas_call | solution.py:122
  92.1 38.4 %attend.1 = (bf16[16,192,128]{2,1,0:T(8,128)(2,1)}, bf16[6144,128]{1,0:T(8,128)(2,1)}, bf16[6144,128]{1,0:T(8,128)(2,1)}, bf16[6144,128]{1,0:T(8,128)(2,1)}, f32[6144,128]{1,0:T(8,128)}) custom-call(s32[4]{0:T(128)} %pad_add_fusion.meta_ref, s32[32]{0:T(128)} %order_ref.3, bf16[16,576,128]{2,1,0:T(8,128)(2,1)} %to_heads_576.1.recv_ref), custom_call_target="tpu_custom_call" | custom-call | flops 38654705664 | bytes 9437184 | tf_op jit(solution)/shard_map/attend/pallas_call | solution.py:344
  131.4 23.4 %to_rows_192.1 = bf16[12,192,128]{2,1,0:T(8,128)(2,1)} custom-call(bf16[16,192,128]{2,1,0:T(8,128)(2,1)} %get-tuple-element.51.send_ref), custom_call_target="tpu_custom_call" | custom-call | flops 48000000000 | bytes 1572864 | tf_op jit(solution)/shard_map/to_rows_192/pallas_call | solution.py:196
  161.5 2.5 constant_dynamic-update-slice_fusion.1
  166.8 14.6 %multiply_convert_fusion = (bf16[384,3072]{1,0:T(8,128)(2,1)S(1)}, f32[384,3072]{1,0:T(8,128)}, f32[384,3072]{1,0:T(8,128)}) fusion(f32[3072]{0:T(1024)S(1)} %copy-done.40, bf16[768,3072]{1,0:T(8,128)(2,1)S(1)} %constant_dynamic-update-slice_fusion.3, f32[384,768]{1,0:T(8,128)S(1)} %get-tuple-element.130, f32[768]{0:T(1024)S(1)} %copy-done.43, ...), kind=kOutput, calls=%fused_computation.8 | convolution fusion | flops 1891270656 | bytes 17716224 | tf_op jit(solution)/shard_map/dot_general | solution.py:842
  187.6 5.8 %fusion.43 = (bf16[3072]{0:T(1024)(128)(2,1)S(1)}, bf16[384,3072]{1,0:T(8,128)(2,1)S(1)}) fusion(f32[384,3072]{1,0:T(8,128)} %get-tuple-element.110, f32[384,3072]{1,0:T(8,128)} %get-tuple-element.131, bf16[384,768]{1,0:T(8,128)(2,1)S(1)} %get-tuple-element.100, bf16[3072,768]{1,0:T(8,128)(2,1)S(1)} %constant_dynamic-update-slice_fusion), kind=kOutput, calls=%fused_computation.150 | convolution fusion | flops 1829630976 | bytes 17111040 | tf_op jit(solution)/shard_map/td,fd->tf/dot_general | solution.py:853
  193.5 4.8 convolution_convert_fusion.1
  200.7 4.3 convolution_convert_fusion.2
  210.0 5.1 select_bitcast_fusion
  218.4 2.6 copy.109
  221.0 19.0 %to_heads_192.1.recv_ref = bf16[16,192,128]{2,1,0:T(8,128)(2,1)} custom-call(bf16[12,192,128]{2,1,0:T(8,128)(2,1)} %copy.98.send_ref), custom_call_target="tpu_custom_call" | custom-call | flops 48000000000 | bytes 1179648 | tf_op jit(solution)/shard_map/to_heads_192/pallas_call | solution.py:122
  240.1 2.9 add_convert_fusion
  244.8 2.5 add_convert_fusion.1
  249.8 69.0 %attend_back.1.send_ref = bf16[16,576,128]{2,1,0:T(8,128)(2,1)} custom-call(s32[4]{0:T(128)} %pad_add_fusion.meta_ref, s32[32]{0:T(128)} %order_ref.3, bf16[16,192,128]{2,1,0:T(8,128)(2,1)} %to_heads_192.1.recv_ref, bf16[6144,128]{1,0:T(8,128)(2,1)} %get-tuple-element.59.qa_ref, bf16[6144,128]{1,0:T(8,128)(2,1)} %get-tuple-element.60.ka_ref, ...), custom_call_target="tpu_custom_call" | custom-call | flops 77309411328 | bytes 12582912 | tf_op jit(solution)/shard_map/attend_back/pallas_call | solution.py:473
  319.9 58.8 %to_rows_576.1 = bf16[12,576,128]{2,1,0:T(8,128)(2,1)} custom-call(bf16[16,576,128]{2,1,0:T(8,128)(2,1)} %attend_back.1.send_ref), custom_call_target="tpu_custom_call" | custom-call | flops 143999991808 | bytes 4718592 | tf_op jit(solution)/shard_map/to_rows_576/pallas_call | solution.py:196
  392.1 4.1 fusion.6
  400.7 129.2 %grad_sum.1 = (bf16[2,2,96,3072]{3,2,1,0:T(8,128)(2,1)}, bf16[2,2,384,768]{3,2,1,0:T(8,128)(2,1)}, bf16[2,2,96,2560]{3,2,1,0:T(8,128)(2,1)}, bf16[2,2,96,1024]{3,2,1,0:T(8,128)(2,1)}) custom-call(bf16[1,1,2,96,3072]{4,3,2,1,0:T(8,128)(2,1)} %bitcast.151, bf16[1,1,2,384,768]{4,3,2,1,0:T(8,128)(2,1)} %bitcast.150, bf16[2,2,2,96,2560]{4,3,2,1,0:T(8,128)(2,1)} %bitcast.160, ...), custom_call_target="tpu_custom_call" | custom-call | flops 78643200000 | bytes 15728640 | tf_op jit(solution)/shard_map/grad_sum/pallas_call | solution.py:686
  538.7 2.7 bitcast_convert_fusion
  541.4 2.9 bitcast_convert_fusion.1
  545.9 2.4 copy.105
  548.3 2.5 fusion.8
  (284 shorter events, 93.8 us)
Async XLA Ops:
  4.1 5.4 copy-start.3
  4.3 5.2 copy-start.8
  5.3 24.8 %collective-permute-start = (bf16[192,2304]{1,0:T(8,128)(2,1)}, bf16[192,2304]{1,0:T(8,128)(2,1)}, u32[]{:S(2)}, u32[]{:S(2)}) collective-permute-start(bf16[192,2304]{1,0:T(8,128)(2,1)} %fusion.33), channel_id=1, source_target_pairs={{0,1},{1,0},{2,3},{3,2},{4,5},{5,4},{6,7},{7,6},{8,9},{9,8},{10,11... | collective-permute-start | bytes 2654216 | tf_op jit(solution)/shard_map/ppermute | solution.py:766
  6.9 19.5 %collective-permute-start.2 = (bf16[16,384]{1,0:T(8,128)(2,1)S(1)}, bf16[16,384]{1,0:T(8,128)(2,1)}, u32[]{:S(2)}, u32[]{:S(2)}) collective-permute-start(bf16[16,384]{1,0:T(8,128)(2,1)S(1)} %concatenate.28), channel_id=1, source_target_pairs={{0,1},{1,0},{2,3},{3,2},{4,5},{5,4},{6,7},{7,6},{8,9},{9,8},{10,11... | collective-permute-start | bytes 36872 | tf_op jit(solution)/shard_map/ppermute | solution.py:797
  8.9 8.4 %slice-start = ((s8[4718592]{0:T(1024)(128)(4,1)}), s8[4194304]{0:T(1024)(128)(4,1)S(1)}, s32[]{:S(2)}) async-start(s8[4718592]{0:T(1024)(128)(4,1)} %bitcast.132), calls=%async_computation | async-start | bytes 8388608
  9.5 7.8 %slice-start.1 = ((s8[4718592]{0:T(1024)(128)(4,1)}), s8[524288]{0:T(1024)(128)(4,1)S(1)}, s32[]{:S(2)}) async-start(s8[4718592]{0:T(1024)(128)(4,1)} %bitcast.132), calls=%async_computation.1 | async-start | bytes 1048576
  28.4 6.8 %copy-start.7 = (bf16[1536,768]{1,0:T(8,128)(2,1)S(1)}, bf16[1536,768]{1,0:T(8,128)(2,1)}, u32[]{:S(2)}) copy-start(bf16[1536,768]{1,0:T(8,128)(2,1)} %get-tuple-element.50) | copy-start | bytes 7077892
  30.0 6.5 %copy-start.19 = (bf16[384,768]{1,0:T(8,128)(2,1)S(1)}, bf16[384,768]{1,0:T(8,128)(2,1)}, u32[]{:S(2)}) copy-start(bf16[384,768]{1,0:T(8,128)(2,1)} %get-tuple-element.48) | copy-start | bytes 1769476
  30.0 9.7 %collective-permute-start.1 = (bf16[192,2304]{1,0:T(8,128)(2,1)}, bf16[192,2304]{1,0:T(8,128)(2,1)S(1)}, u32[]{:S(2)}, u32[]{:S(2)}) collective-permute-start(bf16[192,2304]{1,0:T(8,128)(2,1)} %collective-permute-done), channel_id=1, source_target_pairs={{0,2},{2,0},{4,6},{6,4},{8,10},{10,8},{12,14},{14,12},{16,18},{18,... | collective-permute-start | bytes 2654216 | tf_op jit(solution)/shard_map/ppermute | solution.py:772
  33.9 96.6 %collective-permute-start.4 = (bf16[192,3072]{1,0:T(8,128)(2,1)}, bf16[192,3072]{1,0:T(8,128)(2,1)}, u32[]{:S(2)}, u32[]{:S(2)}) collective-permute-start(bf16[192,3072]{1,0:T(8,128)(2,1)} %constant_dynamic-slice_fusion.1), channel_id=1, source_target_pairs={{0,1},{1,0},{2,3},{3,2},{4,5},{5,4},{6,7},{7,6},{8,9},{9,8},{10,11... | collective-permute-start | bytes 3538952 | tf_op jit(solution)/shard_map/ppermute | solution.py:766
  36.3 94.2 %collective-permute-start.5 = (bf16[768,768]{1,0:T(8,128)(2,1)}, bf16[768,768]{1,0:T(8,128)(2,1)}, u32[]{:S(2)}, u32[]{:S(2)}) collective-permute-start(bf16[768,768]{1,0:T(8,128)(2,1)} %constant_dynamic-slice_fusion), channel_id=1, source_target_pairs={{0,1},{1,0},{2,3},{3,2},{4,5},{5,4},{6,7},{7,6},{8,9},{9,8},{10,11... | collective-permute-start | bytes 3538952 | tf_op jit(solution)/shard_map/ppermute | solution.py:766
  37.2 93.3 %collective-permute-start.3 = (bf16[192,768]{1,0:T(8,128)(2,1)}, bf16[192,768]{1,0:T(8,128)(2,1)}, u32[]{:S(2)}, u32[]{:S(2)}) collective-permute-start(bf16[192,768]{1,0:T(8,128)(2,1)} %constant_dynamic-slice_fusion.2), channel_id=1, source_target_pairs={{0,1},{1,0},{2,3},{3,2},{4,5},{5,4},{6,7},{7,6},{8,9},{9,8},{10,11... | collective-permute-start | bytes 884744 | tf_op jit(solution)/shard_map/ppermute | solution.py:766
  130.5 50.9 %collective-permute-start.8 = (bf16[768,768]{1,0:T(8,128)(2,1)}, bf16[768,768]{1,0:T(8,128)(2,1)}, u32[]{:S(2)}, u32[]{:S(2)}) collective-permute-start(bf16[768,768]{1,0:T(8,128)(2,1)} %collective-permute-done.5), channel_id=1, source_target_pairs={{0,2},{2,0},{4,6},{6,4},{8,10},{10,8},{12,14},{14,12},{16,18},{18,... | collective-permute-start | bytes 3538952 | tf_op jit(solution)/shard_map/ppermute | solution.py:772
  131.3 32.7 %collective-permute-start.6 = (bf16[192,768]{1,0:T(8,128)(2,1)}, bf16[192,768]{1,0:T(8,128)(2,1)S(1)}, u32[]{:S(2)}, u32[]{:S(2)}) collective-permute-start(bf16[192,768]{1,0:T(8,128)(2,1)} %collective-permute-done.3), channel_id=1, source_target_pairs={{0,2},{2,0},{4,6},{6,4},{8,10},{10,8},{12,14},{14,12},{16,18},{18,... | collective-permute-start | bytes 884744 | tf_op jit(solution)/shard_map/ppermute | solution.py:772
  154.9 10.3 %collective-permute-start.7 = (bf16[192,3072]{1,0:T(8,128)(2,1)}, bf16[192,3072]{1,0:T(8,128)(2,1)}, u32[]{:S(2)}, u32[]{:S(2)}) collective-permute-start(bf16[192,3072]{1,0:T(8,128)(2,1)} %collective-permute-done.4), channel_id=1, source_target_pairs={{0,2},{2,0},{4,6},{6,4},{8,10},{10,8},{12,14},{14,12},{16,18},{18,... | collective-permute-start | bytes 3538952 | tf_op jit(solution)/shard_map/ppermute | solution.py:772
  158.6 6.6 %slice-start.6 = ((s8[4718592]{0:T(1024)(128)(4,1)}), s8[524288]{0:T(1024)(128)(4,1)S(1)}, s32[]{:S(2)}) async-start(s8[4718592]{0:T(1024)(128)(4,1)} %bitcast.140), calls=%async_computation.6 | async-start | bytes 1048576
  165.2 16.2 %slice-start.4 = ((s8[4718592]{0:T(1024)(128)(4,1)}), s8[4194304]{0:T(1024)(128)(4,1)S(1)}, s32[]{:S(2)}) async-start(s8[4718592]{0:T(1024)(128)(4,1)} %bitcast.138), calls=%async_computation.4 | async-start | bytes 8388608
  166.8 14.6 %slice-start.5 = ((s8[4718592]{0:T(1024)(128)(4,1)}), s8[524288]{0:T(1024)(128)(4,1)S(1)}, s32[]{:S(2)}) async-start(s8[4718592]{0:T(1024)(128)(4,1)} %bitcast.138), calls=%async_computation.5 | async-start | bytes 1048576
  215.1 25.0 %collective-permute-start.10 = (bf16[2,768,768]{2,1,0:T(8,128)(2,1)}, bf16[2,768,768]{2,1,0:T(8,128)(2,1)}, u32[]{:S(2)}, u32[]{:S(2)}) collective-permute-start(bf16[2,768,768]{2,1,0:T(8,128)(2,1)} %get-tuple-element.115), channel_id=1, source_target_pairs={{0,2},{2,0},{4,6},{6,4},{8,10},{10,8},{12,14},{14,12},{16,18},{18,... | collective-permute-start | bytes 7077896 | tf_op jit(solution)/shard_map/ppermute | solution.py:901
  216.9 23.2 %collective-permute-start.9 = (bf16[2,192,3072]{2,1,0:T(8,128)(2,1)}, bf16[2,192,3072]{2,1,0:T(8,128)(2,1)}, u32[]{:S(2)}, u32[]{:S(2)}) collective-permute-start(bf16[2,192,3072]{2,1,0:T(8,128)(2,1)} %get-tuple-element.117), channel_id=1, source_target_pairs={{0,2},{2,0},{4,6},{6,4},{8,10},{10,8},{12,14},{14,12},{16,18},{18,... | collective-permute-start | bytes 7077896 | tf_op jit(solution)/shard_map/ppermute | solution.py:901
  244.6 74.2 %collective-permute-start.12 = (bf16[768,768]{1,0:T(8,128)(2,1)}, bf16[768,768]{1,0:T(8,128)(2,1)S(1)}, u32[]{:S(2)}, u32[]{:S(2)}) collective-permute-start(bf16[768,768]{1,0:T(8,128)(2,1)} %get-tuple-element.122), channel_id=1, source_target_pairs={{0,1},{1,0},{2,3},{3,2},{4,5},{5,4},{6,7},{7,6},{8,9},{9,8},{10,11... | collective-permute-start | bytes 3538952 | tf_op jit(solution)/shard_map/ppermute | solution.py:906
  248.5 70.3 %collective-permute-start.11 = (bf16[192,3072]{1,0:T(8,128)(2,1)S(1)}, bf16[192,3072]{1,0:T(8,128)(2,1)S(1)}, u32[]{:S(2)}, u32[]{:S(2)}) collective-permute-start(bf16[192,3072]{1,0:T(8,128)(2,1)S(1)} %get-tuple-element.124), channel_id=1, source_target_pairs={{0,1},{1,0},{2,3},{3,2},{4,5},{5,4},{6,7},{7,6},{8,9},{9,8},{10,11... | collective-permute-start | bytes 3538952 | tf_op jit(solution)/shard_map/ppermute | solution.py:906
  318.8 59.9 %copy-start.20 = (bf16[768,768]{1,0:T(8,128)(2,1)}, bf16[768,768]{1,0:T(8,128)(2,1)S(1)}, u32[]{:S(2)}) copy-start(bf16[768,768]{1,0:T(8,128)(2,1)S(1)} %collective-permute-done.12) | copy-start | bytes 3538948
  541.4 7.0 %copy-start.2 = (bf16[768,2304]{1,0:T(8,128)(2,1)S(1)}, bf16[768,2304]{1,0:T(8,128)(2,1)}, u32[]{:S(2)}) copy-start(bf16[768,2304]{1,0:T(8,128)(2,1)} %copy-done.1) | copy-start | bytes 10616836
  (54 other events, 148.3 us)

commit v9 on v8

--- a/solution.py
+++ b/solution.py
@@ -248,6 +248,53 @@
         compiler_params=pltpu.CompilerParams(vmem_limit_bytes=VMEM_BYTES),
         name="project",
     )(x, pack, vectors)
+
+
+def unpack_kernel(grads_ref, all_ref, pair_ref, sums_ref):
+    rows, width = pair_ref.shape[0], pair_ref.shape[1] // 2
+    half = rows // 2
+    low_lanes, high_lanes = slice(0, HEAD_DIM), slice(HEAD_DIM, LANES)
+    for base in range(0, HEADS, 2):
+        at = base * HEAD_DIM
+        for head in (base, base + 1):
+            pair_ref[:, head * LANES : (head + 1) * LANES] = grads_ref[head, 0:rows, :]
+        first, second = grads_ref[base], grads_ref[base + 1]
+        for part, lanes in ((0, low_lanes), (1, high_lanes)):
+            query = jnp.concatenate([first[rows:, lanes], second[rows:, lanes]], axis=1)
+            all_ref[part * half : (part + 1) * half, at : at + LANES] = (
+                query.astype(jnp.float32) * 0.125
+            ).astype(low_type)
+            kept = jnp.concatenate([first[:rows, lanes], second[:rows, lanes]], axis=1)
+            start = (part + 1) * width + at
+            all_ref[:, start : start + LANES] = kept
+    lanes = all_ref.shape[1] - 3 * width
+    all_ref[:, 3 * width :] = jnp.zeros((rows, lanes), low_type)
+    query_sums = jnp.sum(all_ref[:, 0:width].astype(jnp.float32), axis=0, keepdims=True)
+    value_sums = jnp.sum(
+        all_ref[:, 2 * width : 3 * width].astype(jnp.float32), axis=0, keepdims=True
+    )
+    row = lax.broadcasted_iota(jnp.int32, (LANES, width), 0)
+    block = jnp.where(row == 0, query_sums, jnp.where(row == 1, value_sums, 0.0))
+    sums_ref[:, 0:LANES] = jnp.transpose(block).astype(low_type)
+    sums_ref[:, LANES:] = jnp.zeros((width, lanes - LANES), low_type)
+
+
+def unpack(grads, width):
+    rows = grads.shape[1] * 2 // 3
+    lanes = 2 * LANES
+    vmem = pl.BlockSpec(memory_space=pltpu.VMEM)
+    return pl.pallas_call(
+        unpack_kernel,
+        out_shape=(
+            jax.ShapeDtypeStruct((rows, 3 * width + lanes), low_type),
+            jax.ShapeDtypeStruct((rows, 2 * width), low_type),
+            jax.ShapeDtypeStruct((width, lanes), low_type),
+        ),
+        in_specs=[vmem],
+        out_specs=(vmem,) * 3,
+        compiler_params=pltpu.CompilerParams(vmem_limit_bytes=VMEM_BYTES),
+        name="unpack",
+    )(grads)
 
 
 def tile_range(meta_ref, first, last, total, step):
@@ -491,7 +538,7 @@
     )(meta, order, recv, qa, ka, va, sums)
 
 
-PART_ORDERS = (("x", "z"), ("x", "z"), ("wa", "x", "z"), ("wa", "x", "z"))
+PART_ORDERS = (("x", "z"), ("x", "z"), ("wa", "x", "z"), ("x", "wa", "z"))
 GATHER_ORDERS = (("z", "x"), ("z", "x"), ("z", "x"), ("x", "z"))
 PARTS = len(PART_ORDERS)
 EARLY = sum(len(order) == 2 for order in PART_ORDERS)
@@ -705,11 +752,6 @@
     return [part.reshape(-1, part.shape[-1]) for part in sums]
 
 
-def column_sums(terms, lanes):
-    block = jnp.stack([jnp.sum(term, axis=0) for term in terms], axis=1).astype(low_type)
-    return jnp.pad(block, ((0, 0), (0, lanes - len(terms))))
-
-
 def reduce_shards(grad):
     part = lax.psum_scatter(
         grad.astype(low_type), ("wa", "ctx"), scatter_dimension=0, tiled=True
@@ -921,26 +963,11 @@
         grads_out = attend_back(meta, block_order, back_at_head, qa, ka, va, sums)
     grads_in = to_rows(grads_out, count, 3)
 
-    d_pair = grads_in[:, :tok_rows, :].transpose(1, 0, 2).reshape(tok_rows, 2 * width)
-    d_queries = (
-        grads_in[:, tok_rows:, :]
-        .reshape(HEADS, half, 2, HEAD_DIM)
-        .transpose(2, 1, 0, 3)
-        .reshape(tok_rows, width)
-        * jnp.asarray(0.125, low_type)
-    )
-    d_keys, d_values = (
-        grads_in[:, :tok_rows, low : low + HEAD_DIM].transpose(1, 0, 2).reshape(tok_rows, width)
-        for low in (0, HEAD_DIM)
-    )
-    d_all = jnp.concatenate(
-        [d_queries, d_keys, d_values, jnp.zeros((tok_rows, lanes), low_type)], axis=1
-    )
+    d_all, d_pair, bias_sums = unpack(grads_in, width)
+    d_queries = d_all[:, :width]
     grad_all = jnp.einsum("tc,td->cd", inputs, d_all, preferred_element_type=jnp.float32)
     last_block = lax.dynamic_update_slice(
-        grad_all.astype(low_type),
-        column_sums([d_queries.astype(jnp.float32), d_values.astype(jnp.float32)], lanes),
-        (0, 3 * width),
+        grad_all.astype(low_type), bias_sums, (0, 3 * width)
     )
     if direct:
         up_sum, down_sum, last_sum, out_sum = grad_sum((*early, last_block, out_block), 4)

time: 559 us -> 541 us (0.968)
  local copies, waits for them, and re-layouts: 57.4 us -> 43.3 us
    transpose x5 -> x0, local copies, waits for them, and re-layouts: 8.58 us -> none  [the longest x3 5 us: body(): grads_in[:, :tok_rows, low:low + HEAD_DIM].transpose(1, 0, 2)]
    unnamed x132 -> x126, local copies, waits for them, and re-layouts: 11.7 us -> 10.8 us
  transfers between devices with their start and end apart: 13 -> 13, of which waited for: 1 -> 1; matrix products, arithmetic and copies ran while one was open for 10% -> 10% of each run, Pallas kernels for 36% -> 37%
where the time goes in v9:
time: 541 us; the launch traced here: 535 us
  Pallas kernels  388 us (72%)
  matrix products  45.3 us (8%)
  local copies, waits for them, and re-layouts  43.3 us (8%)
  other arithmetic  42.3 us (8%)
  starting transfers between devices  9.68 us (2%)
    pallas_call x1, Pallas kernels, grad_sum(): pl.pallas_call(grad_sum_kernel, out_shape=tuple(outs), in_specs=[vmem] *...  124 us
    pallas_call x2, Pallas kernels, to_rows(): pl.pallas_call(partial(to_rows_kernel, count), out_shape=jax.ShapeDtypeSt...  83.1 us
    pallas_call x1, Pallas kernels, attend_back(): pl.pallas_call(attend_back_kernel, out_shape=jax.ShapeDtypeStruct((count,...  68.9 us
    pallas_call x2, Pallas kernels, to_heads(): pl.pallas_call(partial(to_heads_kernel, count), out_shape=jax.ShapeDtypeS...  64.6 us
    pallas_call x1, Pallas kernels, attend(): pl.pallas_call(attend_kernel, out_shape=(jax.ShapeDtypeStruct((count, row...  38.4 us
    dot_general x1, matrix products, body(): jnp.dot(norm_low, up_weight, preferred_element_type=jnp.float32) + up_bias  14.6 us
  transfers between devices with their start and end apart: 13, of which 1 were waited for; matrix products, arithmetic and copies ran while one was open for 10% of the time, Pallas kernels for 37%

profile of v9, /device:TPU:9, one launch (start us, length us, event | category | flops | bytes accessed | tf_op | source)
XLA Modules:
  0.0 535.2 jit_solution(3190646157712822898)
XLA Ops:
  9.5 4.6 constant_dynamic-update-slice_fusion.6
  22.5 3.8 collective-permute-done.2
  41.6 5.0 project.1.send_ref
  46.5 45.6 %to_heads_576.1.recv_ref = bf16[16,576,128]{2,1,0:T(8,128)(2,1)} custom-call(bf16[12,576,128]{2,1,0:T(8,128)(2,1)} %project.1.send_ref), custom_call_target="tpu_custom_call" | custom-call | flops 143999991808 | bytes 3538944 | tf_op jit(solution)/shard_map/to_heads_576/pallas_call | solution.py:122
  92.1 38.4 %attend.1 = (bf16[16,192,128]{2,1,0:T(8,128)(2,1)}, bf16[6144,128]{1,0:T(8,128)(2,1)}, bf16[6144,128]{1,0:T(8,128)(2,1)}, bf16[6144,128]{1,0:T(8,128)(2,1)}, f32[6144,128]{1,0:T(8,128)}) custom-call(s32[4]{0:T(128)} %pad_add_fusion.meta_ref, s32[32]{0:T(128)} %order_ref.3, bf16[16,576,128]{2,1,0:T(8,128)(2,1)} %to_heads_576.1.recv_ref), custom_call_target="tpu_custom_call" | custom-call | flops 38654705664 | bytes 9437184 | tf_op jit(solution)/shard_map/attend/pallas_call | solution.py:391
  131.4 23.4 %to_rows_192.1 = bf16[12,192,128]{2,1,0:T(8,128)(2,1)} custom-call(bf16[16,192,128]{2,1,0:T(8,128)(2,1)} %get-tuple-element.54.send_ref), custom_call_target="tpu_custom_call" | custom-call | flops 48000000000 | bytes 1572864 | tf_op jit(solution)/shard_map/to_rows_192/pallas_call | solution.py:196
  161.5 2.5 constant_dynamic-update-slice_fusion.2
  166.8 14.6 %multiply_convert_fusion = (bf16[384,3072]{1,0:T(8,128)(2,1)S(1)}, f32[384,3072]{1,0:T(8,128)}, f32[384,3072]{1,0:T(8,128)}) fusion(f32[3072]{0:T(1024)S(1)} %copy-done.38, bf16[768,3072]{1,0:T(8,128)(2,1)S(1)} %constant_dynamic-update-slice_fusion.4, f32[384,768]{1,0:T(8,128)S(1)} %get-tuple-element.134, f32[768]{0:T(1024)S(1)} %copy-done.40, ...), kind=kOutput, calls=%fused_computation.8 | convolution fusion | flops 1891270656 | bytes 17716224 | tf_op jit(solution)/shard_map/dot_general | solution.py:884
  187.7 5.8 %fusion.35 = (bf16[3072]{0:T(1024)(128)(2,1)S(1)}, bf16[384,3072]{1,0:T(8,128)(2,1)S(1)}) fusion(f32[384,3072]{1,0:T(8,128)} %get-tuple-element.116, f32[384,3072]{1,0:T(8,128)} %get-tuple-element.135, bf16[384,768]{1,0:T(8,128)(2,1)S(1)} %get-tuple-element.106, bf16[3072,768]{1,0:T(8,128)(2,1)S(1)} %constant_dynamic-update-slice_fusion.1), kind=kOutput, calls=%fused_computation.136 | convolution fusion | flops 1829630976 | bytes 17111040 | tf_op jit(solution)/shard_map/td,fd->tf/dot_general | solution.py:895
  193.5 4.8 convolution_convert_fusion.1
  200.7 4.3 convolution_convert_fusion.2
  210.1 5.1 select_bitcast_fusion
  218.5 2.6 copy.74
  221.1 19.0 %to_heads_192.1.recv_ref = bf16[16,192,128]{2,1,0:T(8,128)(2,1)} custom-call(bf16[12,192,128]{2,1,0:T(8,128)(2,1)} %copy.69.send_ref), custom_call_target="tpu_custom_call" | custom-call | flops 48000000000 | bytes 1179648 | tf_op jit(solution)/shard_map/to_heads_192/pallas_call | solution.py:122
  240.1 2.9 add_convert_fusion
  244.6 2.5 add_convert_fusion.1
  249.8 68.9 %attend_back.1.send_ref = bf16[16,576,128]{2,1,0:T(8,128)(2,1)} custom-call(s32[4]{0:T(128)} %pad_add_fusion.meta_ref, s32[32]{0:T(128)} %order_ref.3, bf16[16,192,128]{2,1,0:T(8,128)(2,1)} %to_heads_192.1.recv_ref, bf16[6144,128]{1,0:T(8,128)(2,1)} %get-tuple-element.62.qa_ref, bf16[6144,128]{1,0:T(8,128)(2,1)} %get-tuple-element.63.ka_ref, ...), custom_call_target="tpu_custom_call" | custom-call | flops 77309411328 | bytes 12582912 | tf_op jit(solution)/shard_map/attend_back/pallas_call | solution.py:520
  318.7 59.7 %to_rows_576.1.grads_ref = bf16[12,576,128]{2,1,0:T(8,128)(2,1)} custom-call(bf16[16,576,128]{2,1,0:T(8,128)(2,1)} %attend_back.1.send_ref), custom_call_target="tpu_custom_call" | custom-call | flops 143999991808 | bytes 4718592 | tf_op jit(solution)/shard_map/to_rows_576/pallas_call | solution.py:196
  378.4 4.1 unpack.1
  382.5 3.9 fusion.6
  391.0 123.8 %grad_sum.1 = (bf16[2,2,96,3072]{3,2,1,0:T(8,128)(2,1)}, bf16[2,2,384,768]{3,2,1,0:T(8,128)(2,1)}, bf16[2,2,96,2560]{3,2,1,0:T(8,128)(2,1)}, bf16[2,2,96,1024]{3,2,1,0:T(8,128)(2,1)}) custom-call(bf16[1,1,2,96,3072]{4,3,2,1,0:T(8,128)(2,1)} %bitcast.134, bf16[1,1,2,384,768]{4,3,2,1,0:T(8,128)(2,1)} %bitcast.133, bf16[2,2,2,96,2560]{4,3,2,1,0:T(8,128)(2,1)} %bitcast.140, ...), custom_call_target="tpu_custom_call" | custom-call | flops 78643200000 | bytes 15728640 | tf_op jit(solution)/shard_map/grad_sum/pallas_call | solution.py:733
  522.4 2.7 bitcast_convert_fusion
  525.1 2.9 bitcast_convert_fusion.1
  532.1 2.6 fusion.16
  (260 shorter events, 78.6 us)
Async XLA Ops:
  4.1 5.4 %copy-start.2 = (bf16[384,1536]{1,0:T(8,128)(2,1)}, bf16[384,1536]{1,0:T(8,128)(2,1)S(1)}, u32[]{:S(2)}) copy-start(bf16[384,1536]{1,0:T(8,128)(2,1)S(1)} %copy.63) | copy-start | bytes 3538948
  5.3 24.8 %collective-permute-start = (bf16[192,2304]{1,0:T(8,128)(2,1)}, bf16[192,2304]{1,0:T(8,128)(2,1)}, u32[]{:S(2)}, u32[]{:S(2)}) collective-permute-start(bf16[192,2304]{1,0:T(8,128)(2,1)} %fusion.26), channel_id=1, source_target_pairs={{0,1},{1,0},{2,3},{3,2},{4,5},{5,4},{6,7},{7,6},{8,9},{9,8},{10,11... | collective-permute-start | bytes 2654216 | tf_op jit(solution)/shard_map/ppermute | solution.py:808
  6.9 19.5 %collective-permute-start.2 = (bf16[16,384]{1,0:T(8,128)(2,1)S(1)}, bf16[16,384]{1,0:T(8,128)(2,1)}, u32[]{:S(2)}, u32[]{:S(2)}) collective-permute-start(bf16[16,384]{1,0:T(8,128)(2,1)S(1)} %concatenate.25), channel_id=1, source_target_pairs={{0,1},{1,0},{2,3},{3,2},{4,5},{5,4},{6,7},{7,6},{8,9},{9,8},{10,11... | collective-permute-start | bytes 36872 | tf_op jit(solution)/shard_map/ppermute | solution.py:839
  8.9 8.4 %slice-start = ((s8[4718592]{0:T(1024)(128)(4,1)}), s8[4194304]{0:T(1024)(128)(4,1)S(1)}, s32[]{:S(2)}) async-start(s8[4718592]{0:T(1024)(128)(4,1)} %bitcast.116), calls=%async_computation | async-start | bytes 8388608
  9.5 7.8 %slice-start.1 = ((s8[4718592]{0:T(1024)(128)(4,1)}), s8[524288]{0:T(1024)(128)(4,1)S(1)}, s32[]{:S(2)}) async-start(s8[4718592]{0:T(1024)(128)(4,1)} %bitcast.116), calls=%async_computation.1 | async-start | bytes 1048576
  28.4 6.8 %copy-start.6 = (bf16[1536,768]{1,0:T(8,128)(2,1)S(1)}, bf16[1536,768]{1,0:T(8,128)(2,1)}, u32[]{:S(2)}) copy-start(bf16[1536,768]{1,0:T(8,128)(2,1)} %get-tuple-element.53) | copy-start | bytes 7077892
  30.0 6.5 %copy-start.16 = (bf16[384,768]{1,0:T(8,128)(2,1)S(1)}, bf16[384,768]{1,0:T(8,128)(2,1)}, u32[]{:S(2)}) copy-start(bf16[384,768]{1,0:T(8,128)(2,1)} %get-tuple-element.51) | copy-start | bytes 1769476
  30.0 9.7 %collective-permute-start.1 = (bf16[192,2304]{1,0:T(8,128)(2,1)}, bf16[192,2304]{1,0:T(8,128)(2,1)S(1)}, u32[]{:S(2)}, u32[]{:S(2)}) collective-permute-start(bf16[192,2304]{1,0:T(8,128)(2,1)} %collective-permute-done), channel_id=1, source_target_pairs={{0,2},{2,0},{4,6},{6,4},{8,10},{10,8},{12,14},{14,12},{16,18},{18,... | collective-permute-start | bytes 2654216 | tf_op jit(solution)/shard_map/ppermute | solution.py:814
  33.9 96.6 %collective-permute-start.4 = (bf16[192,3072]{1,0:T(8,128)(2,1)}, bf16[192,3072]{1,0:T(8,128)(2,1)}, u32[]{:S(2)}, u32[]{:S(2)}) collective-permute-start(bf16[192,3072]{1,0:T(8,128)(2,1)} %constant_dynamic-slice_fusion.1), channel_id=1, source_target_pairs={{0,1},{1,0},{2,3},{3,2},{4,5},{5,4},{6,7},{7,6},{8,9},{9,8},{10,11... | collective-permute-start | bytes 3538952 | tf_op jit(solution)/shard_map/ppermute | solution.py:808
  36.3 94.2 %collective-permute-start.5 = (bf16[768,768]{1,0:T(8,128)(2,1)}, bf16[768,768]{1,0:T(8,128)(2,1)}, u32[]{:S(2)}, u32[]{:S(2)}) collective-permute-start(bf16[768,768]{1,0:T(8,128)(2,1)} %constant_dynamic-slice_fusion), channel_id=1, source_target_pairs={{0,1},{1,0},{2,3},{3,2},{4,5},{5,4},{6,7},{7,6},{8,9},{9,8},{10,11... | collective-permute-start | bytes 3538952 | tf_op jit(solution)/shard_map/ppermute | solution.py:808
  37.2 93.3 %collective-permute-start.3 = (bf16[192,768]{1,0:T(8,128)(2,1)}, bf16[192,768]{1,0:T(8,128)(2,1)}, u32[]{:S(2)}, u32[]{:S(2)}) collective-permute-start(bf16[192,768]{1,0:T(8,128)(2,1)} %constant_dynamic-slice_fusion.2), channel_id=1, source_target_pairs={{0,1},{1,0},{2,3},{3,2},{4,5},{5,4},{6,7},{7,6},{8,9},{9,8},{10,11... | collective-permute-start | bytes 884744 | tf_op jit(solution)/shard_map/ppermute | solution.py:808
  130.5 51.0 %collective-permute-start.8 = (bf16[768,768]{1,0:T(8,128)(2,1)}, bf16[768,768]{1,0:T(8,128)(2,1)}, u32[]{:S(2)}, u32[]{:S(2)}) collective-permute-start(bf16[768,768]{1,0:T(8,128)(2,1)} %collective-permute-done.5), channel_id=1, source_target_pairs={{0,2},{2,0},{4,6},{6,4},{8,10},{10,8},{12,14},{14,12},{16,18},{18,... | collective-permute-start | bytes 3538952 | tf_op jit(solution)/shard_map/ppermute | solution.py:814
  131.3 32.8 %collective-permute-start.6 = (bf16[192,768]{1,0:T(8,128)(2,1)}, bf16[192,768]{1,0:T(8,128)(2,1)S(1)}, u32[]{:S(2)}, u32[]{:S(2)}) collective-permute-start(bf16[192,768]{1,0:T(8,128)(2,1)} %collective-permute-done.3), channel_id=1, source_target_pairs={{0,2},{2,0},{4,6},{6,4},{8,10},{10,8},{12,14},{14,12},{16,18},{18,... | collective-permute-start | bytes 884744 | tf_op jit(solution)/shard_map/ppermute | solution.py:814
  154.9 10.3 %collective-permute-start.7 = (bf16[192,3072]{1,0:T(8,128)(2,1)}, bf16[192,3072]{1,0:T(8,128)(2,1)}, u32[]{:S(2)}, u32[]{:S(2)}) collective-permute-start(bf16[192,3072]{1,0:T(8,128)(2,1)} %collective-permute-done.4), channel_id=1, source_target_pairs={{0,2},{2,0},{4,6},{6,4},{8,10},{10,8},{12,14},{14,12},{16,18},{18,... | collective-permute-start | bytes 3538952 | tf_op jit(solution)/shard_map/ppermute | solution.py:814
  158.6 6.6 %slice-start.6 = ((s8[4718592]{0:T(1024)(128)(4,1)}), s8[524288]{0:T(1024)(128)(4,1)S(1)}, s32[]{:S(2)}) async-start(s8[4718592]{0:T(1024)(128)(4,1)} %bitcast.124), calls=%async_computation.6 | async-start | bytes 1048576
  165.2 16.2 %slice-start.4 = ((s8[4718592]{0:T(1024)(128)(4,1)}), s8[4194304]{0:T(1024)(128)(4,1)S(1)}, s32[]{:S(2)}) async-start(s8[4718592]{0:T(1024)(128)(4,1)} %bitcast.122), calls=%async_computation.4 | async-start | bytes 8388608
  166.8 14.6 %slice-start.5 = ((s8[4718592]{0:T(1024)(128)(4,1)}), s8[524288]{0:T(1024)(128)(4,1)S(1)}, s32[]{:S(2)}) async-start(s8[4718592]{0:T(1024)(128)(4,1)} %bitcast.122), calls=%async_computation.5 | async-start | bytes 1048576
  215.2 24.9 %collective-permute-start.10 = (bf16[2,768,768]{2,1,0:T(8,128)(2,1)}, bf16[2,768,768]{2,1,0:T(8,128)(2,1)}, u32[]{:S(2)}, u32[]{:S(2)}) collective-permute-start(bf16[2,768,768]{2,1,0:T(8,128)(2,1)} %get-tuple-element.121), channel_id=1, source_target_pairs={{0,2},{2,0},{4,6},{6,4},{8,10},{10,8},{12,14},{14,12},{16,18},{18,... | collective-permute-start | bytes 7077896 | tf_op jit(solution)/shard_map/ppermute | solution.py:943
  217.0 23.2 %collective-permute-start.9 = (bf16[2,192,3072]{2,1,0:T(8,128)(2,1)}, bf16[2,192,3072]{2,1,0:T(8,128)(2,1)}, u32[]{:S(2)}, u32[]{:S(2)}) collective-permute-start(bf16[2,192,3072]{2,1,0:T(8,128)(2,1)} %get-tuple-element.123), channel_id=1, source_target_pairs={{0,2},{2,0},{4,6},{6,4},{8,10},{10,8},{12,14},{14,12},{16,18},{18,... | collective-permute-start | bytes 7077896 | tf_op jit(solution)/shard_map/ppermute | solution.py:943
  244.6 74.1 %collective-permute-start.12 = (bf16[768,768]{1,0:T(8,128)(2,1)}, bf16[768,768]{1,0:T(8,128)(2,1)S(1)}, u32[]{:S(2)}, u32[]{:S(2)}) collective-permute-start(bf16[768,768]{1,0:T(8,128)(2,1)} %get-tuple-element.128), channel_id=1, source_target_pairs={{0,1},{1,0},{2,3},{3,2},{4,5},{5,4},{6,7},{7,6},{8,9},{9,8},{10,11... | collective-permute-start | bytes 3538952 | tf_op jit(solution)/shard_map/ppermute | solution.py:948
  248.3 70.3 %collective-permute-start.11 = (bf16[192,3072]{1,0:T(8,128)(2,1)S(1)}, bf16[192,3072]{1,0:T(8,128)(2,1)S(1)}, u32[]{:S(2)}, u32[]{:S(2)}) collective-permute-start(bf16[192,3072]{1,0:T(8,128)(2,1)S(1)} %get-tuple-element.130), channel_id=1, source_target_pairs={{0,1},{1,0},{2,3},{3,2},{4,5},{5,4},{6,7},{7,6},{8,9},{9,8},{10,11... | collective-permute-start | bytes 3538952 | tf_op jit(solution)/shard_map/ppermute | solution.py:948
  318.7 59.7 %copy-start.17 = (bf16[768,768]{1,0:T(8,128)(2,1)}, bf16[768,768]{1,0:T(8,128)(2,1)S(1)}, u32[]{:S(2)}) copy-start(bf16[768,768]{1,0:T(8,128)(2,1)S(1)} %collective-permute-done.12) | copy-start | bytes 3538948
  318.7 59.7 %copy-start.19 = (bf16[192,3072]{1,0:T(8,128)(2,1)}, bf16[192,3072]{1,0:T(8,128)(2,1)S(1)}, u32[]{:S(2)}) copy-start(bf16[192,3072]{1,0:T(8,128)(2,1)S(1)} %collective-permute-done.11) | copy-start | bytes 3538948
  318.7 63.8 %copy-start.28 = (bf16[1,384,768]{2,1,0:T(8,128)(2,1)S(1)}, bf16[1,384,768]{2,1,0:T(8,128)(2,1)}, u32[]{:S(2)}) copy-start(bf16[1,384,768]{2,1,0:T(8,128)(2,1)} %param.19) | copy-start | bytes 1769476
  (51 other events, 144.9 us)
